TPU v7x, 256 devices: a whole 4x4x8 slice. The times are simulated.
256 devices in a mesh: row: 8 (over y_hi, x), col: 32 (over z, y_lo, core).
Axes of the slice: x: 4, y: 4 (y_hi: 2, y_lo: 2; y = y_hi * 2 + y_lo), z: 8, core: 2. Of those that a mesh axis runs over, the one named last changes fastest.
Arguments:
- legendre: bfloat16 [512, 512, 512], P('row', 'col'), may hold values from -6 to 6
- vectors: bfloat16 [512, 512, 256], P('row', 'col'), may hold values from -6 to 6
- panel_orders: int32 [8], replicated, may hold values from 0 to 511, as said below
- cycle_span: int32 [512, 2], replicated, may hold values from 0 to 2047, as said below
- cycle_weight: float32 [512], replicated, may hold values from 0.0009765625 to 0.0029296875
Outputs:
- projected: bfloat16 [512, 8, 256], P('col', 'row')
Inputs may be any that keep to these rules, and one draw needn't show every extreme that they name: `panel_orders`: the 8 entries are distinct orders; 0 and 511 are among them. `cycle_span`: in every cycle the first entry is smaller than the second.
All inputs are finite; a program needn't handle non-finite values.
Results may differ from a plain program's by a relative error of at most 0.008.
Values may be sent and summed in bfloat16 or wider, within the bound.
No kernel may reach another device: no remote copies, remote signals or barrier semaphores. Data moves between devices by JAX's collectives and lax.ppermute only.
A program may use at most 64 MiB of HBM per device.

v0:
```python
import math

import jax
import jax.numpy as jnp
from jax import lax
from jax.experimental import pallas as pl
from jax.experimental.pallas import tpu as pltpu
from jax.sharding import Mesh, PartitionSpec as P


NPHI = 2048
CELL = 2.0 * math.pi / NPHI
ROW = ("yh", "x")
COL = ("z", "yl", "core")
PLANE = ("z", "yl")


def sine_of_angle(x):
    square = x * x
    value = jnp.float32(-1.0 / 39916800.0)
    for term in (1.0 / 362880.0, -1.0 / 5040.0, 1.0 / 120.0, -1.0 / 6.0, 1.0):
        value = value * square + jnp.float32(term)
    return value * x


def sine_of_cells(cells):
    shifted = cells + NPHI // 4
    centred = (shifted & (NPHI // 2 - 1)) - NPHI // 4
    value = sine_of_angle(centred.astype(jnp.float32) * jnp.float32(CELL))
    return jnp.where((shifted & (NPHI // 2)) == 0, value, -value)


def half_denominator(wavenumber):
    angle = wavenumber.astype(jnp.float32) * jnp.float32(math.pi / NPHI)
    sine = 2.0 * sine_of_angle(angle)
    zero = wavenumber == 0
    return jnp.where(zero, 0.0, jnp.float32(CELL) / jnp.where(zero, 1.0, sine))


def picks_kernel(orders_ref, leg_ref, picks_ref, rows, sems):
    panels, degrees, cycles = picks_ref.shape
    half = cycles // 2
    first_order = lax.axis_index(ROW) * leg_ref.shape[0]
    core = lax.axis_index("core")
    first_degree = lax.axis_index(COL) * degrees
    own = pl.ds(pl.multiple_of(core * half, half), half)
    other = pl.ds(pl.multiple_of((1 - core) * half, half), half)
    copies = []
    for p in range(panels):
        at = jnp.clip(orders_ref[p] - first_order, 0, leg_ref.shape[0] - 1)
        copies.append(pltpu.make_async_copy(leg_ref.at[at], rows.at[p], sems.at[p]))
        copies[-1].start()
    degree = lax.broadcasted_iota(jnp.int32, (degrees, half), 0) + first_degree
    for p in range(panels):
        copies[p].wait()
        place = orders_ref[p] - first_order
        held = (place >= 0) & (place < leg_ref.shape[0])
        kept = degree >= jnp.where(held, orders_ref[p], leg_ref.shape[0] * lax.axis_size(ROW))
        for lanes, part in ((own, slice(0, half)), (other, slice(half, cycles))):
            picks_ref[p, :, part] = jnp.where(kept, rows[p, :, lanes].astype(jnp.float32), 0.0).astype(jnp.bfloat16)


def coef_kernel(orders_ref, span_ref, weight_ref, coef_ref):
    panels, orders, half = coef_ref.shape
    own = pl.ds(pl.multiple_of(lax.axis_index("core") * half, half), half)
    start, stop = span_ref[0:1, own], span_ref[1:2, own]
    weight = 0.5 * weight_ref[0:1, own]
    first_order = lax.axis_index(ROW) * orders
    order = lax.broadcasted_iota(jnp.int32, (orders, half), 0) + first_order
    quarter = NPHI // 4
    sin_stop, cos_stop = sine_of_cells(order * stop), sine_of_cells(order * stop + quarter)
    sin_start, cos_start = sine_of_cells(order * start), sine_of_cells(order * start + quarter)
    width = weight * (jnp.float32(CELL) * (stop - start).astype(jnp.float32))
    column = lax.broadcasted_iota(jnp.int32, (orders, 128), 0) + first_order
    for p in range(panels):
        panel = orders_ref[p]
        panel_stop, panel_start = panel * stop, panel * start
        a = weight * sine_of_cells(panel_stop)
        b = weight * sine_of_cells(panel_start)
        c = weight * sine_of_cells(panel_stop + quarter)
        d = weight * sine_of_cells(panel_start + quarter)
        over_sum, over_gap = half_denominator(panel + column), half_denominator(panel - column)
        even = (over_sum + over_gap)[:, :1]
        odd = (over_sum - over_gap)[:, :1]
        at_zero = jnp.where(panel == column, 1.0, 0.0) + jnp.where(panel + column == 0, 1.0, 0.0)
        coef_ref[p] = (
            even * (a * cos_stop - b * cos_start)
            + odd * (c * sin_stop - d * sin_start)
            + at_zero[:, :1] * width
        )


def panel_kernel(coef_ref, own_t_ref, other_t_ref, own_v_ref, other_v_ref, out_ref, tables, turned):
    panels, orders, half = coef_ref.shape
    degrees, vecs = own_v_ref.shape[1:]
    block = 256 // degrees
    core = lax.axis_index("core")
    lanes = pl.ds(pl.multiple_of(core * half, half), half)
    first_order = lax.axis_index(ROW) * orders
    pair_degree = lax.axis_index(PLANE) * (2 * degrees)
    degree = lax.broadcasted_iota(jnp.int32, (degrees, half), 0)
    for side, (t_ref, v_ref) in enumerate(((own_t_ref, own_v_ref), (other_t_ref, other_v_ref))):
        offset = core if side == 0 else 1 - core
        gap = degree + (pair_degree + offset * degrees - first_order)

        def prepare(step, carry, side=side, t_ref=t_ref, v_ref=v_ref, gap=gap):
            start = pl.multiple_of(step * block, block)
            for i in range(block):
                table = t_ref[start + i, :, lanes].astype(jnp.float32)
                tables[side, start + i] = jnp.where(gap - start >= i, table, 0.0).astype(jnp.bfloat16)
            columns = pl.ds(pl.multiple_of(step * block * degrees, block * degrees), block * degrees)
            turned[side, :, columns] = v_ref[pl.ds(start, block)].reshape(block * degrees, vecs).T
            return carry

        lax.fori_loop(0, orders // block, prepare, 0)

    def per_panel(p, carry):
        total = None
        for side in range(2):
            for first in range(0, orders, block):
                rows = []
                for o in range(first, first + block):
                    coef = jnp.broadcast_to(coef_ref[p, pl.ds(o, 1), :], (degrees, half))
                    rows.append(coef.astype(jnp.bfloat16) * tables[side, o])
                weighted = jnp.concatenate(rows, axis=0)
                columns = slice(first * degrees, (first + block) * degrees)
                part = jnp.dot(turned[side, :, columns], weighted, preferred_element_type=jnp.float32)
                total = part if total is None else total + part
        out_ref[p] = total.astype(jnp.bfloat16)
        return carry

    lax.fori_loop(0, panels, per_panel, 0)


def join_kernel(own_ref, other_ref, out_ref):
    yl = lax.axis_index("yl")
    out_ref[yl] = own_ref[...]
    out_ref[1 - yl] = other_ref[...]


def place_kernel(*refs):
    *row_refs, out_ref = refs
    count = len(row_refs)
    degrees = row_refs[0].shape[1]
    z = lax.axis_index("z")
    for distance, row_ref in enumerate(row_refs):
        origin = lax.rem(z + (count - distance), count)
        for yl in range(2):
            at = pl.multiple_of((origin * 2 + yl) * degrees, degrees)
            out_ref[pl.ds(at, degrees), :] = row_ref[yl]


def apply_kernel(rows_ref, own_ref, other_ref, out_ref):
    half = own_ref.shape[1]
    dims = (((1,), (1,)), ((), ()))
    applied = lax.dot_general(rows_ref[:, :half], own_ref[...], dims, preferred_element_type=jnp.float32)
    applied += lax.dot_general(rows_ref[:, half:], other_ref[...], dims, preferred_element_type=jnp.float32)
    out_ref[...] = applied.astype(jnp.bfloat16).reshape(out_ref.shape)


def swapped(array):
    return lax.ppermute(array, "core", [(0, 1), (1, 0)])


def stages(legendre, vectors, panel_orders, cycle_span, cycle_weight):
    orders, degrees, cycles = legendre.shape
    vecs = vectors.shape[2]
    panels = panel_orders.shape[0]
    half = cycles // 2
    pairs = orders * degrees
    vmem = pl.BlockSpec(memory_space=pltpu.VMEM)
    smem = pl.BlockSpec(memory_space=pltpu.SMEM)
    bf16 = jnp.bfloat16
    params = pltpu.CompilerParams(vmem_limit_bytes=24 * 1024 * 1024)

    other_tables = swapped(legendre)
    other_vectors = swapped(vectors)
    picks = pl.pallas_call(
        picks_kernel,
        in_specs=[smem, pl.BlockSpec(memory_space=pltpu.HBM)],
        out_specs=vmem,
        out_shape=jax.ShapeDtypeStruct((panels, degrees, cycles), bf16),
        scratch_shapes=[
            pltpu.VMEM((panels, degrees, cycles), bf16),
            pltpu.SemaphoreType.DMA((panels,)),
        ],
        cost_estimate=pl.CostEstimate(flops=1_000_000, bytes_accessed=400_000, transcendentals=0),
        compiler_params=params,
    )(panel_orders, legendre)
    picked = lax.all_to_all(picks, ROW, 0, 0, tiled=True)

    coef = pl.pallas_call(
        coef_kernel,
        in_specs=[smem, vmem, vmem],
        out_specs=vmem,
        out_shape=jax.ShapeDtypeStruct((panels, orders, half), jnp.float32),
        cost_estimate=pl.CostEstimate(flops=10_000_000, bytes_accessed=500_000, transcendentals=0),
        compiler_params=params,
    )(panel_orders, cycle_span.T, cycle_weight.reshape(1, cycles))
    partial = pl.pallas_call(
        panel_kernel,
        in_specs=[vmem] * 5,
        out_specs=vmem,
        out_shape=jax.ShapeDtypeStruct((panels, vecs, half), bf16),
        scratch_shapes=[
            pltpu.VMEM((2, orders, degrees, half), bf16),
            pltpu.VMEM((2, vecs, pairs), bf16),
        ],
        cost_estimate=pl.CostEstimate(
            flops=2 * panels * vecs * half * 2 * pairs, bytes_accessed=3_500_000, transcendentals=0
        ),
        compiler_params=params,
    )(coef, legendre, other_tables, vectors, other_vectors)

    rows = jnp.sum(picked.astype(jnp.float32), axis=0).astype(bf16)
    paired = lax.ppermute(rows, "yl", [(0, 1), (1, 0)])
    joined = pl.pallas_call(
        join_kernel,
        in_specs=[vmem] * 2,
        out_specs=vmem,
        out_shape=jax.ShapeDtypeStruct((2, degrees, cycles), bf16),
        cost_estimate=pl.CostEstimate(flops=100_000, bytes_accessed=64_000, transcendentals=0),
        compiler_params=params,
    )(rows, paired)
    spread = [joined]
    count = lax.axis_size("z")
    for distance in range(1, count):
        spread.append(lax.ppermute(joined, "z", [(i, (i + distance) % count) for i in range(count)]))

    shared = 2 * count * degrees
    panel_rows = pl.pallas_call(
        place_kernel,
        in_specs=[vmem] * count,
        out_specs=vmem,
        out_shape=jax.ShapeDtypeStruct((shared, cycles), bf16),
        cost_estimate=pl.CostEstimate(flops=500_000, bytes_accessed=500_000, transcendentals=0),
        compiler_params=params,
    )(*spread)

    pieces = lax.all_to_all(partial, ROW, 0, 0, tiled=True)
    own = jnp.sum(pieces.astype(jnp.float32), axis=0).astype(bf16)
    other = swapped(own)
    applied = pl.pallas_call(
        apply_kernel,
        in_specs=[vmem] * 3,
        out_specs=vmem,
        out_shape=jax.ShapeDtypeStruct((2 * count, degrees, vecs), bf16),
        cost_estimate=pl.CostEstimate(flops=2 * shared * cycles * vecs, bytes_accessed=700_000, transcendentals=0),
        compiler_params=params,
    )(panel_rows, own, other)
    shares = lax.all_to_all(applied, PLANE, 0, 0, tiled=True)
    result = jnp.sum(shares.astype(jnp.float32), axis=0).astype(bf16)
    return result[:, None, :]


def solution(mesh):
    axes = Mesh(mesh.devices.reshape(2, 4, 8, 2, 2), ROW + COL)
    in_specs = (P(ROW, COL, None), P(ROW, COL, None), P(), P(), P())
    out_specs = P(COL, ROW, None)
    return jax.shard_map(stages, mesh=axes, in_specs=in_specs, out_specs=out_specs, check_vma=False)
```

profile of v0, /device:TPU:2, one launch (start us, length us, event | category | flops | bytes accessed | tf_op | source)
XLA Modules:
  0.0 86.1 jit_solution(2231645958154562789)
XLA Ops:
  0.0 0.0 collective-permute-start.8
  0.0 0.5 collective-permute-start.9
  0.5 0.2 copy-done.3
  0.7 0.5 copy-done.4
  1.2 0.7 copy-done.2
  1.9 1.5 %shard_map.58.coef_ref = f32[8,64,256]{2,1,0:T(8,128)S(1)} custom-call(s32[8]{0:T(128)S(1)} %copy-done.4, s32[2,512]{1,0:T(2,128)S(1)} %bitcast.3, f32[1,512]{1,0:T(1,128)S(1)} %bitcast.4), custom_call_target="tpu_custom_call" | custom-call | flops 10000000 | bytes 500000 | tf_op jit(solution)/shard_map/pallas_call | solution.py:192
  3.3 0.3 collective-permute-done.9.other_v_ref
  3.6 0.0 collective-permute-done.8.other_t_ref
  3.6 1.2 %copy-done = bf16[64,16,512]{2,1,0:T(8,128)(2,1)S(1)} copy-done((bf16[64,16,512]{2,1,0:T(8,128)(2,1)S(1)}, bf16[64,16,512]{2,1,0:T(8,128)(2,1)}, u32[]{:S(2)}) %copy-start) | copy-done | bytes 1048600
  4.9 5.2 %shard_map.59 = bf16[8,256,256]{2,1,0:T(8,128)(2,1)} custom-call(f32[8,64,256]{2,1,0:T(8,128)S(1)} %shard_map.58.coef_ref, bf16[64,16,512]{2,1,0:T(8,128)(2,1)S(1)} %copy-done, bf16[64,16,512]{2,1,0:T(8,128)(2,1)S(1)} %collective-permute-done.8.other_t_ref, bf16[64,16,256]{2,1,0:T(8,128)(2,1)S(1)} %copy-done.5, ...), custom_call_target="tpu_custom_call" | custom-call | flops 2147483648 | bytes 3500000 | tf_op jit(solution)/shard_map/pallas_call | solution.py:200
  10.1 7.6 %all-to-all-start.1 = ((bf16[8,256,256]{2,1,0:T(8,128)(2,1)}), bf16[8,256,256]{2,1,0:T(8,128)(2,1)S(1)}, u32[]{:S(2)}, u32[]{:S(2)}) async-start(bf16[8,256,256]{2,1,0:T(8,128)(2,1)} %shard_map.59), calls=%async_computation.1 | async-start | bytes 2097152 | tf_op jit(solution)/shard_map/all_to_all | solution.py:240
  17.7 1.6 %shard_map.55 = bf16[8,16,512]{2,1,0:T(8,128)(2,1)} custom-call(s32[8]{0:T(128)S(1)} %copy-done.4, bf16[64,16,512]{2,1,0:T(8,128)(2,1)S(1)} %copy-done.1), custom_call_target="tpu_custom_call" | custom-call | flops 1000000 | bytes 400000 | tf_op jit(solution)/shard_map/pallas_call | solution.py:178
  19.3 14.8 %all-to-all-done.1 = bf16[8,256,256]{2,1,0:T(8,128)(2,1)S(1)} async-done(((bf16[8,256,256]{2,1,0:T(8,128)(2,1)}), bf16[8,256,256]{2,1,0:T(8,128)(2,1)S(1)}, u32[]{:S(2)}, u32[]{:S(2)}) %all-to-all-start.1) | async-done | bytes 1048608 | tf_op jit(solution)/shard_map/all_to_all | solution.py:240
  34.0 4.4 %all-to-all-start = ((bf16[8,16,512]{2,1,0:T(8,128)(2,1)}), bf16[8,16,512]{2,1,0:T(8,128)(2,1)S(1)}, u32[]{:S(2)}, u32[]{:S(2)}) async-start(bf16[8,16,512]{2,1,0:T(8,128)(2,1)} %shard_map.55), calls=%async_computation | async-start | bytes 262144 | tf_op jit(solution)/shard_map/all_to_all | solution.py:190
  38.5 0.1 reduce_sum.37.own_ref
  38.6 0.1 collective-permute-start.10
  38.7 6.7 %all-to-all-done = bf16[8,16,512]{2,1,0:T(8,128)(2,1)S(1)} async-done(((bf16[8,16,512]{2,1,0:T(8,128)(2,1)}), bf16[8,16,512]{2,1,0:T(8,128)(2,1)S(1)}, u32[]{:S(2)}, u32[]{:S(2)}) %all-to-all-start) | async-done | bytes 131104 | tf_op jit(solution)/shard_map/all_to_all | solution.py:190
  45.5 0.8 collective-permute-start
  46.2 3.1 %collective-permute-done.other_ref = bf16[16,512]{1,0:T(8,128)(2,1)S(1)} collective-permute-done((bf16[16,512]{1,0:T(8,128)(2,1)S(1)}, bf16[16,512]{1,0:T(8,128)(2,1)S(1)}, u32[]{:S(2)}, u32[]{:S(2)}) %collective-permute-start) | collective-permute-done | bytes 16416 | tf_op jit(solution)/shard_map/ppermute | solution.py:216
  49.3 5.9 %collective-permute-start.7 = (bf16[2,16,512]{2,1,0:T(8,128)(2,1)S(1)}, bf16[2,16,512]{2,1,0:T(8,128)(2,1)S(1)}, u32[]{:S(2)}, u32[]{:S(2)}) collective-permute-start(bf16[2,16,512]{2,1,0:T(8,128)(2,1)S(1)} %shard_map.56.refs_0_), channel_id=1, source_target_pairs={{0,28},{4,0},{8,4},{12,8},{16,12},{20,16},{24,20},{28,24},{1,29},{... | collective-permute-start | bytes 98312 | tf_op jit(solution)/shard_map/ppermute | solution.py:228
  55.2 1.5 %collective-permute-start.6 = (bf16[2,16,512]{2,1,0:T(8,128)(2,1)S(1)}, bf16[2,16,512]{2,1,0:T(8,128)(2,1)S(1)}, u32[]{:S(2)}, u32[]{:S(2)}) collective-permute-start(bf16[2,16,512]{2,1,0:T(8,128)(2,1)S(1)} %shard_map.56.refs_0_), channel_id=1, source_target_pairs={{0,24},{4,28},{8,0},{12,4},{16,8},{20,12},{24,16},{28,20},{1,25},{... | collective-permute-start | bytes 98312 | tf_op jit(solution)/shard_map/ppermute | solution.py:228
  56.6 0.4 collective-permute-start.5
  57.1 5.0 %collective-permute-start.4 = (bf16[2,16,512]{2,1,0:T(8,128)(2,1)S(1)}, bf16[2,16,512]{2,1,0:T(8,128)(2,1)S(1)}, u32[]{:S(2)}, u32[]{:S(2)}) collective-permute-start(bf16[2,16,512]{2,1,0:T(8,128)(2,1)S(1)} %shard_map.56.refs_0_), channel_id=1, source_target_pairs={{0,16},{4,20},{8,24},{12,28},{16,0},{20,4},{24,8},{28,12},{1,17},{... | collective-permute-start | bytes 98312 | tf_op jit(solution)/shard_map/ppermute | solution.py:228
  62.1 0.0 collective-permute-done.7.refs_7_
  62.1 2.5 %collective-permute-start.2 = (bf16[2,16,512]{2,1,0:T(8,128)(2,1)S(1)}, bf16[2,16,512]{2,1,0:T(8,128)(2,1)S(1)}, u32[]{:S(2)}, u32[]{:S(2)}) collective-permute-start(bf16[2,16,512]{2,1,0:T(8,128)(2,1)S(1)} %shard_map.56.refs_0_), channel_id=1, source_target_pairs={{0,8},{4,12},{8,16},{12,20},{16,24},{20,28},{24,0},{28,4},{1,9},{5... | collective-permute-start | bytes 98312 | tf_op jit(solution)/shard_map/ppermute | solution.py:228
  64.6 1.9 %collective-permute-start.1 = (bf16[2,16,512]{2,1,0:T(8,128)(2,1)S(1)}, bf16[2,16,512]{2,1,0:T(8,128)(2,1)S(1)}, u32[]{:S(2)}, u32[]{:S(2)}) collective-permute-start(bf16[2,16,512]{2,1,0:T(8,128)(2,1)S(1)} %shard_map.56.refs_0_), channel_id=1, source_target_pairs={{0,4},{4,8},{8,12},{12,16},{16,20},{20,24},{24,28},{28,0},{1,5},{5... | collective-permute-start | bytes 98312 | tf_op jit(solution)/shard_map/ppermute | solution.py:228
  66.5 2.5 %collective-permute-done.3.refs_3_ = bf16[2,16,512]{2,1,0:T(8,128)(2,1)S(1)} collective-permute-done((bf16[2,16,512]{2,1,0:T(8,128)(2,1)S(1)}, bf16[2,16,512]{2,1,0:T(8,128)(2,1)S(1)}, u32[]{:S(2)}, u32[]{:S(2)}) %collective-permute-start.3) | collective-permute-done | bytes 32800 | tf_op jit(solution)/shard_map/ppermute | solution.py:228
  69.0 0.7 collective-permute-done.2.refs_2_
  69.8 0.2 collective-permute-done.1.refs_1_
  70.0 0.3 shard_map.60
  70.3 15.1 %all_to_all.15 = bf16[16,16,256]{2,1,0:T(8,128)(2,1)S(1)} all-to-all(bf16[16,16,256]{2,1,0:T(8,128)(2,1)S(1)} %shard_map.60), channel_id=1, replica_groups=mesh['yh'=2,'x'=4,'z'=8,'yl'=2,'core'=2] {'z','yl'}, dimensions={0} | all-to-all | bytes 262144 | tf_op jit(solution)/shard_map/all_to_all | solution.py:251
  85.4 0.6 reduce_sum.38
  (16 shorter events, 0.1 us)
Async XLA Ops:
  0.0 0.7 copy-start.3
  0.0 3.6 %collective-permute-start.8 = (bf16[64,16,512]{2,1,0:T(8,128)(2,1)}, bf16[64,16,512]{2,1,0:T(8,128)(2,1)S(1)}, u32[]{:S(2)}, u32[]{:S(2)}) collective-permute-start(bf16[64,16,512]{2,1,0:T(8,128)(2,1)} %own_t_ref.1), channel_id=1, source_target_pairs={{0,1},{1,0},{2,3},{3,2},{4,5},{5,4},{6,7},{7,6},{8,9},{9,8},{10,11... | collective-permute-start | bytes 3145736 | tf_op jit(solution)/shard_map/ppermute | solution.py:162
  0.0 3.6 %collective-permute-start.9 = (bf16[64,16,256]{2,1,0:T(8,128)(2,1)}, bf16[64,16,256]{2,1,0:T(8,128)(2,1)S(1)}, u32[]{:S(2)}, u32[]{:S(2)}) collective-permute-start(bf16[64,16,256]{2,1,0:T(8,128)(2,1)} %own_v_ref.1), channel_id=1, source_target_pairs={{0,1},{1,0},{2,3},{3,2},{4,5},{5,4},{6,7},{7,6},{8,9},{9,8},{10,11... | collective-permute-start | bytes 1572872 | tf_op jit(solution)/shard_map/ppermute | solution.py:162
  0.5 0.7 copy-start.4
  1.2 0.7 copy-start.2
  1.9 1.8 %copy-start.5 = (bf16[64,16,256]{2,1,0:T(8,128)(2,1)S(1)}, bf16[64,16,256]{2,1,0:T(8,128)(2,1)}, u32[]{:S(2)}) copy-start(bf16[64,16,256]{2,1,0:T(8,128)(2,1)} %own_v_ref.1) | copy-start | bytes 1572868
  3.6 1.2 %copy-start = (bf16[64,16,512]{2,1,0:T(8,128)(2,1)S(1)}, bf16[64,16,512]{2,1,0:T(8,128)(2,1)}, u32[]{:S(2)}) copy-start(bf16[64,16,512]{2,1,0:T(8,128)(2,1)} %own_t_ref.1) | copy-start | bytes 3145732
  10.1 7.6 %copy-start.1 = (bf16[64,16,512]{2,1,0:T(8,128)(2,1)S(1)}, bf16[64,16,512]{2,1,0:T(8,128)(2,1)}, u32[]{:S(2)}) copy-start(bf16[64,16,512]{2,1,0:T(8,128)(2,1)} %own_t_ref.1) | copy-start | bytes 3145732
  10.1 23.9 %all-to-all-start.1 = ((bf16[8,256,256]{2,1,0:T(8,128)(2,1)}), bf16[8,256,256]{2,1,0:T(8,128)(2,1)S(1)}, u32[]{:S(2)}, u32[]{:S(2)}) async-start(bf16[8,256,256]{2,1,0:T(8,128)(2,1)} %shard_map.59), calls=%async_computation.1 | async-start | bytes 2097152 | tf_op jit(solution)/shard_map/all_to_all | solution.py:240
  34.0 11.4 %all-to-all-start = ((bf16[8,16,512]{2,1,0:T(8,128)(2,1)}), bf16[8,16,512]{2,1,0:T(8,128)(2,1)S(1)}, u32[]{:S(2)}, u32[]{:S(2)}) async-start(bf16[8,16,512]{2,1,0:T(8,128)(2,1)} %shard_map.55), calls=%async_computation | async-start | bytes 262144 | tf_op jit(solution)/shard_map/all_to_all | solution.py:190
  38.6 31.4 %collective-permute-start.10 = (bf16[256,256]{1,0:T(8,128)(2,1)S(1)}, bf16[256,256]{1,0:T(8,128)(2,1)S(1)}, u32[]{:S(2)}, u32[]{:S(2)}) collective-permute-start(bf16[256,256]{1,0:T(8,128)(2,1)S(1)} %reduce_sum.37.own_ref), channel_id=1, source_target_pairs={{0,1},{1,0},{2,3},{3,2},{4,5},{5,4},{6,7},{7,6},{8,9},{9,8},{10,11... | collective-permute-start | bytes 393224 | tf_op jit(solution)/shard_map/ppermute | solution.py:162
  45.5 3.8 %collective-permute-start = (bf16[16,512]{1,0:T(8,128)(2,1)S(1)}, bf16[16,512]{1,0:T(8,128)(2,1)S(1)}, u32[]{:S(2)}, u32[]{:S(2)}) collective-permute-start(bf16[16,512]{1,0:T(8,128)(2,1)S(1)} %reduce_sum.36.own_ref), channel_id=1, source_target_pairs={{0,2},{2,0},{1,3},{3,1},{4,6},{6,4},{5,7},{7,5},{8,10},{10,8},{9,1... | collective-permute-start | bytes 49160 | tf_op jit(solution)/shard_map/ppermute | solution.py:216
  49.3 12.8 %collective-permute-start.7 = (bf16[2,16,512]{2,1,0:T(8,128)(2,1)S(1)}, bf16[2,16,512]{2,1,0:T(8,128)(2,1)S(1)}, u32[]{:S(2)}, u32[]{:S(2)}) collective-permute-start(bf16[2,16,512]{2,1,0:T(8,128)(2,1)S(1)} %shard_map.56.refs_0_), channel_id=1, source_target_pairs={{0,28},{4,0},{8,4},{12,8},{16,12},{20,16},{24,20},{28,24},{1,29},{... | collective-permute-start | bytes 98312 | tf_op jit(solution)/shard_map/ppermute | solution.py:228
  55.2 7.0 %collective-permute-start.6 = (bf16[2,16,512]{2,1,0:T(8,128)(2,1)S(1)}, bf16[2,16,512]{2,1,0:T(8,128)(2,1)S(1)}, u32[]{:S(2)}, u32[]{:S(2)}) collective-permute-start(bf16[2,16,512]{2,1,0:T(8,128)(2,1)S(1)} %shard_map.56.refs_0_), channel_id=1, source_target_pairs={{0,24},{4,28},{8,0},{12,4},{16,8},{20,12},{24,16},{28,20},{1,25},{... | collective-permute-start | bytes 98312 | tf_op jit(solution)/shard_map/ppermute | solution.py:228
  56.6 8.0 %collective-permute-start.5 = (bf16[2,16,512]{2,1,0:T(8,128)(2,1)S(1)}, bf16[2,16,512]{2,1,0:T(8,128)(2,1)S(1)}, u32[]{:S(2)}, u32[]{:S(2)}) collective-permute-start(bf16[2,16,512]{2,1,0:T(8,128)(2,1)S(1)} %shard_map.56.refs_0_), channel_id=1, source_target_pairs={{0,20},{4,24},{8,28},{12,0},{16,4},{20,8},{24,12},{28,16},{1,21},{... | collective-permute-start | bytes 98312 | tf_op jit(solution)/shard_map/ppermute | solution.py:228
  57.1 9.4 %collective-permute-start.4 = (bf16[2,16,512]{2,1,0:T(8,128)(2,1)S(1)}, bf16[2,16,512]{2,1,0:T(8,128)(2,1)S(1)}, u32[]{:S(2)}, u32[]{:S(2)}) collective-permute-start(bf16[2,16,512]{2,1,0:T(8,128)(2,1)S(1)} %shard_map.56.refs_0_), channel_id=1, source_target_pairs={{0,16},{4,20},{8,24},{12,28},{16,0},{20,4},{24,8},{28,12},{1,17},{... | collective-permute-start | bytes 98312 | tf_op jit(solution)/shard_map/ppermute | solution.py:228
  62.1 6.9 %collective-permute-start.3 = (bf16[2,16,512]{2,1,0:T(8,128)(2,1)S(1)}, bf16[2,16,512]{2,1,0:T(8,128)(2,1)S(1)}, u32[]{:S(2)}, u32[]{:S(2)}) collective-permute-start(bf16[2,16,512]{2,1,0:T(8,128)(2,1)S(1)} %shard_map.56.refs_0_), channel_id=1, source_target_pairs={{0,12},{4,16},{8,20},{12,24},{16,28},{20,0},{24,4},{28,8},{1,13},{... | collective-permute-start | bytes 98312 | tf_op jit(solution)/shard_map/ppermute | solution.py:228
  62.1 7.7 %collective-permute-start.2 = (bf16[2,16,512]{2,1,0:T(8,128)(2,1)S(1)}, bf16[2,16,512]{2,1,0:T(8,128)(2,1)S(1)}, u32[]{:S(2)}, u32[]{:S(2)}) collective-permute-start(bf16[2,16,512]{2,1,0:T(8,128)(2,1)S(1)} %shard_map.56.refs_0_), channel_id=1, source_target_pairs={{0,8},{4,12},{8,16},{12,20},{16,24},{20,28},{24,0},{28,4},{1,9},{5... | collective-permute-start | bytes 98312 | tf_op jit(solution)/shard_map/ppermute | solution.py:228
  64.6 5.4 %collective-permute-start.1 = (bf16[2,16,512]{2,1,0:T(8,128)(2,1)S(1)}, bf16[2,16,512]{2,1,0:T(8,128)(2,1)S(1)}, u32[]{:S(2)}, u32[]{:S(2)}) collective-permute-start(bf16[2,16,512]{2,1,0:T(8,128)(2,1)S(1)} %shard_map.56.refs_0_), channel_id=1, source_target_pairs={{0,4},{4,8},{8,12},{12,16},{16,20},{20,24},{24,28},{28,0},{1,5},{5... | collective-permute-start | bytes 98312 | tf_op jit(solution)/shard_map/ppermute | solution.py:228
where the time goes:
time: 86.4 us; the launch traced here: 86.1 us
  starting transfers between devices  30.6 us (35%)
  waiting for transfers between devices  28.3 us (33%)
  blocking collectives  15.1 us (17%)
  Pallas kernels  8.59 us (10%)
  local copies, waits for them, and re-layouts  2.57 us (3%)
    ppermute x7, starting transfers between devices, stages(): lax.ppermute(joined, 'z', [(i, (i + distance) % count) for i in range(cou...  17.2 us
    all_to_all x1, blocking collectives, stages(): shares = lax.all_to_all(applied, PLANE, 0, 0, tiled=True)  15.1 us
    all_to_all x1, waiting for transfers between devices, stages(): pieces = lax.all_to_all(partial, ROW, 0, 0, tiled=True)  14.8 us
    all_to_all x1, starting transfers between devices, stages(): pieces = lax.all_to_all(partial, ROW, 0, 0, tiled=True)  7.59 us
    all_to_all x1, waiting for transfers between devices, stages(): picked = lax.all_to_all(picks, ROW, 0, 0, tiled=True)  6.71 us
    pallas_call x1, Pallas kernels, stages(): pl.pallas_call(panel_kernel, in_specs=[vmem] * 5, out_specs=vmem, out_sha...  5.25 us
    all_to_all x1, starting transfers between devices, stages(): picked = lax.all_to_all(picks, ROW, 0, 0, tiled=True)  4.44 us
    ppermute x7, waiting for transfers between devices, stages(): lax.ppermute(joined, 'z', [(i, (i + distance) % count) for i in range(cou...  3.5 us
  transfers between devices with their start and end apart: 13, of which 7 were waited for; matrix products, arithmetic and copies ran while one was open for 0% of the time, Pallas kernels for 4%

commit v1 on v0

--- a/solution.py
+++ b/solution.py
@@ -13,6 +13,7 @@
 ROW = ("yh", "x")
 COL = ("z", "yl", "core")
 PLANE = ("z", "yl")
+ROW_PAIR = ("yh", "x", "yl")
 
 
 def sine_of_angle(x):
@@ -38,7 +39,7 @@
 
 
 def picks_kernel(orders_ref, leg_ref, picks_ref, rows, sems):
-    panels, degrees, cycles = picks_ref.shape
+    panels, sharers, degrees, cycles = picks_ref.shape
     half = cycles // 2
     first_order = lax.axis_index(ROW) * leg_ref.shape[0]
     core = lax.axis_index("core")
@@ -57,7 +58,9 @@
         held = (place >= 0) & (place < leg_ref.shape[0])
         kept = degree >= jnp.where(held, orders_ref[p], leg_ref.shape[0] * lax.axis_size(ROW))
         for lanes, part in ((own, slice(0, half)), (other, slice(half, cycles))):
-            picks_ref[p, :, part] = jnp.where(kept, rows[p, :, lanes].astype(jnp.float32), 0.0).astype(jnp.bfloat16)
+            pick = jnp.where(kept, rows[p, :, lanes].astype(jnp.float32), 0.0).astype(jnp.bfloat16)
+            for sharer in range(sharers):
+                picks_ref[p, sharer, :, part] = pick
 
 
 def coef_kernel(orders_ref, span_ref, weight_ref, coef_ref):
@@ -133,21 +136,17 @@
 
 
 def join_kernel(own_ref, other_ref, out_ref):
-    yl = lax.axis_index("yl")
-    out_ref[yl] = own_ref[...]
-    out_ref[1 - yl] = other_ref[...]
+    mine = lax.rem(lax.axis_index("z"), 2)
+    out_ref[mine] = own_ref[...]
+    out_ref[1 - mine] = other_ref[...]
 
 
 def place_kernel(*refs):
     *row_refs, out_ref = refs
     count = len(row_refs)
-    degrees = row_refs[0].shape[1]
-    z = lax.axis_index("z")
+    pair = lax.div(lax.axis_index("z"), 2)
     for distance, row_ref in enumerate(row_refs):
-        origin = lax.rem(z + (count - distance), count)
-        for yl in range(2):
-            at = pl.multiple_of((origin * 2 + yl) * degrees, degrees)
-            out_ref[pl.ds(at, degrees), :] = row_ref[yl]
+        out_ref[lax.rem(pair + (count - distance), count)] = row_ref[...]
 
 
 def apply_kernel(rows_ref, own_ref, other_ref, out_ref):
@@ -179,15 +178,15 @@
         picks_kernel,
         in_specs=[smem, pl.BlockSpec(memory_space=pltpu.HBM)],
         out_specs=vmem,
-        out_shape=jax.ShapeDtypeStruct((panels, degrees, cycles), bf16),
+        out_shape=jax.ShapeDtypeStruct((panels, lax.axis_size("yl"), degrees, cycles), bf16),
         scratch_shapes=[
             pltpu.VMEM((panels, degrees, cycles), bf16),
             pltpu.SemaphoreType.DMA((panels,)),
         ],
         cost_estimate=pl.CostEstimate(flops=1_000_000, bytes_accessed=400_000, transcendentals=0),
-        compiler_params=params,
+        compiler_params=pltpu.CompilerParams(vmem_limit_bytes=61 * 1024 * 1024),
     )(panel_orders, legendre)
-    picked = lax.all_to_all(picks, ROW, 0, 0, tiled=True)
+    picked = lax.all_to_all(picks.reshape(-1, degrees, cycles), ROW_PAIR, 0, 0, tiled=True)
 
     coef = pl.pallas_call(
         coef_kernel,
@@ -212,30 +211,28 @@
         compiler_params=params,
     )(coef, legendre, other_tables, vectors, other_vectors)
 
-    rows = jnp.sum(picked.astype(jnp.float32), axis=0).astype(bf16)
-    paired = lax.ppermute(rows, "yl", [(0, 1), (1, 0)])
+    rows = jnp.sum(picked.reshape(picks.shape).astype(jnp.float32), axis=0).astype(bf16)
+    count = lax.axis_size("z")
+    paired = lax.ppermute(rows, "z", [(i, i ^ 1) for i in range(count)])
     joined = pl.pallas_call(
         join_kernel,
         in_specs=[vmem] * 2,
         out_specs=vmem,
-        out_shape=jax.ShapeDtypeStruct((2, degrees, cycles), bf16),
-        cost_estimate=pl.CostEstimate(flops=100_000, bytes_accessed=64_000, transcendentals=0),
+        out_shape=jax.ShapeDtypeStruct((2, *rows.shape), bf16),
+        cost_estimate=pl.CostEstimate(flops=100_000, bytes_accessed=128_000, transcendentals=0),
         compiler_params=params,
     )(rows, paired)
     spread = [joined]
-    count = lax.axis_size("z")
-    for distance in range(1, count):
+    for distance in range(2, count, 2):
         spread.append(lax.ppermute(joined, "z", [(i, (i + distance) % count) for i in range(count)]))
-
-    shared = 2 * count * degrees
     panel_rows = pl.pallas_call(
         place_kernel,
-        in_specs=[vmem] * count,
-        out_specs=vmem,
-        out_shape=jax.ShapeDtypeStruct((shared, cycles), bf16),
+        in_specs=[vmem] * len(spread),
+        out_specs=vmem,
+        out_shape=jax.ShapeDtypeStruct((len(spread), *joined.shape), bf16),
         cost_estimate=pl.CostEstimate(flops=500_000, bytes_accessed=500_000, transcendentals=0),
         compiler_params=params,
-    )(*spread)
+    )(*spread).reshape(-1, cycles)
 
     pieces = lax.all_to_all(partial, ROW, 0, 0, tiled=True)
     own = jnp.sum(pieces.astype(jnp.float32), axis=0).astype(bf16)
@@ -245,7 +242,7 @@
         in_specs=[vmem] * 3,
         out_specs=vmem,
         out_shape=jax.ShapeDtypeStruct((2 * count, degrees, vecs), bf16),
-        cost_estimate=pl.CostEstimate(flops=2 * shared * cycles * vecs, bytes_accessed=700_000, transcendentals=0),
+        cost_estimate=pl.CostEstimate(flops=2 * panel_rows.size * vecs, bytes_accessed=700_000, transcendentals=0),
         compiler_params=params,
     )(panel_rows, own, other)
     shares = lax.all_to_all(applied, PLANE, 0, 0, tiled=True)

time: 86.4 us -> 81.3 us (0.941)
  the two profiles are of different devices: /device:TPU:2 before, /device:TPU:8 now
where the time goes in v1:
time: 81.3 us; the launch traced here: 80.7 us
  waiting for transfers between devices  29.4 us (36%)
  starting transfers between devices  23.7 us (29%)
  blocking collectives  14.7 us (18%)
  Pallas kernels  9.49 us (12%)
  local copies, waits for them, and re-layouts  2.57 us (3%)
    all_to_all x1, waiting for transfers between devices, stages(): pieces = lax.all_to_all(partial, ROW, 0, 0, tiled=True)  15.1 us
    all_to_all x1, blocking collectives, stages(): shares = lax.all_to_all(applied, PLANE, 0, 0, tiled=True)  14.7 us
    ppermute x3, starting transfers between devices, stages(): lax.ppermute(joined, 'z', [(i, (i + distance) % count) for i in range(cou...  10.4 us
    all_to_all x1, waiting for transfers between devices, stages(): lax.all_to_all(picks.reshape(-1, degrees, cycles), ROW_PAIR, 0, 0, tiled=...  7.17 us
    all_to_all x1, starting transfers between devices, stages(): pieces = lax.all_to_all(partial, ROW, 0, 0, tiled=True)  6.02 us
    pallas_call x1, Pallas kernels, stages(): pl.pallas_call(panel_kernel, in_specs=[vmem] * 5, out_specs=vmem, out_sha...  5.34 us
    ppermute x3, waiting for transfers between devices, stages(): lax.ppermute(joined, 'z', [(i, (i + distance) % count) for i in range(cou...  4.83 us
    all_to_all x1, starting transfers between devices, stages(): lax.all_to_all(picks.reshape(-1, degrees, cycles), ROW_PAIR, 0, 0, tiled=...  4.67 us
  transfers between devices with their start and end apart: 9, of which 6 were waited for; matrix products, arithmetic and copies ran while one was open for 0% of the time, Pallas kernels for 5%

profile of v1, /device:TPU:8, one launch (start us, length us, event | category | flops | bytes accessed | tf_op | source)
XLA Modules:
  0.0 80.7 jit_solution(11212764445154321973)
XLA Ops:
  0.0 0.0 copy-start.2
  0.0 0.0 collective-permute-start.4
  0.0 0.5 collective-permute-start.5
  0.5 0.0 copy-start.3
  0.5 0.2 copy-done.2
  0.7 0.5 copy-done.3
  1.2 0.7 copy-done.1
  1.9 1.5 %shard_map.58.coef_ref = f32[8,64,256]{2,1,0:T(8,128)S(1)} custom-call(s32[8]{0:T(128)S(1)} %copy-done.3, s32[2,512]{1,0:T(2,128)S(1)} %bitcast.7, f32[1,512]{1,0:T(1,128)S(1)} %bitcast.8), custom_call_target="tpu_custom_call" | custom-call | flops 10000000 | bytes 500000 | tf_op jit(solution)/shard_map/pallas_call | solution.py:191
  3.3 0.3 collective-permute-done.5.other_v_ref
  3.6 0.0 collective-permute-done.4.other_t_ref
  3.6 0.0 copy-done.4
  3.6 1.2 %copy-done = bf16[64,16,512]{2,1,0:T(8,128)(2,1)S(1)} copy-done((bf16[64,16,512]{2,1,0:T(8,128)(2,1)S(1)}, bf16[64,16,512]{2,1,0:T(8,128)(2,1)}, u32[]{:S(2)}) %copy-start) | copy-done | bytes 1048600
  4.9 5.3 %shard_map.59 = bf16[8,256,256]{2,1,0:T(8,128)(2,1)} custom-call(f32[8,64,256]{2,1,0:T(8,128)S(1)} %shard_map.58.coef_ref, bf16[64,16,512]{2,1,0:T(8,128)(2,1)S(1)} %copy-done, bf16[64,16,512]{2,1,0:T(8,128)(2,1)S(1)} %collective-permute-done.4.other_t_ref, bf16[64,16,256]{2,1,0:T(8,128)(2,1)S(1)} %copy-done.4, ...), custom_call_target="tpu_custom_call" | custom-call | flops 2147483648 | bytes 3500000 | tf_op jit(solution)/shard_map/pallas_call | solution.py:199
  10.2 6.0 %all-to-all-start.1 = ((bf16[8,256,256]{2,1,0:T(8,128)(2,1)}), bf16[8,256,256]{2,1,0:T(8,128)(2,1)S(1)}, u32[]{:S(2)}, u32[]{:S(2)}) async-start(bf16[8,256,256]{2,1,0:T(8,128)(2,1)} %shard_map.59), calls=%async_computation.1 | async-start | bytes 2097152 | tf_op jit(solution)/shard_map/all_to_all | solution.py:237
  16.2 2.4 %shard_map.55 = bf16[8,2,16,512]{3,2,1,0:T(8,128)(2,1)} custom-call(s32[8]{0:T(128)} %orders_ref.3, bf16[64,16,512]{2,1,0:T(8,128)(2,1)} %own_t_ref.1), custom_call_target="tpu_custom_call" | custom-call | flops 1000000 | bytes 400000 | tf_op jit(solution)/shard_map/pallas_call | solution.py:177
  18.6 15.1 %all-to-all-done.1 = bf16[8,256,256]{2,1,0:T(8,128)(2,1)S(1)} async-done(((bf16[8,256,256]{2,1,0:T(8,128)(2,1)}), bf16[8,256,256]{2,1,0:T(8,128)(2,1)S(1)}, u32[]{:S(2)}, u32[]{:S(2)}) %all-to-all-start.1) | async-done | bytes 1048608 | tf_op jit(solution)/shard_map/all_to_all | solution.py:237
  33.7 4.7 %all-to-all-start = ((bf16[16,16,512]{2,1,0:T(8,128)(2,1)}), bf16[16,16,512]{2,1,0:T(8,128)(2,1)S(1)}, u32[]{:S(2)}, u32[]{:S(2)}) async-start(bf16[16,16,512]{2,1,0:T(8,128)(2,1)} %bitcast.9), calls=%async_computation | async-start | bytes 524288 | tf_op jit(solution)/shard_map/all_to_all | solution.py:189
  38.4 0.1 reduce_sum.37.own_ref
  38.6 0.1 collective-permute-start.6
  38.7 7.2 %all-to-all-done = bf16[16,16,512]{2,1,0:T(8,128)(2,1)S(1)} async-done(((bf16[16,16,512]{2,1,0:T(8,128)(2,1)}), bf16[16,16,512]{2,1,0:T(8,128)(2,1)S(1)}, u32[]{:S(2)}, u32[]{:S(2)}) %all-to-all-start) | async-done | bytes 262176 | tf_op jit(solution)/shard_map/all_to_all | solution.py:189
  45.9 2.0 %collective-permute-start = (bf16[2,16,512]{2,1,0:T(8,128)(2,1)S(1)}, bf16[2,16,512]{2,1,0:T(8,128)(2,1)S(1)}, u32[]{:S(2)}, u32[]{:S(2)}) collective-permute-start(bf16[2,16,512]{2,1,0:T(8,128)(2,1)S(1)} %reduce_sum.36.own_ref), channel_id=1, source_target_pairs={{0,4},{4,0},{8,12},{12,8},{16,20},{20,16},{24,28},{28,24},{1,5},{5... | collective-permute-start | bytes 98312 | tf_op jit(solution)/shard_map/ppermute | solution.py:216
  47.9 2.0 %collective-permute-done.other_ref = bf16[2,16,512]{2,1,0:T(8,128)(2,1)S(1)} collective-permute-done((bf16[2,16,512]{2,1,0:T(8,128)(2,1)S(1)}, bf16[2,16,512]{2,1,0:T(8,128)(2,1)S(1)}, u32[]{:S(2)}, u32[]{:S(2)}) %collective-permute-start) | collective-permute-done | bytes 32800 | tf_op jit(solution)/shard_map/ppermute | solution.py:216
  49.9 6.4 %collective-permute-start.3 = (bf16[2,2,16,512]{3,2,1,0:T(8,128)(2,1)S(1)}, bf16[2,2,16,512]{3,2,1,0:T(8,128)(2,1)S(1)}, u32[]{:S(2)}, u32[]{:S(2)}) collective-permute-start(bf16[2,2,16,512]{3,2,1,0:T(8,128)(2,1)S(1)} %shard_map.56.refs_0_), channel_id=1, source_target_pairs={{0,24},{4,28},{8,0},{12,4},{16,8},{20,12},{24,16},{28,20},{1,25},{... | collective-permute-start | bytes 196616 | tf_op jit(solution)/shard_map/ppermute | solution.py:227
  56.2 1.2 %collective-permute-start.2 = (bf16[2,2,16,512]{3,2,1,0:T(8,128)(2,1)S(1)}, bf16[2,2,16,512]{3,2,1,0:T(8,128)(2,1)S(1)}, u32[]{:S(2)}, u32[]{:S(2)}) collective-permute-start(bf16[2,2,16,512]{3,2,1,0:T(8,128)(2,1)S(1)} %shard_map.56.refs_0_), channel_id=1, source_target_pairs={{0,16},{4,20},{8,24},{12,28},{16,0},{20,4},{24,8},{28,12},{1,17},{... | collective-permute-start | bytes 196616 | tf_op jit(solution)/shard_map/ppermute | solution.py:227
  57.5 2.8 %collective-permute-start.1 = (bf16[2,2,16,512]{3,2,1,0:T(8,128)(2,1)S(1)}, bf16[2,2,16,512]{3,2,1,0:T(8,128)(2,1)S(1)}, u32[]{:S(2)}, u32[]{:S(2)}) collective-permute-start(bf16[2,2,16,512]{3,2,1,0:T(8,128)(2,1)S(1)} %shard_map.56.refs_0_), channel_id=1, source_target_pairs={{0,8},{4,12},{8,16},{12,20},{16,24},{20,28},{24,0},{28,4},{1,9},{5... | collective-permute-start | bytes 196616 | tf_op jit(solution)/shard_map/ppermute | solution.py:227
  60.3 0.0 collective-permute-done.3.refs_3_
  60.3 4.4 %collective-permute-done.2.refs_2_ = bf16[2,2,16,512]{3,2,1,0:T(8,128)(2,1)S(1)} collective-permute-done((bf16[2,2,16,512]{3,2,1,0:T(8,128)(2,1)S(1)}, bf16[2,2,16,512]{3,2,1,0:T(8,128)(2,1)S(1)}, u32[]{:S(2)}, u32[]{:S(2)}) %collective-permute-start.2) | collective-permute-done | bytes 65568 | tf_op jit(solution)/shard_map/ppermute | solution.py:227
  64.7 0.4 collective-permute-done.1.refs_1_
  65.2 0.0 collective-permute-done.6.other_ref
  65.2 0.3 shard_map.60
  65.4 14.7 %all_to_all.15 = bf16[16,16,256]{2,1,0:T(8,128)(2,1)S(1)} all-to-all(bf16[16,16,256]{2,1,0:T(8,128)(2,1)S(1)} %shard_map.60), channel_id=1, replica_groups=mesh['yh'=2,'x'=4,'z'=8,'yl'=2,'core'=2] {'z','yl'}, dimensions={0} | all-to-all | bytes 262144 | tf_op jit(solution)/shard_map/all_to_all | solution.py:248
  80.1 0.6 reduce_sum.38
  (6 shorter events, 0.1 us)
Async XLA Ops:
  0.0 0.7 copy-start.2
  0.0 3.6 %collective-permute-start.4 = (bf16[64,16,512]{2,1,0:T(8,128)(2,1)}, bf16[64,16,512]{2,1,0:T(8,128)(2,1)S(1)}, u32[]{:S(2)}, u32[]{:S(2)}) collective-permute-start(bf16[64,16,512]{2,1,0:T(8,128)(2,1)} %own_t_ref.1), channel_id=1, source_target_pairs={{0,1},{1,0},{2,3},{3,2},{4,5},{5,4},{6,7},{7,6},{8,9},{9,8},{10,11... | collective-permute-start | bytes 3145736 | tf_op jit(solution)/shard_map/ppermute | solution.py:161
  0.0 3.6 %collective-permute-start.5 = (bf16[64,16,256]{2,1,0:T(8,128)(2,1)}, bf16[64,16,256]{2,1,0:T(8,128)(2,1)S(1)}, u32[]{:S(2)}, u32[]{:S(2)}) collective-permute-start(bf16[64,16,256]{2,1,0:T(8,128)(2,1)} %own_v_ref.1), channel_id=1, source_target_pairs={{0,1},{1,0},{2,3},{3,2},{4,5},{5,4},{6,7},{7,6},{8,9},{9,8},{10,11... | collective-permute-start | bytes 1572872 | tf_op jit(solution)/shard_map/ppermute | solution.py:161
  0.5 0.7 copy-start.3
  1.2 0.7 copy-start.1
  1.9 1.8 %copy-start.4 = (bf16[64,16,256]{2,1,0:T(8,128)(2,1)S(1)}, bf16[64,16,256]{2,1,0:T(8,128)(2,1)}, u32[]{:S(2)}) copy-start(bf16[64,16,256]{2,1,0:T(8,128)(2,1)} %own_v_ref.1) | copy-start | bytes 1572868
  3.6 1.2 %copy-start = (bf16[64,16,512]{2,1,0:T(8,128)(2,1)S(1)}, bf16[64,16,512]{2,1,0:T(8,128)(2,1)}, u32[]{:S(2)}) copy-start(bf16[64,16,512]{2,1,0:T(8,128)(2,1)} %own_t_ref.1) | copy-start | bytes 3145732
  10.2 23.5 %all-to-all-start.1 = ((bf16[8,256,256]{2,1,0:T(8,128)(2,1)}), bf16[8,256,256]{2,1,0:T(8,128)(2,1)S(1)}, u32[]{:S(2)}, u32[]{:S(2)}) async-start(bf16[8,256,256]{2,1,0:T(8,128)(2,1)} %shard_map.59), calls=%async_computation.1 | async-start | bytes 2097152 | tf_op jit(solution)/shard_map/all_to_all | solution.py:237
  33.7 12.1 %all-to-all-start = ((bf16[16,16,512]{2,1,0:T(8,128)(2,1)}), bf16[16,16,512]{2,1,0:T(8,128)(2,1)S(1)}, u32[]{:S(2)}, u32[]{:S(2)}) async-start(bf16[16,16,512]{2,1,0:T(8,128)(2,1)} %bitcast.9), calls=%async_computation | async-start | bytes 524288 | tf_op jit(solution)/shard_map/all_to_all | solution.py:189
  38.6 26.6 %collective-permute-start.6 = (bf16[256,256]{1,0:T(8,128)(2,1)S(1)}, bf16[256,256]{1,0:T(8,128)(2,1)S(1)}, u32[]{:S(2)}, u32[]{:S(2)}) collective-permute-start(bf16[256,256]{1,0:T(8,128)(2,1)S(1)} %reduce_sum.37.own_ref), channel_id=1, source_target_pairs={{0,1},{1,0},{2,3},{3,2},{4,5},{5,4},{6,7},{7,6},{8,9},{9,8},{10,11... | collective-permute-start | bytes 393224 | tf_op jit(solution)/shard_map/ppermute | solution.py:161
  45.9 4.0 %collective-permute-start = (bf16[2,16,512]{2,1,0:T(8,128)(2,1)S(1)}, bf16[2,16,512]{2,1,0:T(8,128)(2,1)S(1)}, u32[]{:S(2)}, u32[]{:S(2)}) collective-permute-start(bf16[2,16,512]{2,1,0:T(8,128)(2,1)S(1)} %reduce_sum.36.own_ref), channel_id=1, source_target_pairs={{0,4},{4,0},{8,12},{12,8},{16,20},{20,16},{24,28},{28,24},{1,5},{5... | collective-permute-start | bytes 98312 | tf_op jit(solution)/shard_map/ppermute | solution.py:216
  49.9 10.4 %collective-permute-start.3 = (bf16[2,2,16,512]{3,2,1,0:T(8,128)(2,1)S(1)}, bf16[2,2,16,512]{3,2,1,0:T(8,128)(2,1)S(1)}, u32[]{:S(2)}, u32[]{:S(2)}) collective-permute-start(bf16[2,2,16,512]{3,2,1,0:T(8,128)(2,1)S(1)} %shard_map.56.refs_0_), channel_id=1, source_target_pairs={{0,24},{4,28},{8,0},{12,4},{16,8},{20,12},{24,16},{28,20},{1,25},{... | collective-permute-start | bytes 196616 | tf_op jit(solution)/shard_map/ppermute | solution.py:227
  56.2 8.4 %collective-permute-start.2 = (bf16[2,2,16,512]{3,2,1,0:T(8,128)(2,1)S(1)}, bf16[2,2,16,512]{3,2,1,0:T(8,128)(2,1)S(1)}, u32[]{:S(2)}, u32[]{:S(2)}) collective-permute-start(bf16[2,2,16,512]{3,2,1,0:T(8,128)(2,1)S(1)} %shard_map.56.refs_0_), channel_id=1, source_target_pairs={{0,16},{4,20},{8,24},{12,28},{16,0},{20,4},{24,8},{28,12},{1,17},{... | collective-permute-start | bytes 196616 | tf_op jit(solution)/shard_map/ppermute | solution.py:227
  57.5 7.7 %collective-permute-start.1 = (bf16[2,2,16,512]{3,2,1,0:T(8,128)(2,1)S(1)}, bf16[2,2,16,512]{3,2,1,0:T(8,128)(2,1)S(1)}, u32[]{:S(2)}, u32[]{:S(2)}) collective-permute-start(bf16[2,2,16,512]{3,2,1,0:T(8,128)(2,1)S(1)} %shard_map.56.refs_0_), channel_id=1, source_target_pairs={{0,8},{4,12},{8,16},{12,20},{16,24},{20,28},{24,0},{28,4},{1,9},{5... | collective-permute-start | bytes 196616 | tf_op jit(solution)/shard_map/ppermute | solution.py:227

commit v2 on v1

--- a/solution.py
+++ b/solution.py
@@ -38,62 +38,60 @@
     return jnp.where(zero, 0.0, jnp.float32(CELL) / jnp.where(zero, 1.0, sine))
 
 
-def picks_kernel(orders_ref, leg_ref, picks_ref, rows, sems):
+def front_kernel(orders_ref, span_ref, weight_ref, leg_ref, picks_ref, coef_ref, rows, sides, sems):
     panels, sharers, degrees, cycles = picks_ref.shape
-    half = cycles // 2
-    first_order = lax.axis_index(ROW) * leg_ref.shape[0]
+    orders, half = coef_ref.shape[1:]
+    first_order = lax.axis_index(ROW) * orders
     core = lax.axis_index("core")
-    first_degree = lax.axis_index(COL) * degrees
     own = pl.ds(pl.multiple_of(core * half, half), half)
     other = pl.ds(pl.multiple_of((1 - core) * half, half), half)
-    copies = []
-    for p in range(panels):
-        at = jnp.clip(orders_ref[p] - first_order, 0, leg_ref.shape[0] - 1)
-        copies.append(pltpu.make_async_copy(leg_ref.at[at], rows.at[p], sems.at[p]))
-        copies[-1].start()
-    degree = lax.broadcasted_iota(jnp.int32, (degrees, half), 0) + first_degree
-    for p in range(panels):
+    places = [jnp.clip(orders_ref[p] - first_order, 0, orders - 1) for p in range(panels)]
+    copies = [pltpu.make_async_copy(leg_ref.at[places[p]], rows.at[p], sems.at[p]) for p in range(panels)]
+    for copy in copies:
+        copy.start()
+
+    start, stop = span_ref[0:1, own], span_ref[1:2, own]
+    weight = 0.5 * weight_ref[0:1, own]
+    width = weight * (jnp.float32(CELL) * (stop - start).astype(jnp.float32))
+    quarter = NPHI // 4
+    sublane = lax.broadcasted_iota(jnp.int32, (panels, half), 0)
+    lane = lax.broadcasted_iota(jnp.int32, (orders, 128), 1)
+    panel_row, panel_lane = jnp.zeros_like(sublane), jnp.zeros_like(lane)
+    for p in range(panels):
+        panel_row = jnp.where(sublane == p, orders_ref[p], panel_row)
+        panel_lane = jnp.where(lane == p, orders_ref[p], panel_lane)
+    sides[0] = weight * sine_of_cells(panel_row * stop)
+    sides[1] = weight * sine_of_cells(panel_row * start)
+    sides[2] = weight * sine_of_cells(panel_row * stop + quarter)
+    sides[3] = weight * sine_of_cells(panel_row * start + quarter)
+    order = lax.broadcasted_iota(jnp.int32, (orders, half), 0) + first_order
+    sin_stop, cos_stop = sine_of_cells(order * stop), sine_of_cells(order * stop + quarter)
+    sin_start, cos_start = sine_of_cells(order * start), sine_of_cells(order * start + quarter)
+    column = lax.broadcasted_iota(jnp.int32, (orders, 128), 0) + first_order
+    over_sum, over_gap = half_denominator(panel_lane + column), half_denominator(panel_lane - column)
+    even, odd = over_sum + over_gap, over_sum - over_gap
+    for p in range(panels):
+        at = slice(p, p + 1)
+        coef_ref[p] = even[:, at] * (sides[0, at] * cos_stop - sides[1, at] * cos_start) + odd[:, at] * (
+            sides[2, at] * sin_stop - sides[3, at] * sin_start
+        )
+
+    degree = lax.broadcasted_iota(jnp.int32, (degrees, half), 0) + lax.axis_index(COL) * degrees
+    for p in range(panels):
+        panel = orders_ref[p]
+        held = (panel >= first_order) & (panel < first_order + orders)
+        zeros = jnp.where(held, jnp.where(panel == 0, 2.0, 1.0), 0.0)
+        at = pl.ds(places[p], 1)
+        coef_ref[p, at, :] = coef_ref[p, at, :] + zeros * width
         copies[p].wait()
-        place = orders_ref[p] - first_order
-        held = (place >= 0) & (place < leg_ref.shape[0])
-        kept = degree >= jnp.where(held, orders_ref[p], leg_ref.shape[0] * lax.axis_size(ROW))
+        kept = degree >= jnp.where(held, panel, orders * lax.axis_size(ROW))
         for lanes, part in ((own, slice(0, half)), (other, slice(half, cycles))):
             pick = jnp.where(kept, rows[p, :, lanes].astype(jnp.float32), 0.0).astype(jnp.bfloat16)
             for sharer in range(sharers):
                 picks_ref[p, sharer, :, part] = pick
 
 
-def coef_kernel(orders_ref, span_ref, weight_ref, coef_ref):
-    panels, orders, half = coef_ref.shape
-    own = pl.ds(pl.multiple_of(lax.axis_index("core") * half, half), half)
-    start, stop = span_ref[0:1, own], span_ref[1:2, own]
-    weight = 0.5 * weight_ref[0:1, own]
-    first_order = lax.axis_index(ROW) * orders
-    order = lax.broadcasted_iota(jnp.int32, (orders, half), 0) + first_order
-    quarter = NPHI // 4
-    sin_stop, cos_stop = sine_of_cells(order * stop), sine_of_cells(order * stop + quarter)
-    sin_start, cos_start = sine_of_cells(order * start), sine_of_cells(order * start + quarter)
-    width = weight * (jnp.float32(CELL) * (stop - start).astype(jnp.float32))
-    column = lax.broadcasted_iota(jnp.int32, (orders, 128), 0) + first_order
-    for p in range(panels):
-        panel = orders_ref[p]
-        panel_stop, panel_start = panel * stop, panel * start
-        a = weight * sine_of_cells(panel_stop)
-        b = weight * sine_of_cells(panel_start)
-        c = weight * sine_of_cells(panel_stop + quarter)
-        d = weight * sine_of_cells(panel_start + quarter)
-        over_sum, over_gap = half_denominator(panel + column), half_denominator(panel - column)
-        even = (over_sum + over_gap)[:, :1]
-        odd = (over_sum - over_gap)[:, :1]
-        at_zero = jnp.where(panel == column, 1.0, 0.0) + jnp.where(panel + column == 0, 1.0, 0.0)
-        coef_ref[p] = (
-            even * (a * cos_stop - b * cos_start)
-            + odd * (c * sin_stop - d * sin_start)
-            + at_zero[:, :1] * width
-        )
-
-
-def panel_kernel(coef_ref, own_t_ref, other_t_ref, own_v_ref, other_v_ref, out_ref, tables, turned):
+def panel_kernel(coef_ref, own_t_ref, other_t_ref, own_v_ref, other_v_ref, out_ref, tables, turned, sums, sems):
     panels, orders, half = coef_ref.shape
     degrees, vecs = own_v_ref.shape[1:]
     block = 256 // degrees
@@ -117,7 +115,14 @@
 
         lax.fori_loop(0, orders // block, prepare, 0)
 
+    def outgoing(p):
+        return pltpu.make_async_copy(sums.at[p], out_ref.at[p], sems.at[p])
+
     def per_panel(p, carry):
+        @pl.when(p > 0)
+        def _():
+            outgoing(jnp.maximum(p - 1, 0)).start()
+
         total = None
         for side in range(2):
             for first in range(0, orders, block):
@@ -129,10 +134,13 @@
                 columns = slice(first * degrees, (first + block) * degrees)
                 part = jnp.dot(turned[side, :, columns], weighted, preferred_element_type=jnp.float32)
                 total = part if total is None else total + part
-        out_ref[p] = total.astype(jnp.bfloat16)
+        sums[p] = total.astype(jnp.bfloat16)
         return carry
 
     lax.fori_loop(0, panels, per_panel, 0)
+    outgoing(panels - 1).start()
+    for p in range(panels):
+        outgoing(p).wait()
 
 
 def join_kernel(own_ref, other_ref, out_ref):
@@ -145,7 +153,8 @@
     *row_refs, out_ref = refs
     count = len(row_refs)
     pair = lax.div(lax.axis_index("z"), 2)
-    for distance, row_ref in enumerate(row_refs):
+    distances = sorted(range(count), key=lambda d: min(d, count - d))
+    for distance, row_ref in zip(distances, row_refs):
         out_ref[lax.rem(pair + (count - distance), count)] = row_ref[...]
 
 
@@ -174,36 +183,34 @@
 
     other_tables = swapped(legendre)
     other_vectors = swapped(vectors)
-    picks = pl.pallas_call(
-        picks_kernel,
-        in_specs=[smem, pl.BlockSpec(memory_space=pltpu.HBM)],
-        out_specs=vmem,
-        out_shape=jax.ShapeDtypeStruct((panels, lax.axis_size("yl"), degrees, cycles), bf16),
+    picks, coef = pl.pallas_call(
+        front_kernel,
+        in_specs=[smem, vmem, vmem, pl.BlockSpec(memory_space=pltpu.HBM)],
+        out_specs=[vmem, vmem],
+        out_shape=[
+            jax.ShapeDtypeStruct((panels, lax.axis_size("yl"), degrees, cycles), bf16),
+            jax.ShapeDtypeStruct((panels, orders, half), jnp.float32),
+        ],
         scratch_shapes=[
             pltpu.VMEM((panels, degrees, cycles), bf16),
+            pltpu.VMEM((4, panels, half), jnp.float32),
             pltpu.SemaphoreType.DMA((panels,)),
         ],
-        cost_estimate=pl.CostEstimate(flops=1_000_000, bytes_accessed=400_000, transcendentals=0),
-        compiler_params=pltpu.CompilerParams(vmem_limit_bytes=61 * 1024 * 1024),
-    )(panel_orders, legendre)
+        cost_estimate=pl.CostEstimate(flops=10_000_000, bytes_accessed=900_000, transcendentals=0),
+        compiler_params=pltpu.CompilerParams(vmem_limit_bytes=60 * 1024 * 1024),
+    )(panel_orders, cycle_span.T, cycle_weight.reshape(1, cycles), legendre)
     picked = lax.all_to_all(picks.reshape(-1, degrees, cycles), ROW_PAIR, 0, 0, tiled=True)
 
-    coef = pl.pallas_call(
-        coef_kernel,
-        in_specs=[smem, vmem, vmem],
-        out_specs=vmem,
-        out_shape=jax.ShapeDtypeStruct((panels, orders, half), jnp.float32),
-        cost_estimate=pl.CostEstimate(flops=10_000_000, bytes_accessed=500_000, transcendentals=0),
-        compiler_params=params,
-    )(panel_orders, cycle_span.T, cycle_weight.reshape(1, cycles))
     partial = pl.pallas_call(
         panel_kernel,
         in_specs=[vmem] * 5,
-        out_specs=vmem,
+        out_specs=pl.BlockSpec(memory_space=pltpu.HBM),
         out_shape=jax.ShapeDtypeStruct((panels, vecs, half), bf16),
         scratch_shapes=[
             pltpu.VMEM((2, orders, degrees, half), bf16),
             pltpu.VMEM((2, vecs, pairs), bf16),
+            pltpu.VMEM((panels, vecs, half), bf16),
+            pltpu.SemaphoreType.DMA((panels,)),
         ],
         cost_estimate=pl.CostEstimate(
             flops=2 * panels * vecs * half * 2 * pairs, bytes_accessed=3_500_000, transcendentals=0
@@ -223,7 +230,7 @@
         compiler_params=params,
     )(rows, paired)
     spread = [joined]
-    for distance in range(2, count, 2):
+    for distance in sorted(range(2, count, 2), key=lambda d: min(d, count - d)):
         spread.append(lax.ppermute(joined, "z", [(i, (i + distance) % count) for i in range(count)]))
     panel_rows = pl.pallas_call(
         place_kernel,

time: 81.3 us -> 82.5 us (1.015)
  blocking collectives: 14.7 us -> 39.9 us
  waiting for transfers between devices: 29.4 us -> 13.1 us
  starting transfers between devices: 23.7 us -> 17.5 us
  Pallas kernels: 9.49 us -> 8.66 us
    all_to_all x0 -> x1, blocking collectives: none -> 23.3 us  [stages(): pieces = lax.all_to_all(partial, ROW, 0, 0, tiled=True)]
    all_to_all x1 -> x0, waiting for transfers between devices: 15.1 us -> none  [stages(): pieces = lax.all_to_all(partial, ROW, 0, 0, tiled=True)]
    all_to_all x1 -> x0, starting transfers between devices: 6.02 us -> none  [stages(): pieces = lax.all_to_all(partial, ROW, 0, 0, tiled=True)]
    all_to_all x1, blocking collectives: 14.7 us -> 16.5 us  [stages(): shares = lax.all_to_all(applied, PLANE, 0, 0, tiled=True)]
    ppermute x3, waiting for transfers between devices: 4.83 us -> 3.65 us  [stages(): lax.ppermute(joined, 'z', [(i, (i + distance) % count) for i in range(cou...]
    pallas_call x3 -> x2, Pallas kernels: 9.19 us -> 8.36 us  [the longest x1 5.69 us: stages(): pl.pallas_call(panel_kernel, in_specs=[vmem] * 5, out_specs=pl.BlockSpec(...]
    unnamed x10 -> x6, local copies, waits for them, and re-layouts: 2.57 us -> 2.09 us
  transfers between devices with their start and end apart: 9 -> 8, of which waited for: 6 -> 5; matrix products, arithmetic and copies ran while one was open for 0% -> 0% of each run, Pallas kernels for 5% -> 3%
where the time goes in v2:
time: 82.5 us; the launch traced here: 82.1 us
  blocking collectives  39.9 us (48%)
  starting transfers between devices  17.5 us (21%)
  waiting for transfers between devices  13.1 us (16%)
  Pallas kernels  8.66 us (10%)
  local copies, waits for them, and re-layouts  2.09 us (3%)
    all_to_all x1, blocking collectives, stages(): pieces = lax.all_to_all(partial, ROW, 0, 0, tiled=True)  23.3 us
    all_to_all x1, blocking collectives, stages(): shares = lax.all_to_all(applied, PLANE, 0, 0, tiled=True)  16.5 us
    ppermute x3, starting transfers between devices, stages(): lax.ppermute(joined, 'z', [(i, (i + distance) % count) for i in range(cou...  10.2 us
    all_to_all x1, waiting for transfers between devices, stages(): lax.all_to_all(picks.reshape(-1, degrees, cycles), ROW_PAIR, 0, 0, tiled=...  6.99 us
    pallas_call x1, Pallas kernels, stages(): pl.pallas_call(panel_kernel, in_specs=[vmem] * 5, out_specs=pl.BlockSpec(...  5.69 us
    all_to_all x1, starting transfers between devices, stages(): lax.all_to_all(picks.reshape(-1, degrees, cycles), ROW_PAIR, 0, 0, tiled=...  4.67 us
    ppermute x3, waiting for transfers between devices, stages(): lax.ppermute(joined, 'z', [(i, (i + distance) % count) for i in range(cou...  3.65 us
    pallas_call x1, Pallas kernels, stages(): pl.pallas_call(front_kernel, in_specs=[smem, vmem, vmem, pl.BlockSpec(mem...  2.67 us
  transfers between devices with their start and end apart: 8, of which 5 were waited for; matrix products, arithmetic and copies ran while one was open for 0% of the time, Pallas kernels for 3%

profile of v2, /device:TPU:8, one launch (start us, length us, event | category | flops | bytes accessed | tf_op | source)
XLA Modules:
  0.0 82.1 jit_solution(4176968520505549578)
XLA Ops:
  0.0 0.0 copy-start
  0.0 0.0 collective-permute-start.4
  0.0 0.5 collective-permute-start.5
  0.5 2.7 %shard_map.55 = (bf16[8,2,16,512]{3,2,1,0:T(8,128)(2,1)}, f32[8,64,256]{2,1,0:T(8,128)}) custom-call(s32[8]{0:T(128)} %orders_ref.1, s32[2,512]{1,0:T(2,128)} %bitcast.8, f32[1,512]{1,0:T(1,128)} %bitcast.9, bf16[64,16,512]{2,1,0:T(8,128)(2,1)} %own_t_ref.1), custom_call_target="tpu_custom_call" | custom-call | flops 10000000 | bytes 900000 | tf_op jit(solution)/shard_map/pallas_call | solution.py:186
  3.2 0.4 collective-permute-done.5.other_v_ref
  3.6 0.0 collective-permute-done.4.other_t_ref
  3.6 0.0 copy-done
  3.6 0.0 copy-start.1
  3.6 1.0 %copy-done.1 = bf16[64,16,256]{2,1,0:T(8,128)(2,1)S(1)} copy-done((bf16[64,16,256]{2,1,0:T(8,128)(2,1)S(1)}, bf16[64,16,256]{2,1,0:T(8,128)(2,1)}, u32[]{:S(2)}) %copy-start.1) | copy-done | bytes 524312
  4.7 0.0 copy-start.2
  4.7 1.0 %copy-done.2 = f32[8,64,256]{2,1,0:T(8,128)S(1)} copy-done((f32[8,64,256]{2,1,0:T(8,128)S(1)}, f32[8,64,256]{2,1,0:T(8,128)}, u32[]{:S(2)}) %copy-start.2) | copy-done | bytes 524312
  5.7 5.7 %shard_map.58 = bf16[8,256,256]{2,1,0:T(8,128)(2,1)S(1)} custom-call(f32[8,64,256]{2,1,0:T(8,128)S(1)} %copy-done.2, bf16[64,16,512]{2,1,0:T(8,128)(2,1)S(1)} %copy-done, bf16[64,16,512]{2,1,0:T(8,128)(2,1)S(1)} %collective-permute-done.4.other_t_ref, bf16[64,16,256]{2,1,0:T(8,128)(2,1)S(1)} %copy-done.1, ...), custom_call_target="tpu_custom_call" | custom-call | flops 2147483648 | bytes 3500000 | tf_op jit(solution)/shard_map/pallas_call | solution.py:204
  11.4 23.3 %all_to_all.15 = bf16[8,256,256]{2,1,0:T(8,128)(2,1)S(1)} all-to-all(bf16[8,256,256]{2,1,0:T(8,128)(2,1)S(1)} %shard_map.58), channel_id=1, replica_groups=mesh['yh'=2,'x'=4,'z'=8,'yl'=2,'core'=2] {'yh','x'}, dimensions={0} | all-to-all | bytes 2097152 | tf_op jit(solution)/shard_map/all_to_all | solution.py:244
  34.8 4.7 %all-to-all-start = ((bf16[16,16,512]{2,1,0:T(8,128)(2,1)}), bf16[16,16,512]{2,1,0:T(8,128)(2,1)S(1)}, u32[]{:S(2)}, u32[]{:S(2)}) async-start(bf16[16,16,512]{2,1,0:T(8,128)(2,1)} %bitcast.2), calls=%async_computation | async-start | bytes 524288 | tf_op jit(solution)/shard_map/all_to_all | solution.py:202
  39.4 0.1 reduce_sum.37.own_ref
  39.6 0.1 collective-permute-start.6
  39.7 7.0 %all-to-all-done = bf16[16,16,512]{2,1,0:T(8,128)(2,1)S(1)} async-done(((bf16[16,16,512]{2,1,0:T(8,128)(2,1)}), bf16[16,16,512]{2,1,0:T(8,128)(2,1)S(1)}, u32[]{:S(2)}, u32[]{:S(2)}) %all-to-all-start) | async-done | bytes 262176 | tf_op jit(solution)/shard_map/all_to_all | solution.py:202
  46.7 2.0 %collective-permute-start = (bf16[2,16,512]{2,1,0:T(8,128)(2,1)S(1)}, bf16[2,16,512]{2,1,0:T(8,128)(2,1)S(1)}, u32[]{:S(2)}, u32[]{:S(2)}) collective-permute-start(bf16[2,16,512]{2,1,0:T(8,128)(2,1)S(1)} %reduce_sum.36.own_ref), channel_id=1, source_target_pairs={{0,4},{4,0},{8,12},{12,8},{16,20},{20,16},{24,28},{28,24},{1,5},{5... | collective-permute-start | bytes 98312 | tf_op jit(solution)/shard_map/ppermute | solution.py:223
  48.7 2.0 %collective-permute-done.other_ref = bf16[2,16,512]{2,1,0:T(8,128)(2,1)S(1)} collective-permute-done((bf16[2,16,512]{2,1,0:T(8,128)(2,1)S(1)}, bf16[2,16,512]{2,1,0:T(8,128)(2,1)S(1)}, u32[]{:S(2)}, u32[]{:S(2)}) %collective-permute-start) | collective-permute-done | bytes 32800 | tf_op jit(solution)/shard_map/ppermute | solution.py:223
  50.7 7.3 %collective-permute-start.3 = (bf16[2,2,16,512]{3,2,1,0:T(8,128)(2,1)S(1)}, bf16[2,2,16,512]{3,2,1,0:T(8,128)(2,1)S(1)}, u32[]{:S(2)}, u32[]{:S(2)}) collective-permute-start(bf16[2,2,16,512]{3,2,1,0:T(8,128)(2,1)S(1)} %shard_map.56.refs_0_), channel_id=1, source_target_pairs={{0,16},{4,20},{8,24},{12,28},{16,0},{20,4},{24,8},{28,12},{1,17},{... | collective-permute-start | bytes 196616 | tf_op jit(solution)/shard_map/ppermute | solution.py:234
  58.0 0.0 collective-permute-start.2
  58.0 2.9 %collective-permute-start.1 = (bf16[2,2,16,512]{3,2,1,0:T(8,128)(2,1)S(1)}, bf16[2,2,16,512]{3,2,1,0:T(8,128)(2,1)S(1)}, u32[]{:S(2)}, u32[]{:S(2)}) collective-permute-start(bf16[2,2,16,512]{3,2,1,0:T(8,128)(2,1)S(1)} %shard_map.56.refs_0_), channel_id=1, source_target_pairs={{0,8},{4,12},{8,16},{12,20},{16,24},{20,28},{24,0},{28,4},{1,9},{5... | collective-permute-start | bytes 196616 | tf_op jit(solution)/shard_map/ppermute | solution.py:234
  60.9 0.2 collective-permute-done.3.refs_3_
  61.2 3.4 %collective-permute-done.2.refs_2_ = bf16[2,2,16,512]{3,2,1,0:T(8,128)(2,1)S(1)} collective-permute-done((bf16[2,2,16,512]{3,2,1,0:T(8,128)(2,1)S(1)}, bf16[2,2,16,512]{3,2,1,0:T(8,128)(2,1)S(1)}, u32[]{:S(2)}, u32[]{:S(2)}) %collective-permute-start.2) | collective-permute-done | bytes 65568 | tf_op jit(solution)/shard_map/ppermute | solution.py:234
  64.6 0.0 collective-permute-done.1.refs_1_
  64.6 0.0 collective-permute-done.6.other_ref
  64.6 0.3 shard_map.59
  64.9 16.5 %all_to_all.16 = bf16[16,16,256]{2,1,0:T(8,128)(2,1)S(1)} all-to-all(bf16[16,16,256]{2,1,0:T(8,128)(2,1)S(1)} %shard_map.59), channel_id=1, replica_groups=mesh['yh'=2,'x'=4,'z'=8,'yl'=2,'core'=2] {'z','yl'}, dimensions={0} | all-to-all | bytes 262144 | tf_op jit(solution)/shard_map/all_to_all | solution.py:255
  81.4 0.6 reduce_sum.38
  (3 shorter events, 0.1 us)
Async XLA Ops:
  0.0 3.6 %copy-start = (bf16[64,16,512]{2,1,0:T(8,128)(2,1)S(1)}, bf16[64,16,512]{2,1,0:T(8,128)(2,1)}, u32[]{:S(2)}) copy-start(bf16[64,16,512]{2,1,0:T(8,128)(2,1)} %own_t_ref.1) | copy-start | bytes 3145732
  0.0 3.6 %collective-permute-start.4 = (bf16[64,16,512]{2,1,0:T(8,128)(2,1)}, bf16[64,16,512]{2,1,0:T(8,128)(2,1)S(1)}, u32[]{:S(2)}, u32[]{:S(2)}) collective-permute-start(bf16[64,16,512]{2,1,0:T(8,128)(2,1)} %own_t_ref.1), channel_id=1, source_target_pairs={{0,1},{1,0},{2,3},{3,2},{4,5},{5,4},{6,7},{7,6},{8,9},{9,8},{10,11... | collective-permute-start | bytes 3145736 | tf_op jit(solution)/shard_map/ppermute | solution.py:170
  0.0 3.6 %collective-permute-start.5 = (bf16[64,16,256]{2,1,0:T(8,128)(2,1)}, bf16[64,16,256]{2,1,0:T(8,128)(2,1)S(1)}, u32[]{:S(2)}, u32[]{:S(2)}) collective-permute-start(bf16[64,16,256]{2,1,0:T(8,128)(2,1)} %own_v_ref.1), channel_id=1, source_target_pairs={{0,1},{1,0},{2,3},{3,2},{4,5},{5,4},{6,7},{7,6},{8,9},{9,8},{10,11... | collective-permute-start | bytes 1572872 | tf_op jit(solution)/shard_map/ppermute | solution.py:170
  3.6 1.0 %copy-start.1 = (bf16[64,16,256]{2,1,0:T(8,128)(2,1)S(1)}, bf16[64,16,256]{2,1,0:T(8,128)(2,1)}, u32[]{:S(2)}) copy-start(bf16[64,16,256]{2,1,0:T(8,128)(2,1)} %own_v_ref.1) | copy-start | bytes 1572868
  4.7 1.0 %copy-start.2 = (f32[8,64,256]{2,1,0:T(8,128)S(1)}, f32[8,64,256]{2,1,0:T(8,128)}, u32[]{:S(2)}) copy-start(f32[8,64,256]{2,1,0:T(8,128)} %get-tuple-element.8.coef_ref) | copy-start | bytes 1572868
  34.8 11.9 %all-to-all-start = ((bf16[16,16,512]{2,1,0:T(8,128)(2,1)}), bf16[16,16,512]{2,1,0:T(8,128)(2,1)S(1)}, u32[]{:S(2)}, u32[]{:S(2)}) async-start(bf16[16,16,512]{2,1,0:T(8,128)(2,1)} %bitcast.2), calls=%async_computation | async-start | bytes 524288 | tf_op jit(solution)/shard_map/all_to_all | solution.py:202
  39.6 25.0 %collective-permute-start.6 = (bf16[256,256]{1,0:T(8,128)(2,1)S(1)}, bf16[256,256]{1,0:T(8,128)(2,1)S(1)}, u32[]{:S(2)}, u32[]{:S(2)}) collective-permute-start(bf16[256,256]{1,0:T(8,128)(2,1)S(1)} %reduce_sum.37.own_ref), channel_id=1, source_target_pairs={{0,1},{1,0},{2,3},{3,2},{4,5},{5,4},{6,7},{7,6},{8,9},{9,8},{10,11... | collective-permute-start | bytes 393224 | tf_op jit(solution)/shard_map/ppermute | solution.py:170
  46.7 4.0 %collective-permute-start = (bf16[2,16,512]{2,1,0:T(8,128)(2,1)S(1)}, bf16[2,16,512]{2,1,0:T(8,128)(2,1)S(1)}, u32[]{:S(2)}, u32[]{:S(2)}) collective-permute-start(bf16[2,16,512]{2,1,0:T(8,128)(2,1)S(1)} %reduce_sum.36.own_ref), channel_id=1, source_target_pairs={{0,4},{4,0},{8,12},{12,8},{16,20},{20,16},{24,28},{28,24},{1,5},{5... | collective-permute-start | bytes 98312 | tf_op jit(solution)/shard_map/ppermute | solution.py:223
  50.7 10.4 %collective-permute-start.3 = (bf16[2,2,16,512]{3,2,1,0:T(8,128)(2,1)S(1)}, bf16[2,2,16,512]{3,2,1,0:T(8,128)(2,1)S(1)}, u32[]{:S(2)}, u32[]{:S(2)}) collective-permute-start(bf16[2,2,16,512]{3,2,1,0:T(8,128)(2,1)S(1)} %shard_map.56.refs_0_), channel_id=1, source_target_pairs={{0,16},{4,20},{8,24},{12,28},{16,0},{20,4},{24,8},{28,12},{1,17},{... | collective-permute-start | bytes 196616 | tf_op jit(solution)/shard_map/ppermute | solution.py:234
  58.0 6.6 %collective-permute-start.2 = (bf16[2,2,16,512]{3,2,1,0:T(8,128)(2,1)S(1)}, bf16[2,2,16,512]{3,2,1,0:T(8,128)(2,1)S(1)}, u32[]{:S(2)}, u32[]{:S(2)}) collective-permute-start(bf16[2,2,16,512]{3,2,1,0:T(8,128)(2,1)S(1)} %shard_map.56.refs_0_), channel_id=1, source_target_pairs={{0,24},{4,28},{8,0},{12,4},{16,8},{20,12},{24,16},{28,20},{1,25},{... | collective-permute-start | bytes 196616 | tf_op jit(solution)/shard_map/ppermute | solution.py:234
  58.0 6.6 %collective-permute-start.1 = (bf16[2,2,16,512]{3,2,1,0:T(8,128)(2,1)S(1)}, bf16[2,2,16,512]{3,2,1,0:T(8,128)(2,1)S(1)}, u32[]{:S(2)}, u32[]{:S(2)}) collective-permute-start(bf16[2,2,16,512]{3,2,1,0:T(8,128)(2,1)S(1)} %shard_map.56.refs_0_), channel_id=1, source_target_pairs={{0,8},{4,12},{8,16},{12,20},{16,24},{20,28},{24,0},{28,4},{1,9},{5... | collective-permute-start | bytes 196616 | tf_op jit(solution)/shard_map/ppermute | solution.py:234

commit v3 on v2

--- a/solution.py
+++ b/solution.py
@@ -38,18 +38,35 @@
     return jnp.where(zero, 0.0, jnp.float32(CELL) / jnp.where(zero, 1.0, sine))
 
 
-def front_kernel(orders_ref, span_ref, weight_ref, leg_ref, picks_ref, coef_ref, rows, sides, sems):
+def picks_kernel(orders_ref, leg_ref, picks_ref, rows, sems):
     panels, sharers, degrees, cycles = picks_ref.shape
-    orders, half = coef_ref.shape[1:]
+    orders = leg_ref.shape[0]
+    half = cycles // 2
     first_order = lax.axis_index(ROW) * orders
     core = lax.axis_index("core")
     own = pl.ds(pl.multiple_of(core * half, half), half)
     other = pl.ds(pl.multiple_of((1 - core) * half, half), half)
-    places = [jnp.clip(orders_ref[p] - first_order, 0, orders - 1) for p in range(panels)]
-    copies = [pltpu.make_async_copy(leg_ref.at[places[p]], rows.at[p], sems.at[p]) for p in range(panels)]
-    for copy in copies:
-        copy.start()
-
+    copies = []
+    for p in range(panels):
+        place = jnp.clip(orders_ref[p] - first_order, 0, orders - 1)
+        copies.append(pltpu.make_async_copy(leg_ref.at[place], rows.at[p], sems.at[p]))
+        copies[p].start()
+    degree = lax.broadcasted_iota(jnp.int32, (degrees, half), 0) + lax.axis_index(COL) * degrees
+    for p in range(panels):
+        panel = orders_ref[p]
+        held = (panel >= first_order) & (panel < first_order + orders)
+        kept = degree >= jnp.where(held, panel, orders * lax.axis_size(ROW))
+        copies[p].wait()
+        for lanes, part in ((own, slice(0, half)), (other, slice(half, cycles))):
+            pick = jnp.where(kept, rows[p, :, lanes].astype(jnp.float32), 0.0).astype(jnp.bfloat16)
+            for sharer in range(sharers):
+                picks_ref[p, sharer, :, part] = pick
+
+
+def fill_coefs(orders_ref, span_ref, weight_ref, coefs, sides):
+    panels, orders, half = coefs.shape
+    first_order = lax.axis_index(ROW) * orders
+    own = pl.ds(pl.multiple_of(lax.axis_index("core") * half, half), half)
     start, stop = span_ref[0:1, own], span_ref[1:2, own]
     weight = 0.5 * weight_ref[0:1, own]
     width = weight * (jnp.float32(CELL) * (stop - start).astype(jnp.float32))
@@ -72,27 +89,20 @@
     even, odd = over_sum + over_gap, over_sum - over_gap
     for p in range(panels):
         at = slice(p, p + 1)
-        coef_ref[p] = even[:, at] * (sides[0, at] * cos_stop - sides[1, at] * cos_start) + odd[:, at] * (
+        coefs[p] = even[:, at] * (sides[0, at] * cos_stop - sides[1, at] * cos_start) + odd[:, at] * (
             sides[2, at] * sin_stop - sides[3, at] * sin_start
         )
-
-    degree = lax.broadcasted_iota(jnp.int32, (degrees, half), 0) + lax.axis_index(COL) * degrees
     for p in range(panels):
         panel = orders_ref[p]
         held = (panel >= first_order) & (panel < first_order + orders)
         zeros = jnp.where(held, jnp.where(panel == 0, 2.0, 1.0), 0.0)
-        at = pl.ds(places[p], 1)
-        coef_ref[p, at, :] = coef_ref[p, at, :] + zeros * width
-        copies[p].wait()
-        kept = degree >= jnp.where(held, panel, orders * lax.axis_size(ROW))
-        for lanes, part in ((own, slice(0, half)), (other, slice(half, cycles))):
-            pick = jnp.where(kept, rows[p, :, lanes].astype(jnp.float32), 0.0).astype(jnp.bfloat16)
-            for sharer in range(sharers):
-                picks_ref[p, sharer, :, part] = pick
-
-
-def panel_kernel(coef_ref, own_t_ref, other_t_ref, own_v_ref, other_v_ref, out_ref, tables, turned, sums, sems):
-    panels, orders, half = coef_ref.shape
+        at = pl.ds(jnp.clip(panel - first_order, 0, orders - 1), 1)
+        coefs[p, at, :] = coefs[p, at, :] + zeros * width
+
+
+def panel_kernel(orders_ref, span_ref, weight_ref, own_t_ref, other_t_ref, own_v_ref, other_v_ref, out_ref, *scratch):
+    coefs, sides, tables, turned, sums, sem = scratch
+    panels, orders, half = coefs.shape
     degrees, vecs = own_v_ref.shape[1:]
     block = 256 // degrees
     core = lax.axis_index("core")
@@ -100,47 +110,29 @@
     first_order = lax.axis_index(ROW) * orders
     pair_degree = lax.axis_index(PLANE) * (2 * degrees)
     degree = lax.broadcasted_iota(jnp.int32, (degrees, half), 0)
-    for side, (t_ref, v_ref) in enumerate(((own_t_ref, own_v_ref), (other_t_ref, other_v_ref))):
-        offset = core if side == 0 else 1 - core
+    fill_coefs(orders_ref, span_ref, weight_ref, coefs, sides)
+    blocks = []
+    for t_ref, v_ref, offset in ((own_t_ref, own_v_ref, core), (other_t_ref, other_v_ref, 1 - core)):
         gap = degree + (pair_degree + offset * degrees - first_order)
-
-        def prepare(step, carry, side=side, t_ref=t_ref, v_ref=v_ref, gap=gap):
-            start = pl.multiple_of(step * block, block)
+        blocks += [(t_ref, v_ref, gap, first) for first in range(0, orders, block)]
+    for p in range(panels):
+        total = None
+        for index, (t_ref, v_ref, gap, first) in enumerate(blocks):
+            if p == 0:
+                for i in range(block):
+                    table = t_ref[first + i, :, lanes].astype(jnp.float32)
+                    tables[index, i] = jnp.where(gap >= first + i, table, 0.0).astype(jnp.bfloat16)
+                turned[index] = v_ref[first : first + block].reshape(block * degrees, vecs).T
+            rows = []
             for i in range(block):
-                table = t_ref[start + i, :, lanes].astype(jnp.float32)
-                tables[side, start + i] = jnp.where(gap - start >= i, table, 0.0).astype(jnp.bfloat16)
-            columns = pl.ds(pl.multiple_of(step * block * degrees, block * degrees), block * degrees)
-            turned[side, :, columns] = v_ref[pl.ds(start, block)].reshape(block * degrees, vecs).T
-            return carry
-
-        lax.fori_loop(0, orders // block, prepare, 0)
-
-    def outgoing(p):
-        return pltpu.make_async_copy(sums.at[p], out_ref.at[p], sems.at[p])
-
-    def per_panel(p, carry):
-        @pl.when(p > 0)
-        def _():
-            outgoing(jnp.maximum(p - 1, 0)).start()
-
-        total = None
-        for side in range(2):
-            for first in range(0, orders, block):
-                rows = []
-                for o in range(first, first + block):
-                    coef = jnp.broadcast_to(coef_ref[p, pl.ds(o, 1), :], (degrees, half))
-                    rows.append(coef.astype(jnp.bfloat16) * tables[side, o])
-                weighted = jnp.concatenate(rows, axis=0)
-                columns = slice(first * degrees, (first + block) * degrees)
-                part = jnp.dot(turned[side, :, columns], weighted, preferred_element_type=jnp.float32)
-                total = part if total is None else total + part
+                coef = jnp.broadcast_to(coefs[p, pl.ds(first + i, 1), :], (degrees, half))
+                rows.append(coef.astype(jnp.bfloat16) * tables[index, i])
+            part = jnp.dot(turned[index], jnp.concatenate(rows, axis=0), preferred_element_type=jnp.float32)
+            total = part if total is None else total + part
         sums[p] = total.astype(jnp.bfloat16)
-        return carry
-
-    lax.fori_loop(0, panels, per_panel, 0)
-    outgoing(panels - 1).start()
-    for p in range(panels):
-        outgoing(p).wait()
+    store = pltpu.make_async_copy(sums, out_ref, sem)
+    store.start()
+    store.wait()
 
 
 def join_kernel(own_ref, other_ref, out_ref):
@@ -183,40 +175,46 @@
 
     other_tables = swapped(legendre)
     other_vectors = swapped(vectors)
-    picks, coef = pl.pallas_call(
-        front_kernel,
-        in_specs=[smem, vmem, vmem, pl.BlockSpec(memory_space=pltpu.HBM)],
-        out_specs=[vmem, vmem],
-        out_shape=[
-            jax.ShapeDtypeStruct((panels, lax.axis_size("yl"), degrees, cycles), bf16),
-            jax.ShapeDtypeStruct((panels, orders, half), jnp.float32),
-        ],
+    picks = pl.pallas_call(
+        picks_kernel,
+        in_specs=[smem, pl.BlockSpec(memory_space=pltpu.HBM)],
+        out_specs=vmem,
+        out_shape=jax.ShapeDtypeStruct((panels, lax.axis_size("yl"), degrees, cycles), bf16),
         scratch_shapes=[
             pltpu.VMEM((panels, degrees, cycles), bf16),
-            pltpu.VMEM((4, panels, half), jnp.float32),
             pltpu.SemaphoreType.DMA((panels,)),
         ],
-        cost_estimate=pl.CostEstimate(flops=10_000_000, bytes_accessed=900_000, transcendentals=0),
+        cost_estimate=pl.CostEstimate(flops=1_000_000, bytes_accessed=400_000, transcendentals=0),
         compiler_params=pltpu.CompilerParams(vmem_limit_bytes=60 * 1024 * 1024),
-    )(panel_orders, cycle_span.T, cycle_weight.reshape(1, cycles), legendre)
+    )(panel_orders, legendre)
     picked = lax.all_to_all(picks.reshape(-1, degrees, cycles), ROW_PAIR, 0, 0, tiled=True)
 
     partial = pl.pallas_call(
         panel_kernel,
-        in_specs=[vmem] * 5,
+        in_specs=[smem] + [vmem] * 6,
         out_specs=pl.BlockSpec(memory_space=pltpu.HBM),
         out_shape=jax.ShapeDtypeStruct((panels, vecs, half), bf16),
         scratch_shapes=[
-            pltpu.VMEM((2, orders, degrees, half), bf16),
-            pltpu.VMEM((2, vecs, pairs), bf16),
+            pltpu.VMEM((panels, orders, half), jnp.float32),
+            pltpu.VMEM((4, panels, half), jnp.float32),
+            pltpu.VMEM((2 * pairs // 256, 256 // degrees, degrees, half), bf16),
+            pltpu.VMEM((2 * pairs // 256, vecs, 256), bf16),
             pltpu.VMEM((panels, vecs, half), bf16),
-            pltpu.SemaphoreType.DMA((panels,)),
+            pltpu.SemaphoreType.DMA,
         ],
         cost_estimate=pl.CostEstimate(
             flops=2 * panels * vecs * half * 2 * pairs, bytes_accessed=3_500_000, transcendentals=0
         ),
         compiler_params=params,
-    )(coef, legendre, other_tables, vectors, other_vectors)
+    )(
+        panel_orders,
+        cycle_span.T,
+        cycle_weight.reshape(1, cycles),
+        legendre,
+        other_tables,
+        vectors,
+        other_vectors,
+    )
 
     rows = jnp.sum(picked.reshape(picks.shape).astype(jnp.float32), axis=0).astype(bf16)
     count = lax.axis_size("z")

time: 82.5 us -> 83.2 us (level)
  blocking collectives: 39.9 us -> 16.3 us
  waiting for transfers between devices: 13.1 us -> 31.1 us
  starting transfers between devices: 17.5 us -> 23.8 us
  Pallas kernels: 8.66 us -> 7.08 us
  local copies, waits for them, and re-layouts: 2.09 us -> 3.61 us
    all_to_all x1 -> x0, blocking collectives: 23.3 us -> none  [stages(): pieces = lax.all_to_all(partial, ROW, 0, 0, tiled=True)]
    all_to_all x0 -> x1, waiting for transfers between devices: none -> 15.1 us  [stages(): pieces = lax.all_to_all(partial, ROW, 0, 0, tiled=True)]
    all_to_all x0 -> x1, starting transfers between devices: none -> 6.04 us  [stages(): pieces = lax.all_to_all(partial, ROW, 0, 0, tiled=True)]
    ppermute x3, waiting for transfers between devices: 0.44 us -> 3.12 us  [swapped(): return lax.ppermute(array, 'core', [(0, 1), (1, 0)])]
    pallas_call x2, Pallas kernels: 8.36 us -> 6.78 us  [the longest x1 4.4 us: stages(): pl.pallas_call(panel_kernel, in_specs=[smem] + [vmem] * 6, out_specs=pl.B...]
    unnamed x6 -> x10, local copies, waits for them, and re-layouts: 2.09 us -> 3.61 us
  transfers between devices with their start and end apart: 8 -> 9, of which waited for: 5 -> 6; matrix products, arithmetic and copies ran while one was open for 0% -> 0% of each run, Pallas kernels for 3% -> 3%
where the time goes in v3:
time: 83.2 us; the launch traced here: 82.7 us
  waiting for transfers between devices  31.1 us (37%)
  starting transfers between devices  23.8 us (29%)
  blocking collectives  16.3 us (20%)
  Pallas kernels  7.08 us (9%)
  local copies, waits for them, and re-layouts  3.61 us (4%)
    all_to_all x1, blocking collectives, stages(): shares = lax.all_to_all(applied, PLANE, 0, 0, tiled=True)  16.3 us
    all_to_all x1, waiting for transfers between devices, stages(): pieces = lax.all_to_all(partial, ROW, 0, 0, tiled=True)  15.1 us
    ppermute x3, starting transfers between devices, stages(): lax.ppermute(joined, 'z', [(i, (i + distance) % count) for i in range(cou...  10.5 us
    all_to_all x1, waiting for transfers between devices, stages(): lax.all_to_all(picks.reshape(-1, degrees, cycles), ROW_PAIR, 0, 0, tiled=...  7.17 us
    all_to_all x1, starting transfers between devices, stages(): pieces = lax.all_to_all(partial, ROW, 0, 0, tiled=True)  6.04 us
    all_to_all x1, starting transfers between devices, stages(): lax.all_to_all(picks.reshape(-1, degrees, cycles), ROW_PAIR, 0, 0, tiled=...  4.67 us
    pallas_call x1, Pallas kernels, stages(): pl.pallas_call(panel_kernel, in_specs=[smem] + [vmem] * 6, out_specs=pl.B...  4.4 us
    ppermute x3, waiting for transfers between devices, stages(): lax.ppermute(joined, 'z', [(i, (i + distance) % count) for i in range(cou...  3.62 us
  transfers between devices with their start and end apart: 9, of which 6 were waited for; matrix products, arithmetic and copies ran while one was open for 0% of the time, Pallas kernels for 3%

profile of v3, /device:TPU:8, one launch (start us, length us, event | category | flops | bytes accessed | tf_op | source)
XLA Modules:
  0.0 82.7 jit_solution(18356354960684271987)
XLA Ops:
  0.0 0.0 copy-start.4
  0.0 0.0 collective-permute-start.4
  0.0 0.5 collective-permute-start.5
  0.5 3.1 %collective-permute-done.5.other_v_ref = bf16[64,16,256]{2,1,0:T(8,128)(2,1)S(1)} collective-permute-done((bf16[64,16,256]{2,1,0:T(8,128)(2,1)}, bf16[64,16,256]{2,1,0:T(8,128)(2,1)S(1)}, u32[]{:S(2)}, u32[]{:S(2)}) %collective-permute-start.5) | collective-permute-done | bytes 524320 | tf_op jit(solution)/shard_map/ppermute | solution.py:162
  3.6 0.0 collective-permute-done.4.other_t_ref
  3.6 0.0 copy-start.1
  3.6 0.0 copy-done.4
  3.6 0.6 copy-done.1
  4.3 0.0 copy-start
  4.3 1.2 %copy-done = bf16[64,16,512]{2,1,0:T(8,128)(2,1)S(1)} copy-done((bf16[64,16,512]{2,1,0:T(8,128)(2,1)S(1)}, bf16[64,16,512]{2,1,0:T(8,128)(2,1)}, u32[]{:S(2)}) %copy-start) | copy-done | bytes 1048600
  5.5 1.0 %copy-done.2 = bf16[64,16,256]{2,1,0:T(8,128)(2,1)S(1)} copy-done((bf16[64,16,256]{2,1,0:T(8,128)(2,1)S(1)}, bf16[64,16,256]{2,1,0:T(8,128)(2,1)}, u32[]{:S(2)}) %copy-start.2) | copy-done | bytes 524312
  6.6 0.7 copy-done.3
  7.2 4.4 %shard_map.58 = bf16[8,256,256]{2,1,0:T(8,128)(2,1)} custom-call(s32[8]{0:T(128)S(1)} %copy-done.1, s32[2,512]{1,0:T(2,128)S(1)} %bitcast.7, f32[1,512]{1,0:T(1,128)S(1)} %bitcast.8, bf16[64,16,512]{2,1,0:T(8,128)(2,1)S(1)} %copy-done, bf16[64,16,512]{2,1,0:T(8,128)(2,1)S(1)} %collective-permute-done.4.other_t_ref, bf16[64,16,256]{2,1,0:T(8,128)(2,1)S(1)} %copy-done.2, ...), custom_call_target="tpu_custom_call" | custom-call | flops 2147483648 | bytes 3500000 | tf_op jit(solution)/shard_map/pallas_call | solution.py:192
  11.6 6.0 %all-to-all-start.1 = ((bf16[8,256,256]{2,1,0:T(8,128)(2,1)}), bf16[8,256,256]{2,1,0:T(8,128)(2,1)S(1)}, u32[]{:S(2)}, u32[]{:S(2)}) async-start(bf16[8,256,256]{2,1,0:T(8,128)(2,1)} %shard_map.58), calls=%async_computation.1 | async-start | bytes 2097152 | tf_op jit(solution)/shard_map/all_to_all | solution.py:242
  17.7 2.4 %shard_map.55 = bf16[8,2,16,512]{3,2,1,0:T(8,128)(2,1)} custom-call(s32[8]{0:T(128)} %orders_ref.3, bf16[64,16,512]{2,1,0:T(8,128)(2,1)} %own_t_ref.1), custom_call_target="tpu_custom_call" | custom-call | flops 1000000 | bytes 400000 | tf_op jit(solution)/shard_map/pallas_call | solution.py:178
  20.1 15.1 %all-to-all-done.1 = bf16[8,256,256]{2,1,0:T(8,128)(2,1)S(1)} async-done(((bf16[8,256,256]{2,1,0:T(8,128)(2,1)}), bf16[8,256,256]{2,1,0:T(8,128)(2,1)S(1)}, u32[]{:S(2)}, u32[]{:S(2)}) %all-to-all-start.1) | async-done | bytes 1048608 | tf_op jit(solution)/shard_map/all_to_all | solution.py:242
  35.2 4.7 %all-to-all-start = ((bf16[16,16,512]{2,1,0:T(8,128)(2,1)}), bf16[16,16,512]{2,1,0:T(8,128)(2,1)S(1)}, u32[]{:S(2)}, u32[]{:S(2)}) async-start(bf16[16,16,512]{2,1,0:T(8,128)(2,1)} %bitcast.9), calls=%async_computation | async-start | bytes 524288 | tf_op jit(solution)/shard_map/all_to_all | solution.py:190
  39.9 0.1 reduce_sum.37.own_ref
  40.0 0.1 collective-permute-start.6
  40.1 7.2 %all-to-all-done = bf16[16,16,512]{2,1,0:T(8,128)(2,1)S(1)} async-done(((bf16[16,16,512]{2,1,0:T(8,128)(2,1)}), bf16[16,16,512]{2,1,0:T(8,128)(2,1)S(1)}, u32[]{:S(2)}, u32[]{:S(2)}) %all-to-all-start) | async-done | bytes 262176 | tf_op jit(solution)/shard_map/all_to_all | solution.py:190
  47.3 2.0 %collective-permute-start = (bf16[2,16,512]{2,1,0:T(8,128)(2,1)S(1)}, bf16[2,16,512]{2,1,0:T(8,128)(2,1)S(1)}, u32[]{:S(2)}, u32[]{:S(2)}) collective-permute-start(bf16[2,16,512]{2,1,0:T(8,128)(2,1)S(1)} %reduce_sum.36.own_ref), channel_id=1, source_target_pairs={{0,4},{4,0},{8,12},{12,8},{16,20},{20,16},{24,28},{28,24},{1,5},{5... | collective-permute-start | bytes 98312 | tf_op jit(solution)/shard_map/ppermute | solution.py:221
  49.3 2.0 %collective-permute-done.other_ref = bf16[2,16,512]{2,1,0:T(8,128)(2,1)S(1)} collective-permute-done((bf16[2,16,512]{2,1,0:T(8,128)(2,1)S(1)}, bf16[2,16,512]{2,1,0:T(8,128)(2,1)S(1)}, u32[]{:S(2)}, u32[]{:S(2)}) %collective-permute-start) | collective-permute-done | bytes 32800 | tf_op jit(solution)/shard_map/ppermute | solution.py:221
  51.4 7.6 %collective-permute-start.3 = (bf16[2,2,16,512]{3,2,1,0:T(8,128)(2,1)S(1)}, bf16[2,2,16,512]{3,2,1,0:T(8,128)(2,1)S(1)}, u32[]{:S(2)}, u32[]{:S(2)}) collective-permute-start(bf16[2,2,16,512]{3,2,1,0:T(8,128)(2,1)S(1)} %shard_map.56.refs_0_), channel_id=1, source_target_pairs={{0,16},{4,20},{8,24},{12,28},{16,0},{20,4},{24,8},{28,12},{1,17},{... | collective-permute-start | bytes 196616 | tf_op jit(solution)/shard_map/ppermute | solution.py:232
  59.0 0.0 collective-permute-start.2
  59.0 2.9 %collective-permute-start.1 = (bf16[2,2,16,512]{3,2,1,0:T(8,128)(2,1)S(1)}, bf16[2,2,16,512]{3,2,1,0:T(8,128)(2,1)S(1)}, u32[]{:S(2)}, u32[]{:S(2)}) collective-permute-start(bf16[2,2,16,512]{3,2,1,0:T(8,128)(2,1)S(1)} %shard_map.56.refs_0_), channel_id=1, source_target_pairs={{0,8},{4,12},{8,16},{12,20},{16,24},{20,28},{24,0},{28,4},{1,9},{5... | collective-permute-start | bytes 196616 | tf_op jit(solution)/shard_map/ppermute | solution.py:232
  61.9 0.0 collective-permute-done.3.refs_3_
  61.9 3.0 %collective-permute-done.2.refs_2_ = bf16[2,2,16,512]{3,2,1,0:T(8,128)(2,1)S(1)} collective-permute-done((bf16[2,2,16,512]{3,2,1,0:T(8,128)(2,1)S(1)}, bf16[2,2,16,512]{3,2,1,0:T(8,128)(2,1)S(1)}, u32[]{:S(2)}, u32[]{:S(2)}) %collective-permute-start.2) | collective-permute-done | bytes 65568 | tf_op jit(solution)/shard_map/ppermute | solution.py:232
  64.9 0.6 collective-permute-done.1.refs_1_
  65.5 0.0 collective-permute-done.6.other_ref
  65.5 0.3 shard_map.59
  65.8 16.3 %all_to_all.15 = bf16[16,16,256]{2,1,0:T(8,128)(2,1)S(1)} all-to-all(bf16[16,16,256]{2,1,0:T(8,128)(2,1)S(1)} %shard_map.59), channel_id=1, replica_groups=mesh['yh'=2,'x'=4,'z'=8,'yl'=2,'core'=2] {'z','yl'}, dimensions={0} | all-to-all | bytes 262144 | tf_op jit(solution)/shard_map/all_to_all | solution.py:253
  82.1 0.6 reduce_sum.38
  (5 shorter events, 0.1 us)
Async XLA Ops:
  0.0 3.6 %copy-start.4 = (f32[512]{0:T(512)S(1)}, f32[512]{0:T(512)}, u32[]{:S(2)}) copy-start(f32[512]{0:T(512)} %param.9) | copy-start | bytes 6148
  0.0 3.6 %collective-permute-start.4 = (bf16[64,16,512]{2,1,0:T(8,128)(2,1)}, bf16[64,16,512]{2,1,0:T(8,128)(2,1)S(1)}, u32[]{:S(2)}, u32[]{:S(2)}) collective-permute-start(bf16[64,16,512]{2,1,0:T(8,128)(2,1)} %own_t_ref.1), channel_id=1, source_target_pairs={{0,1},{1,0},{2,3},{3,2},{4,5},{5,4},{6,7},{7,6},{8,9},{9,8},{10,11... | collective-permute-start | bytes 3145736 | tf_op jit(solution)/shard_map/ppermute | solution.py:162
  0.0 3.6 %collective-permute-start.5 = (bf16[64,16,256]{2,1,0:T(8,128)(2,1)}, bf16[64,16,256]{2,1,0:T(8,128)(2,1)S(1)}, u32[]{:S(2)}, u32[]{:S(2)}) collective-permute-start(bf16[64,16,256]{2,1,0:T(8,128)(2,1)} %own_v_ref.1), channel_id=1, source_target_pairs={{0,1},{1,0},{2,3},{3,2},{4,5},{5,4},{6,7},{7,6},{8,9},{9,8},{10,11... | collective-permute-start | bytes 1572872 | tf_op jit(solution)/shard_map/ppermute | solution.py:162
  3.6 0.7 copy-start.1
  4.3 1.2 %copy-start = (bf16[64,16,512]{2,1,0:T(8,128)(2,1)S(1)}, bf16[64,16,512]{2,1,0:T(8,128)(2,1)}, u32[]{:S(2)}) copy-start(bf16[64,16,512]{2,1,0:T(8,128)(2,1)} %own_t_ref.1) | copy-start | bytes 3145732
  5.5 1.0 %copy-start.2 = (bf16[64,16,256]{2,1,0:T(8,128)(2,1)S(1)}, bf16[64,16,256]{2,1,0:T(8,128)(2,1)}, u32[]{:S(2)}) copy-start(bf16[64,16,256]{2,1,0:T(8,128)(2,1)} %own_v_ref.1) | copy-start | bytes 1572868
  6.6 0.7 copy-start.3
  11.6 23.6 %all-to-all-start.1 = ((bf16[8,256,256]{2,1,0:T(8,128)(2,1)}), bf16[8,256,256]{2,1,0:T(8,128)(2,1)S(1)}, u32[]{:S(2)}, u32[]{:S(2)}) async-start(bf16[8,256,256]{2,1,0:T(8,128)(2,1)} %shard_map.58), calls=%async_computation.1 | async-start | bytes 2097152 | tf_op jit(solution)/shard_map/all_to_all | solution.py:242
  35.2 12.1 %all-to-all-start = ((bf16[16,16,512]{2,1,0:T(8,128)(2,1)}), bf16[16,16,512]{2,1,0:T(8,128)(2,1)S(1)}, u32[]{:S(2)}, u32[]{:S(2)}) async-start(bf16[16,16,512]{2,1,0:T(8,128)(2,1)} %bitcast.9), calls=%async_computation | async-start | bytes 524288 | tf_op jit(solution)/shard_map/all_to_all | solution.py:190
  40.0 25.5 %collective-permute-start.6 = (bf16[256,256]{1,0:T(8,128)(2,1)S(1)}, bf16[256,256]{1,0:T(8,128)(2,1)S(1)}, u32[]{:S(2)}, u32[]{:S(2)}) collective-permute-start(bf16[256,256]{1,0:T(8,128)(2,1)S(1)} %reduce_sum.37.own_ref), channel_id=1, source_target_pairs={{0,1},{1,0},{2,3},{3,2},{4,5},{5,4},{6,7},{7,6},{8,9},{9,8},{10,11... | collective-permute-start | bytes 393224 | tf_op jit(solution)/shard_map/ppermute | solution.py:162
  47.3 4.0 %collective-permute-start = (bf16[2,16,512]{2,1,0:T(8,128)(2,1)S(1)}, bf16[2,16,512]{2,1,0:T(8,128)(2,1)S(1)}, u32[]{:S(2)}, u32[]{:S(2)}) collective-permute-start(bf16[2,16,512]{2,1,0:T(8,128)(2,1)S(1)} %reduce_sum.36.own_ref), channel_id=1, source_target_pairs={{0,4},{4,0},{8,12},{12,8},{16,20},{20,16},{24,28},{28,24},{1,5},{5... | collective-permute-start | bytes 98312 | tf_op jit(solution)/shard_map/ppermute | solution.py:221
  51.4 10.5 %collective-permute-start.3 = (bf16[2,2,16,512]{3,2,1,0:T(8,128)(2,1)S(1)}, bf16[2,2,16,512]{3,2,1,0:T(8,128)(2,1)S(1)}, u32[]{:S(2)}, u32[]{:S(2)}) collective-permute-start(bf16[2,2,16,512]{3,2,1,0:T(8,128)(2,1)S(1)} %shard_map.56.refs_0_), channel_id=1, source_target_pairs={{0,16},{4,20},{8,24},{12,28},{16,0},{20,4},{24,8},{28,12},{1,17},{... | collective-permute-start | bytes 196616 | tf_op jit(solution)/shard_map/ppermute | solution.py:232
  59.0 5.9 %collective-permute-start.2 = (bf16[2,2,16,512]{3,2,1,0:T(8,128)(2,1)S(1)}, bf16[2,2,16,512]{3,2,1,0:T(8,128)(2,1)S(1)}, u32[]{:S(2)}, u32[]{:S(2)}) collective-permute-start(bf16[2,2,16,512]{3,2,1,0:T(8,128)(2,1)S(1)} %shard_map.56.refs_0_), channel_id=1, source_target_pairs={{0,24},{4,28},{8,0},{12,4},{16,8},{20,12},{24,16},{28,20},{1,25},{... | collective-permute-start | bytes 196616 | tf_op jit(solution)/shard_map/ppermute | solution.py:232
  59.0 6.5 %collective-permute-start.1 = (bf16[2,2,16,512]{3,2,1,0:T(8,128)(2,1)S(1)}, bf16[2,2,16,512]{3,2,1,0:T(8,128)(2,1)S(1)}, u32[]{:S(2)}, u32[]{:S(2)}) collective-permute-start(bf16[2,2,16,512]{3,2,1,0:T(8,128)(2,1)S(1)} %shard_map.56.refs_0_), channel_id=1, source_target_pairs={{0,8},{4,12},{8,16},{12,20},{16,24},{20,28},{24,0},{28,4},{1,9},{5... | collective-permute-start | bytes 196616 | tf_op jit(solution)/shard_map/ppermute | solution.py:232

commit v4 on v3

--- a/solution.py
+++ b/solution.py
@@ -38,29 +38,65 @@
     return jnp.where(zero, 0.0, jnp.float32(CELL) / jnp.where(zero, 1.0, sine))
 
 
-def picks_kernel(orders_ref, leg_ref, picks_ref, rows, sems):
-    panels, sharers, degrees, cycles = picks_ref.shape
+def picks_kernel(orders_ref, leg_ref, picks_ref, sems):
+    panels, sharers = picks_ref.shape[:2]
     orders = leg_ref.shape[0]
+    first_order = lax.axis_index(ROW) * orders
+
+    def copies(p):
+        place = jnp.clip(orders_ref[p] - first_order, 0, orders - 1)
+        return [
+            pltpu.make_async_copy(leg_ref.at[place], picks_ref.at[p, sharer], sems.at[p, sharer])
+            for sharer in range(sharers)
+        ]
+
+    def held(p):
+        return (orders_ref[p] >= first_order) & (orders_ref[p] < first_order + orders)
+
+    for p in range(panels):
+
+        @pl.when(held(p))
+        def _():
+            for copy in copies(p):
+                copy.start()
+
+        @pl.when(jnp.logical_not(held(p)))
+        def _():
+            picks_ref[p] = jnp.zeros_like(picks_ref[p])
+
+    for p in range(panels):
+
+        @pl.when(held(p))
+        def _():
+            for copy in copies(p):
+                copy.wait()
+
+
+def rows_kernel(orders_ref, picked_ref, rows_ref):
+    sharers, degrees, cycles = rows_ref.shape
     half = cycles // 2
-    first_order = lax.axis_index(ROW) * orders
     core = lax.axis_index("core")
+    panel = orders_ref[lax.axis_index(ROW)]
     own = pl.ds(pl.multiple_of(core * half, half), half)
     other = pl.ds(pl.multiple_of((1 - core) * half, half), half)
-    copies = []
-    for p in range(panels):
-        place = jnp.clip(orders_ref[p] - first_order, 0, orders - 1)
-        copies.append(pltpu.make_async_copy(leg_ref.at[place], rows.at[p], sems.at[p]))
-        copies[p].start()
-    degree = lax.broadcasted_iota(jnp.int32, (degrees, half), 0) + lax.axis_index(COL) * degrees
-    for p in range(panels):
-        panel = orders_ref[p]
-        held = (panel >= first_order) & (panel < first_order + orders)
-        kept = degree >= jnp.where(held, panel, orders * lax.axis_size(ROW))
-        copies[p].wait()
+    for sharer in range(sharers):
+        place = (lax.axis_index("z") * sharers + sharer) * lax.axis_size("core") + core
+        degree = lax.broadcasted_iota(jnp.int32, (degrees, half), 0) + place * degrees
         for lanes, part in ((own, slice(0, half)), (other, slice(half, cycles))):
-            pick = jnp.where(kept, rows[p, :, lanes].astype(jnp.float32), 0.0).astype(jnp.bfloat16)
-            for sharer in range(sharers):
-                picks_ref[p, sharer, :, part] = pick
+            total = picked_ref[sharer, :, lanes].astype(jnp.float32)
+            for source in range(sharers + sharer, picked_ref.shape[0], sharers):
+                total += picked_ref[source, :, lanes].astype(jnp.float32)
+            rows_ref[sharer, :, part] = jnp.where(degree >= panel, total, 0.0).astype(jnp.bfloat16)
+
+
+def sum_kernel(pieces_ref, out_ref):
+    count, rows, _ = pieces_ref.shape
+    for first in range(0, rows, 16):
+        at = slice(first, first + 16)
+        terms = [pieces_ref[i, at].astype(jnp.float32) for i in range(count)]
+        while len(terms) > 1:
+            terms = [sum(terms[i : i + 2]) for i in range(0, len(terms), 2)]
+        out_ref[at] = terms[0].astype(jnp.bfloat16)
 
 
 def fill_coefs(orders_ref, span_ref, weight_ref, coefs, sides):
@@ -162,6 +198,17 @@
     return lax.ppermute(array, "core", [(0, 1), (1, 0)])
 
 
+def summed(pieces, params):
+    return pl.pallas_call(
+        sum_kernel,
+        in_specs=[pl.BlockSpec(memory_space=pltpu.VMEM)],
+        out_specs=pl.BlockSpec(memory_space=pltpu.VMEM),
+        out_shape=jax.ShapeDtypeStruct(pieces.shape[1:], pieces.dtype),
+        cost_estimate=pl.CostEstimate(flops=pieces.size, bytes_accessed=3 * pieces.size, transcendentals=0),
+        compiler_params=params,
+    )(pieces)
+
+
 def stages(legendre, vectors, panel_orders, cycle_span, cycle_weight):
     orders, degrees, cycles = legendre.shape
     vecs = vectors.shape[2]
@@ -180,10 +227,7 @@
         in_specs=[smem, pl.BlockSpec(memory_space=pltpu.HBM)],
         out_specs=vmem,
         out_shape=jax.ShapeDtypeStruct((panels, lax.axis_size("yl"), degrees, cycles), bf16),
-        scratch_shapes=[
-            pltpu.VMEM((panels, degrees, cycles), bf16),
-            pltpu.SemaphoreType.DMA((panels,)),
-        ],
+        scratch_shapes=[pltpu.SemaphoreType.DMA((panels, lax.axis_size("yl")))],
         cost_estimate=pl.CostEstimate(flops=1_000_000, bytes_accessed=400_000, transcendentals=0),
         compiler_params=pltpu.CompilerParams(vmem_limit_bytes=60 * 1024 * 1024),
     )(panel_orders, legendre)
@@ -216,7 +260,14 @@
         other_vectors,
     )
 
-    rows = jnp.sum(picked.reshape(picks.shape).astype(jnp.float32), axis=0).astype(bf16)
+    rows = pl.pallas_call(
+        rows_kernel,
+        in_specs=[smem, vmem],
+        out_specs=vmem,
+        out_shape=jax.ShapeDtypeStruct(picks.shape[1:], bf16),
+        cost_estimate=pl.CostEstimate(flops=500_000, bytes_accessed=300_000, transcendentals=0),
+        compiler_params=params,
+    )(panel_orders, picked)
     count = lax.axis_size("z")
     paired = lax.ppermute(rows, "z", [(i, i ^ 1) for i in range(count)])
     joined = pl.pallas_call(
@@ -240,7 +291,7 @@
     )(*spread).reshape(-1, cycles)
 
     pieces = lax.all_to_all(partial, ROW, 0, 0, tiled=True)
-    own = jnp.sum(pieces.astype(jnp.float32), axis=0).astype(bf16)
+    own = summed(pieces, params)
     other = swapped(own)
     applied = pl.pallas_call(
         apply_kernel,
@@ -251,7 +302,7 @@
         compiler_params=params,
     )(panel_rows, own, other)
     shares = lax.all_to_all(applied, PLANE, 0, 0, tiled=True)
-    result = jnp.sum(shares.astype(jnp.float32), axis=0).astype(bf16)
+    result = summed(shares, params)
     return result[:, None, :]
 
 

time: 83.2 us -> 83.8 us (level)
  Pallas kernels: 7.08 us -> 8.4 us
    pallas_call x0 -> x3, Pallas kernels: none -> 1.35 us  [the longest x2 0.75 us: summed(): pl.pallas_call(sum_kernel, in_specs=[pl.BlockSpec(memory_space=pltpu.VMEM...]
    unnamed x10 -> x12, local copies, waits for them, and re-layouts: 3.61 us -> 3.61 us
  transfers between devices with their start and end apart: 9 -> 9, of which waited for: 6 -> 6; matrix products, arithmetic and copies ran while one was open for 0% -> 0% of each run, Pallas kernels for 3% -> 4%
where the time goes in v4:
time: 83.8 us; the launch traced here: 83.3 us
  waiting for transfers between devices  31.1 us (37%)
  starting transfers between devices  23.8 us (28%)
  blocking collectives  16.3 us (19%)
  Pallas kernels  8.4 us (10%)
  local copies, waits for them, and re-layouts  3.61 us (4%)
    all_to_all x1, blocking collectives, stages(): shares = lax.all_to_all(applied, PLANE, 0, 0, tiled=True)  16.3 us
    all_to_all x1, waiting for transfers between devices, stages(): pieces = lax.all_to_all(partial, ROW, 0, 0, tiled=True)  15.2 us
    ppermute x3, starting transfers between devices, stages(): lax.ppermute(joined, 'z', [(i, (i + distance) % count) for i in range(cou...  10.5 us
    all_to_all x1, waiting for transfers between devices, stages(): lax.all_to_all(picks.reshape(-1, degrees, cycles), ROW_PAIR, 0, 0, tiled=...  7.17 us
    all_to_all x1, starting transfers between devices, stages(): pieces = lax.all_to_all(partial, ROW, 0, 0, tiled=True)  6.04 us
    all_to_all x1, starting transfers between devices, stages(): lax.all_to_all(picks.reshape(-1, degrees, cycles), ROW_PAIR, 0, 0, tiled=...  4.67 us
    pallas_call x1, Pallas kernels, stages(): pl.pallas_call(panel_kernel, in_specs=[smem] + [vmem] * 6, out_specs=pl.B...  4.41 us
    ppermute x3, waiting for transfers between devices, stages(): lax.ppermute(joined, 'z', [(i, (i + distance) % count) for i in range(cou...  3.62 us
  transfers between devices with their start and end apart: 9, of which 6 were waited for; matrix products, arithmetic and copies ran while one was open for 0% of the time, Pallas kernels for 4%

profile of v4, /device:TPU:8, one launch (start us, length us, event | category | flops | bytes accessed | tf_op | source)
XLA Modules:
  0.0 83.3 jit_solution(5261719878277147911)
XLA Ops:
  0.0 0.0 copy-start.5
  0.0 0.0 collective-permute-start.4
  0.0 0.5 collective-permute-start.5
  0.5 3.1 %collective-permute-done.5.other_v_ref = bf16[64,16,256]{2,1,0:T(8,128)(2,1)S(1)} collective-permute-done((bf16[64,16,256]{2,1,0:T(8,128)(2,1)}, bf16[64,16,256]{2,1,0:T(8,128)(2,1)S(1)}, u32[]{:S(2)}, u32[]{:S(2)}) %collective-permute-start.5) | collective-permute-done | bytes 524320 | tf_op jit(solution)/shard_map/ppermute | solution.py:198
  3.6 0.0 collective-permute-done.4.other_t_ref
  3.6 0.0 copy-done.5
  3.6 0.6 copy-done.1
  4.3 1.2 %copy-done = bf16[64,16,512]{2,1,0:T(8,128)(2,1)S(1)} copy-done((bf16[64,16,512]{2,1,0:T(8,128)(2,1)S(1)}, bf16[64,16,512]{2,1,0:T(8,128)(2,1)}, u32[]{:S(2)}) %copy-start) | copy-done | bytes 1048600
  5.5 1.0 %copy-done.3 = bf16[64,16,256]{2,1,0:T(8,128)(2,1)S(1)} copy-done((bf16[64,16,256]{2,1,0:T(8,128)(2,1)S(1)}, bf16[64,16,256]{2,1,0:T(8,128)(2,1)}, u32[]{:S(2)}) %copy-start.3) | copy-done | bytes 524312
  6.6 0.7 copy-done.4
  7.2 4.4 %shard_map.59 = bf16[8,256,256]{2,1,0:T(8,128)(2,1)} custom-call(s32[8]{0:T(128)S(1)} %copy-done.1, s32[2,512]{1,0:T(2,128)S(1)} %bitcast.6, f32[1,512]{1,0:T(1,128)S(1)} %bitcast.7, bf16[64,16,512]{2,1,0:T(8,128)(2,1)S(1)} %copy-done, bf16[64,16,512]{2,1,0:T(8,128)(2,1)S(1)} %collective-permute-done.4.other_t_ref, bf16[64,16,256]{2,1,0:T(8,128)(2,1)S(1)} %copy-done.3, ...), custom_call_target="tpu_custom_call" | custom-call | flops 2147483648 | bytes 3500000 | tf_op jit(solution)/shard_map/pallas_call | solution.py:236
  11.7 6.0 %all-to-all-start.1 = ((bf16[8,256,256]{2,1,0:T(8,128)(2,1)}), bf16[8,256,256]{2,1,0:T(8,128)(2,1)S(1)}, u32[]{:S(2)}, u32[]{:S(2)}) async-start(bf16[8,256,256]{2,1,0:T(8,128)(2,1)} %shard_map.59), calls=%async_computation.1 | async-start | bytes 2097152 | tf_op jit(solution)/shard_map/all_to_all | solution.py:293
  17.7 2.4 %shard_map.55 = bf16[8,2,16,512]{3,2,1,0:T(8,128)(2,1)} custom-call(s32[8]{0:T(128)} %orders_ref.5, bf16[64,16,512]{2,1,0:T(8,128)(2,1)} %own_t_ref.1), custom_call_target="tpu_custom_call" | custom-call | flops 1000000 | bytes 400000 | tf_op jit(solution)/shard_map/pallas_call | solution.py:225
  20.1 15.2 %all-to-all-done.1.pieces_ref = bf16[8,256,256]{2,1,0:T(8,128)(2,1)S(1)} async-done(((bf16[8,256,256]{2,1,0:T(8,128)(2,1)}), bf16[8,256,256]{2,1,0:T(8,128)(2,1)S(1)}, u32[]{:S(2)}, u32[]{:S(2)}) %all-to-all-start.1) | async-done | bytes 1048608 | tf_op jit(solution)/shard_map/all_to_all | solution.py:293
  35.2 4.7 %all-to-all-start = ((bf16[16,16,512]{2,1,0:T(8,128)(2,1)}), bf16[16,16,512]{2,1,0:T(8,128)(2,1)S(1)}, u32[]{:S(2)}, u32[]{:S(2)}) async-start(bf16[16,16,512]{2,1,0:T(8,128)(2,1)} %bitcast.8), calls=%async_computation | async-start | bytes 524288 | tf_op jit(solution)/shard_map/all_to_all | solution.py:234
  39.9 0.1 shard_map.60.own_ref
  40.0 0.1 collective-permute-start.6
  40.1 7.2 %all-to-all-done.picked_ref = bf16[16,16,512]{2,1,0:T(8,128)(2,1)S(1)} async-done(((bf16[16,16,512]{2,1,0:T(8,128)(2,1)}), bf16[16,16,512]{2,1,0:T(8,128)(2,1)S(1)}, u32[]{:S(2)}, u32[]{:S(2)}) %all-to-all-start) | async-done | bytes 262176 | tf_op jit(solution)/shard_map/all_to_all | solution.py:234
  47.3 0.0 copy-done.2
  47.3 0.6 shard_map.56.own_ref
  47.9 2.0 %collective-permute-start = (bf16[2,16,512]{2,1,0:T(8,128)(2,1)S(1)}, bf16[2,16,512]{2,1,0:T(8,128)(2,1)S(1)}, u32[]{:S(2)}, u32[]{:S(2)}) collective-permute-start(bf16[2,16,512]{2,1,0:T(8,128)(2,1)S(1)} %shard_map.56.own_ref), channel_id=1, source_target_pairs={{0,4},{4,0},{8,12},{12,8},{16,20},{20,16},{24,28},{28,24},{1,5},{5... | collective-permute-start | bytes 98312 | tf_op jit(solution)/shard_map/ppermute | solution.py:272
  49.9 2.0 %collective-permute-done.other_ref = bf16[2,16,512]{2,1,0:T(8,128)(2,1)S(1)} collective-permute-done((bf16[2,16,512]{2,1,0:T(8,128)(2,1)S(1)}, bf16[2,16,512]{2,1,0:T(8,128)(2,1)S(1)}, u32[]{:S(2)}, u32[]{:S(2)}) %collective-permute-start) | collective-permute-done | bytes 32800 | tf_op jit(solution)/shard_map/ppermute | solution.py:272
  51.9 7.6 %collective-permute-start.3 = (bf16[2,2,16,512]{3,2,1,0:T(8,128)(2,1)S(1)}, bf16[2,2,16,512]{3,2,1,0:T(8,128)(2,1)S(1)}, u32[]{:S(2)}, u32[]{:S(2)}) collective-permute-start(bf16[2,2,16,512]{3,2,1,0:T(8,128)(2,1)S(1)} %shard_map.57.refs_0_), channel_id=1, source_target_pairs={{0,16},{4,20},{8,24},{12,28},{16,0},{20,4},{24,8},{28,12},{1,17},{... | collective-permute-start | bytes 196616 | tf_op jit(solution)/shard_map/ppermute | solution.py:283
  59.5 0.0 collective-permute-start.2
  59.5 2.9 %collective-permute-start.1 = (bf16[2,2,16,512]{3,2,1,0:T(8,128)(2,1)S(1)}, bf16[2,2,16,512]{3,2,1,0:T(8,128)(2,1)S(1)}, u32[]{:S(2)}, u32[]{:S(2)}) collective-permute-start(bf16[2,2,16,512]{3,2,1,0:T(8,128)(2,1)S(1)} %shard_map.57.refs_0_), channel_id=1, source_target_pairs={{0,8},{4,12},{8,16},{12,20},{16,24},{20,28},{24,0},{28,4},{1,9},{5... | collective-permute-start | bytes 196616 | tf_op jit(solution)/shard_map/ppermute | solution.py:283
  62.5 0.0 collective-permute-done.3.refs_3_
  62.5 3.0 %collective-permute-done.2.refs_2_ = bf16[2,2,16,512]{3,2,1,0:T(8,128)(2,1)S(1)} collective-permute-done((bf16[2,2,16,512]{3,2,1,0:T(8,128)(2,1)S(1)}, bf16[2,2,16,512]{3,2,1,0:T(8,128)(2,1)S(1)}, u32[]{:S(2)}, u32[]{:S(2)}) %collective-permute-start.2) | collective-permute-done | bytes 65568 | tf_op jit(solution)/shard_map/ppermute | solution.py:283
  65.4 0.6 collective-permute-done.1.refs_1_
  66.1 0.0 collective-permute-done.6.other_ref
  66.1 0.3 shard_map.61
  66.4 16.3 %all_to_all.15.pieces_ref = bf16[16,16,256]{2,1,0:T(8,128)(2,1)S(1)} all-to-all(bf16[16,16,256]{2,1,0:T(8,128)(2,1)S(1)} %shard_map.61), channel_id=1, replica_groups=mesh['yh'=2,'x'=4,'z'=8,'yl'=2,'core'=2] {'z','yl'}, dimensions={0} | all-to-all | bytes 262144 | tf_op jit(solution)/shard_map/all_to_all | solution.py:304
  82.7 0.6 shard_map.62
  (7 shorter events, 0.0 us)
Async XLA Ops:
  0.0 3.6 %copy-start.5 = (f32[512]{0:T(512)S(1)}, f32[512]{0:T(512)}, u32[]{:S(2)}) copy-start(f32[512]{0:T(512)} %param.9) | copy-start | bytes 6148
  0.0 3.6 %collective-permute-start.4 = (bf16[64,16,512]{2,1,0:T(8,128)(2,1)}, bf16[64,16,512]{2,1,0:T(8,128)(2,1)S(1)}, u32[]{:S(2)}, u32[]{:S(2)}) collective-permute-start(bf16[64,16,512]{2,1,0:T(8,128)(2,1)} %own_t_ref.1), channel_id=1, source_target_pairs={{0,1},{1,0},{2,3},{3,2},{4,5},{5,4},{6,7},{7,6},{8,9},{9,8},{10,11... | collective-permute-start | bytes 3145736 | tf_op jit(solution)/shard_map/ppermute | solution.py:198
  0.0 3.6 %collective-permute-start.5 = (bf16[64,16,256]{2,1,0:T(8,128)(2,1)}, bf16[64,16,256]{2,1,0:T(8,128)(2,1)S(1)}, u32[]{:S(2)}, u32[]{:S(2)}) collective-permute-start(bf16[64,16,256]{2,1,0:T(8,128)(2,1)} %own_v_ref.1), channel_id=1, source_target_pairs={{0,1},{1,0},{2,3},{3,2},{4,5},{5,4},{6,7},{7,6},{8,9},{9,8},{10,11... | collective-permute-start | bytes 1572872 | tf_op jit(solution)/shard_map/ppermute | solution.py:198
  3.6 0.7 copy-start.1
  4.3 1.2 %copy-start = (bf16[64,16,512]{2,1,0:T(8,128)(2,1)S(1)}, bf16[64,16,512]{2,1,0:T(8,128)(2,1)}, u32[]{:S(2)}) copy-start(bf16[64,16,512]{2,1,0:T(8,128)(2,1)} %own_t_ref.1) | copy-start | bytes 3145732
  5.5 1.0 %copy-start.3 = (bf16[64,16,256]{2,1,0:T(8,128)(2,1)S(1)}, bf16[64,16,256]{2,1,0:T(8,128)(2,1)}, u32[]{:S(2)}) copy-start(bf16[64,16,256]{2,1,0:T(8,128)(2,1)} %own_v_ref.1) | copy-start | bytes 1572868
  6.6 0.7 copy-start.4
  11.7 23.6 %all-to-all-start.1 = ((bf16[8,256,256]{2,1,0:T(8,128)(2,1)}), bf16[8,256,256]{2,1,0:T(8,128)(2,1)S(1)}, u32[]{:S(2)}, u32[]{:S(2)}) async-start(bf16[8,256,256]{2,1,0:T(8,128)(2,1)} %shard_map.59), calls=%async_computation.1 | async-start | bytes 2097152 | tf_op jit(solution)/shard_map/all_to_all | solution.py:293
  35.2 12.1 %all-to-all-start = ((bf16[16,16,512]{2,1,0:T(8,128)(2,1)}), bf16[16,16,512]{2,1,0:T(8,128)(2,1)S(1)}, u32[]{:S(2)}, u32[]{:S(2)}) async-start(bf16[16,16,512]{2,1,0:T(8,128)(2,1)} %bitcast.8), calls=%async_computation | async-start | bytes 524288 | tf_op jit(solution)/shard_map/all_to_all | solution.py:234
  39.9 7.4 %copy-start.2 = (s32[8]{0:T(128)S(1)}, s32[8]{0:T(128)}, u32[]{:S(2)}) copy-start(s32[8]{0:T(128)} %orders_ref.5) | copy-start | bytes 100
  40.0 26.1 %collective-permute-start.6 = (bf16[256,256]{1,0:T(8,128)(2,1)S(1)}, bf16[256,256]{1,0:T(8,128)(2,1)S(1)}, u32[]{:S(2)}, u32[]{:S(2)}) collective-permute-start(bf16[256,256]{1,0:T(8,128)(2,1)S(1)} %shard_map.60.own_ref), channel_id=1, source_target_pairs={{0,1},{1,0},{2,3},{3,2},{4,5},{5,4},{6,7},{7,6},{8,9},{9,8},{10,11... | collective-permute-start | bytes 393224 | tf_op jit(solution)/shard_map/ppermute | solution.py:198
  47.9 4.0 %collective-permute-start = (bf16[2,16,512]{2,1,0:T(8,128)(2,1)S(1)}, bf16[2,16,512]{2,1,0:T(8,128)(2,1)S(1)}, u32[]{:S(2)}, u32[]{:S(2)}) collective-permute-start(bf16[2,16,512]{2,1,0:T(8,128)(2,1)S(1)} %shard_map.56.own_ref), channel_id=1, source_target_pairs={{0,4},{4,0},{8,12},{12,8},{16,20},{20,16},{24,28},{28,24},{1,5},{5... | collective-permute-start | bytes 98312 | tf_op jit(solution)/shard_map/ppermute | solution.py:272
  51.9 10.5 %collective-permute-start.3 = (bf16[2,2,16,512]{3,2,1,0:T(8,128)(2,1)S(1)}, bf16[2,2,16,512]{3,2,1,0:T(8,128)(2,1)S(1)}, u32[]{:S(2)}, u32[]{:S(2)}) collective-permute-start(bf16[2,2,16,512]{3,2,1,0:T(8,128)(2,1)S(1)} %shard_map.57.refs_0_), channel_id=1, source_target_pairs={{0,16},{4,20},{8,24},{12,28},{16,0},{20,4},{24,8},{28,12},{1,17},{... | collective-permute-start | bytes 196616 | tf_op jit(solution)/shard_map/ppermute | solution.py:283
  59.5 5.9 %collective-permute-start.2 = (bf16[2,2,16,512]{3,2,1,0:T(8,128)(2,1)S(1)}, bf16[2,2,16,512]{3,2,1,0:T(8,128)(2,1)S(1)}, u32[]{:S(2)}, u32[]{:S(2)}) collective-permute-start(bf16[2,2,16,512]{3,2,1,0:T(8,128)(2,1)S(1)} %shard_map.57.refs_0_), channel_id=1, source_target_pairs={{0,24},{4,28},{8,0},{12,4},{16,8},{20,12},{24,16},{28,20},{1,25},{... | collective-permute-start | bytes 196616 | tf_op jit(solution)/shard_map/ppermute | solution.py:283
  59.5 6.5 %collective-permute-start.1 = (bf16[2,2,16,512]{3,2,1,0:T(8,128)(2,1)S(1)}, bf16[2,2,16,512]{3,2,1,0:T(8,128)(2,1)S(1)}, u32[]{:S(2)}, u32[]{:S(2)}) collective-permute-start(bf16[2,2,16,512]{3,2,1,0:T(8,128)(2,1)S(1)} %shard_map.57.refs_0_), channel_id=1, source_target_pairs={{0,8},{4,12},{8,16},{12,20},{16,24},{20,28},{24,0},{28,4},{1,9},{5... | collective-permute-start | bytes 196616 | tf_op jit(solution)/shard_map/ppermute | solution.py:283

commit v5 on v3

--- a/solution.py
+++ b/solution.py
@@ -158,6 +158,16 @@
     out_ref[...] = applied.astype(jnp.bfloat16).reshape(out_ref.shape)
 
 
+def finish_kernel(shares_ref, out_ref):
+    count, _, width = shares_ref.shape
+    sharers = out_ref.shape[1] // width
+    for sharer in range(sharers):
+        terms = [shares_ref[i].astype(jnp.float32) for i in range(sharer, count, sharers)]
+        while len(terms) > 1:
+            terms = [sum(terms[i : i + 2]) for i in range(0, len(terms), 2)]
+        out_ref[:, sharer * width : (sharer + 1) * width] = terms[0].astype(jnp.bfloat16)
+
+
 def swapped(array):
     return lax.ppermute(array, "core", [(0, 1), (1, 0)])
 
@@ -239,19 +249,27 @@
         compiler_params=params,
     )(*spread).reshape(-1, cycles)
 
-    pieces = lax.all_to_all(partial, ROW, 0, 0, tiled=True)
+    halves = partial.reshape(-1, vecs // lax.axis_size("yl"), half)
+    pieces = lax.all_to_all(halves, ROW_PAIR, 0, 0, tiled=True)
     own = jnp.sum(pieces.astype(jnp.float32), axis=0).astype(bf16)
     other = swapped(own)
     applied = pl.pallas_call(
         apply_kernel,
         in_specs=[vmem] * 3,
         out_specs=vmem,
-        out_shape=jax.ShapeDtypeStruct((2 * count, degrees, vecs), bf16),
-        cost_estimate=pl.CostEstimate(flops=2 * panel_rows.size * vecs, bytes_accessed=700_000, transcendentals=0),
+        out_shape=jax.ShapeDtypeStruct((2 * count, degrees, own.shape[0]), bf16),
+        cost_estimate=pl.CostEstimate(flops=2 * panel_rows.size * own.shape[0], bytes_accessed=700_000, transcendentals=0),
         compiler_params=params,
     )(panel_rows, own, other)
     shares = lax.all_to_all(applied, PLANE, 0, 0, tiled=True)
-    result = jnp.sum(shares.astype(jnp.float32), axis=0).astype(bf16)
+    result = pl.pallas_call(
+        finish_kernel,
+        in_specs=[vmem],
+        out_specs=vmem,
+        out_shape=jax.ShapeDtypeStruct((degrees, vecs), bf16),
+        cost_estimate=pl.CostEstimate(flops=shares.size, bytes_accessed=200_000, transcendentals=0),
+        compiler_params=params,
+    )(shares)
     return result[:, None, :]
 
 

time: 83.2 us -> 60 us (0.72)
  the two profiles are of different devices: /device:TPU:8 before, /device:TPU:1 now
where the time goes in v5:
time: 60 us; the launch traced here: 59.5 us
  starting transfers between devices  26.7 us (44%)
  blocking collectives  16 us (27%)
  waiting for transfers between devices  8.13 us (14%)
  Pallas kernels  7.8 us (13%)
  local copies, waits for them, and re-layouts  0.63 us (1%)
    all_to_all x1, blocking collectives, stages(): shares = lax.all_to_all(applied, PLANE, 0, 0, tiled=True)  16 us
    ppermute x3, starting transfers between devices, stages(): lax.ppermute(joined, 'z', [(i, (i + distance) % count) for i in range(cou...  9.18 us
    ppermute x3, starting transfers between devices, swapped(): return lax.ppermute(array, 'core', [(0, 1), (1, 0)])  6.17 us
    all_to_all x1, starting transfers between devices, stages(): lax.all_to_all(picks.reshape(-1, degrees, cycles), ROW_PAIR, 0, 0, tiled=...  5.26 us
    pallas_call x1, Pallas kernels, stages(): pl.pallas_call(panel_kernel, in_specs=[smem] + [vmem] * 6, out_specs=pl.B...  4.39 us
    all_to_all x1, starting transfers between devices, stages(): pieces = lax.all_to_all(halves, ROW_PAIR, 0, 0, tiled=True)  4.34 us
    all_to_all x1, waiting for transfers between devices, stages(): pieces = lax.all_to_all(halves, ROW_PAIR, 0, 0, tiled=True)  3.63 us
    pallas_call x1, Pallas kernels, stages(): pl.pallas_call(picks_kernel, in_specs=[smem, pl.BlockSpec(memory_space=pl...  2.53 us
  transfers between devices with their start and end apart: 9, of which 4 were waited for; matrix products, arithmetic and copies ran while one was open for 0% of the time, Pallas kernels for 12%

profile of v5, /device:TPU:1, one launch (start us, length us, event | category | flops | bytes accessed | tf_op | source)
XLA Modules:
  0.0 59.5 jit_solution(2886708346488605855)
XLA Ops:
  0.0 3.2 %collective-permute-start.4 = (bf16[64,16,512]{2,1,0:T(8,128)(2,1)}, bf16[64,16,512]{2,1,0:T(8,128)(2,1)S(1)}, u32[]{:S(2)}, u32[]{:S(2)}) collective-permute-start(bf16[64,16,512]{2,1,0:T(8,128)(2,1)} %own_t_ref.1), channel_id=1, source_target_pairs={{0,1},{1,0},{2,3},{3,2},{4,5},{5,4},{6,7},{7,6},{8,9},{9,8},{10,11... | collective-permute-start | bytes 3145736 | tf_op jit(solution)/shard_map/ppermute | solution.py:172
  3.2 0.0 collective-permute-start.5
  3.2 2.5 %shard_map.55 = bf16[8,2,16,512]{3,2,1,0:T(8,128)(2,1)} custom-call(s32[8]{0:T(128)} %orders_ref.3, bf16[64,16,512]{2,1,0:T(8,128)(2,1)} %own_t_ref.1), custom_call_target="tpu_custom_call" | custom-call | flops 1000000 | bytes 400000 | tf_op jit(solution)/shard_map/pallas_call | solution.py:188
  5.7 0.0 copy-start.2
  5.8 0.0 copy-start.3
  5.8 5.3 %all-to-all-start = ((bf16[16,16,512]{2,1,0:T(8,128)(2,1)}), bf16[16,16,512]{2,1,0:T(8,128)(2,1)S(1)}, u32[]{:S(2)}, u32[]{:S(2)}) async-start(bf16[16,16,512]{2,1,0:T(8,128)(2,1)} %bitcast.10), calls=%async_computation | async-start | bytes 524288 | tf_op jit(solution)/shard_map/all_to_all | solution.py:200
  11.0 0.0 collective-permute-done.5.other_v_ref
  11.0 0.0 collective-permute-done.4.other_t_ref
  11.1 0.0 copy-start.1
  11.1 0.0 copy-done
  11.1 0.0 copy-done.4
  11.1 0.0 copy-done.2
  11.1 0.0 copy-done.3
  11.1 0.6 %copy-done.1 = s32[8]{0:T(128)S(1)} copy-done((s32[8]{0:T(128)S(1)}, s32[8]{0:T(128)}, u32[]{:S(2)}) %copy-start.1) | copy-done | bytes 56
  11.7 4.4 %shard_map.58 = bf16[8,256,256]{2,1,0:T(8,128)(2,1)} custom-call(s32[8]{0:T(128)S(1)} %copy-done.1, s32[2,512]{1,0:T(2,128)S(1)} %bitcast.8, f32[1,512]{1,0:T(1,128)S(1)} %bitcast.9, bf16[64,16,512]{2,1,0:T(8,128)(2,1)S(1)} %copy-done, bf16[64,16,512]{2,1,0:T(8,128)(2,1)S(1)} %collective-permute-done.4.other_t_ref, bf16[64,16,256]{2,1,0:T(8,128)(2,1)S(1)} %copy-done.2, ...), custom_call_target="tpu_custom_call" | custom-call | flops 2147483648 | bytes 3500000 | tf_op jit(solution)/shard_map/pallas_call | solution.py:202
  16.1 2.3 %all-to-all-done = bf16[16,16,512]{2,1,0:T(8,128)(2,1)S(1)} async-done(((bf16[16,16,512]{2,1,0:T(8,128)(2,1)}), bf16[16,16,512]{2,1,0:T(8,128)(2,1)S(1)}, u32[]{:S(2)}, u32[]{:S(2)}) %all-to-all-start) | async-done | bytes 262176 | tf_op jit(solution)/shard_map/all_to_all | solution.py:200
  18.5 4.3 %all-to-all-start.1 = ((bf16[16,128,256]{2,1,0:T(8,128)(2,1)}), bf16[16,128,256]{2,1,0:T(8,128)(2,1)S(1)}, u32[]{:S(2)}, u32[]{:S(2)}) async-start(bf16[16,128,256]{2,1,0:T(8,128)(2,1)} %bitcast.5), calls=%async_computation.1 | async-start | bytes 2097152 | tf_op jit(solution)/shard_map/all_to_all | solution.py:253
  22.9 1.7 %collective-permute-start = (bf16[2,16,512]{2,1,0:T(8,128)(2,1)S(1)}, bf16[2,16,512]{2,1,0:T(8,128)(2,1)S(1)}, u32[]{:S(2)}, u32[]{:S(2)}) collective-permute-start(bf16[2,16,512]{2,1,0:T(8,128)(2,1)S(1)} %reduce_sum.24.own_ref), channel_id=1, source_target_pairs={{0,4},{4,0},{8,12},{12,8},{16,20},{20,16},{24,28},{28,24},{1,5},{5... | collective-permute-start | bytes 98312 | tf_op jit(solution)/shard_map/ppermute | solution.py:231
  24.6 1.3 %collective-permute-done.other_ref = bf16[2,16,512]{2,1,0:T(8,128)(2,1)S(1)} collective-permute-done((bf16[2,16,512]{2,1,0:T(8,128)(2,1)S(1)}, bf16[2,16,512]{2,1,0:T(8,128)(2,1)S(1)}, u32[]{:S(2)}, u32[]{:S(2)}) %collective-permute-start) | collective-permute-done | bytes 32800 | tf_op jit(solution)/shard_map/ppermute | solution.py:231
  25.9 6.8 %collective-permute-start.3 = (bf16[2,2,16,512]{3,2,1,0:T(8,128)(2,1)S(1)}, bf16[2,2,16,512]{3,2,1,0:T(8,128)(2,1)S(1)}, u32[]{:S(2)}, u32[]{:S(2)}) collective-permute-start(bf16[2,2,16,512]{3,2,1,0:T(8,128)(2,1)S(1)} %shard_map.56.refs_0_), channel_id=1, source_target_pairs={{0,16},{4,20},{8,24},{12,28},{16,0},{20,4},{24,8},{28,12},{1,17},{... | collective-permute-start | bytes 196616 | tf_op jit(solution)/shard_map/ppermute | solution.py:242
  32.7 0.0 collective-permute-start.2
  32.7 2.4 %collective-permute-start.1 = (bf16[2,2,16,512]{3,2,1,0:T(8,128)(2,1)S(1)}, bf16[2,2,16,512]{3,2,1,0:T(8,128)(2,1)S(1)}, u32[]{:S(2)}, u32[]{:S(2)}) collective-permute-start(bf16[2,2,16,512]{3,2,1,0:T(8,128)(2,1)S(1)} %shard_map.56.refs_0_), channel_id=1, source_target_pairs={{0,8},{4,12},{8,16},{12,20},{16,24},{20,28},{24,0},{28,4},{1,9},{5... | collective-permute-start | bytes 196616 | tf_op jit(solution)/shard_map/ppermute | solution.py:242
  35.1 3.6 %all-to-all-done.1 = bf16[16,128,256]{2,1,0:T(8,128)(2,1)S(1)} async-done(((bf16[16,128,256]{2,1,0:T(8,128)(2,1)}), bf16[16,128,256]{2,1,0:T(8,128)(2,1)S(1)}, u32[]{:S(2)}, u32[]{:S(2)}) %all-to-all-start.1) | async-done | bytes 1048608 | tf_op jit(solution)/shard_map/all_to_all | solution.py:253
  38.7 0.1 reduce_sum.25.own_ref
  38.8 3.0 %collective-permute-start.6 = (bf16[128,256]{1,0:T(8,128)(2,1)S(1)}, bf16[128,256]{1,0:T(8,128)(2,1)S(1)}, u32[]{:S(2)}, u32[]{:S(2)}) collective-permute-start(bf16[128,256]{1,0:T(8,128)(2,1)S(1)} %reduce_sum.25.own_ref), channel_id=1, source_target_pairs={{0,1},{1,0},{2,3},{3,2},{4,5},{5,4},{6,7},{7,6},{8,9},{9,8},{10,11... | collective-permute-start | bytes 196616 | tf_op jit(solution)/shard_map/ppermute | solution.py:172
  41.8 0.0 collective-permute-done.3.refs_3_
  41.8 0.0 collective-permute-done.2.refs_2_
  41.8 0.0 collective-permute-done.1.refs_1_
  41.9 0.8 %collective-permute-done.6.other_ref = bf16[128,256]{1,0:T(8,128)(2,1)S(1)} collective-permute-done((bf16[128,256]{1,0:T(8,128)(2,1)S(1)}, bf16[128,256]{1,0:T(8,128)(2,1)S(1)}, u32[]{:S(2)}, u32[]{:S(2)}) %collective-permute-start.6) | collective-permute-done | bytes 65568 | tf_op jit(solution)/shard_map/ppermute | solution.py:172
  42.7 0.2 shard_map.59
  42.9 16.0 %all_to_all.15.shares_ref = bf16[16,16,128]{2,1,0:T(8,128)(2,1)S(1)} all-to-all(bf16[16,16,128]{2,1,0:T(8,128)(2,1)S(1)} %shard_map.59), channel_id=1, replica_groups=mesh['yh'=2,'x'=4,'z'=8,'yl'=2,'core'=2] {'z','yl'}, dimensions={0} | all-to-all | bytes 131072 | tf_op jit(solution)/shard_map/all_to_all | solution.py:264
  58.9 0.6 %shard_map.60 = bf16[16,256]{1,0:T(8,128)(2,1)} custom-call(bf16[16,16,128]{2,1,0:T(8,128)(2,1)S(1)} %all_to_all.15.shares_ref), custom_call_target="tpu_custom_call" | custom-call | flops 32768 | bytes 200000 | tf_op jit(solution)/shard_map/pallas_call | solution.py:265
  (5 shorter events, 0.1 us)
Async XLA Ops:
  0.0 11.1 %copy-start = (bf16[64,16,512]{2,1,0:T(8,128)(2,1)S(1)}, bf16[64,16,512]{2,1,0:T(8,128)(2,1)}, u32[]{:S(2)}) copy-start(bf16[64,16,512]{2,1,0:T(8,128)(2,1)} %own_t_ref.1) | copy-start | bytes 3145732
  0.0 11.0 %collective-permute-start.4 = (bf16[64,16,512]{2,1,0:T(8,128)(2,1)}, bf16[64,16,512]{2,1,0:T(8,128)(2,1)S(1)}, u32[]{:S(2)}, u32[]{:S(2)}) collective-permute-start(bf16[64,16,512]{2,1,0:T(8,128)(2,1)} %own_t_ref.1), channel_id=1, source_target_pairs={{0,1},{1,0},{2,3},{3,2},{4,5},{5,4},{6,7},{7,6},{8,9},{9,8},{10,11... | collective-permute-start | bytes 3145736 | tf_op jit(solution)/shard_map/ppermute | solution.py:172
  3.2 7.8 %collective-permute-start.5 = (bf16[64,16,256]{2,1,0:T(8,128)(2,1)}, bf16[64,16,256]{2,1,0:T(8,128)(2,1)S(1)}, u32[]{:S(2)}, u32[]{:S(2)}) collective-permute-start(bf16[64,16,256]{2,1,0:T(8,128)(2,1)} %own_v_ref.1), channel_id=1, source_target_pairs={{0,1},{1,0},{2,3},{3,2},{4,5},{5,4},{6,7},{7,6},{8,9},{9,8},{10,11... | collective-permute-start | bytes 1572872 | tf_op jit(solution)/shard_map/ppermute | solution.py:172
  3.2 7.9 %copy-start.4 = (f32[512]{0:T(512)S(1)}, f32[512]{0:T(512)}, u32[]{:S(2)}) copy-start(f32[512]{0:T(512)} %param.9) | copy-start | bytes 6148
  5.7 5.3 %copy-start.2 = (bf16[64,16,256]{2,1,0:T(8,128)(2,1)S(1)}, bf16[64,16,256]{2,1,0:T(8,128)(2,1)}, u32[]{:S(2)}) copy-start(bf16[64,16,256]{2,1,0:T(8,128)(2,1)} %own_v_ref.1) | copy-start | bytes 1572868
  5.8 5.3 %copy-start.3 = (s32[512,2]{0,1:T(2,128)S(1)}, s32[512,2]{0,1:T(2,128)}, u32[]{:S(2)}) copy-start(s32[512,2]{0,1:T(2,128)} %param.8) | copy-start | bytes 12292
  5.8 12.7 %all-to-all-start = ((bf16[16,16,512]{2,1,0:T(8,128)(2,1)}), bf16[16,16,512]{2,1,0:T(8,128)(2,1)S(1)}, u32[]{:S(2)}, u32[]{:S(2)}) async-start(bf16[16,16,512]{2,1,0:T(8,128)(2,1)} %bitcast.10), calls=%async_computation | async-start | bytes 524288 | tf_op jit(solution)/shard_map/all_to_all | solution.py:200
  11.1 0.7 %copy-start.1 = (s32[8]{0:T(128)S(1)}, s32[8]{0:T(128)}, u32[]{:S(2)}) copy-start(s32[8]{0:T(128)} %orders_ref.3) | copy-start | bytes 100
  18.5 20.2 %all-to-all-start.1 = ((bf16[16,128,256]{2,1,0:T(8,128)(2,1)}), bf16[16,128,256]{2,1,0:T(8,128)(2,1)S(1)}, u32[]{:S(2)}, u32[]{:S(2)}) async-start(bf16[16,128,256]{2,1,0:T(8,128)(2,1)} %bitcast.5), calls=%async_computation.1 | async-start | bytes 2097152 | tf_op jit(solution)/shard_map/all_to_all | solution.py:253
  22.9 3.0 %collective-permute-start = (bf16[2,16,512]{2,1,0:T(8,128)(2,1)S(1)}, bf16[2,16,512]{2,1,0:T(8,128)(2,1)S(1)}, u32[]{:S(2)}, u32[]{:S(2)}) collective-permute-start(bf16[2,16,512]{2,1,0:T(8,128)(2,1)S(1)} %reduce_sum.24.own_ref), channel_id=1, source_target_pairs={{0,4},{4,0},{8,12},{12,8},{16,20},{20,16},{24,28},{28,24},{1,5},{5... | collective-permute-start | bytes 98312 | tf_op jit(solution)/shard_map/ppermute | solution.py:231
  25.9 15.9 %collective-permute-start.3 = (bf16[2,2,16,512]{3,2,1,0:T(8,128)(2,1)S(1)}, bf16[2,2,16,512]{3,2,1,0:T(8,128)(2,1)S(1)}, u32[]{:S(2)}, u32[]{:S(2)}) collective-permute-start(bf16[2,2,16,512]{3,2,1,0:T(8,128)(2,1)S(1)} %shard_map.56.refs_0_), channel_id=1, source_target_pairs={{0,16},{4,20},{8,24},{12,28},{16,0},{20,4},{24,8},{28,12},{1,17},{... | collective-permute-start | bytes 196616 | tf_op jit(solution)/shard_map/ppermute | solution.py:242
  32.7 9.1 %collective-permute-start.2 = (bf16[2,2,16,512]{3,2,1,0:T(8,128)(2,1)S(1)}, bf16[2,2,16,512]{3,2,1,0:T(8,128)(2,1)S(1)}, u32[]{:S(2)}, u32[]{:S(2)}) collective-permute-start(bf16[2,2,16,512]{3,2,1,0:T(8,128)(2,1)S(1)} %shard_map.56.refs_0_), channel_id=1, source_target_pairs={{0,24},{4,28},{8,0},{12,4},{16,8},{20,12},{24,16},{28,20},{1,25},{... | collective-permute-start | bytes 196616 | tf_op jit(solution)/shard_map/ppermute | solution.py:242
  32.7 9.1 %collective-permute-start.1 = (bf16[2,2,16,512]{3,2,1,0:T(8,128)(2,1)S(1)}, bf16[2,2,16,512]{3,2,1,0:T(8,128)(2,1)S(1)}, u32[]{:S(2)}, u32[]{:S(2)}) collective-permute-start(bf16[2,2,16,512]{3,2,1,0:T(8,128)(2,1)S(1)} %shard_map.56.refs_0_), channel_id=1, source_target_pairs={{0,8},{4,12},{8,16},{12,20},{16,24},{20,28},{24,0},{28,4},{1,9},{5... | collective-permute-start | bytes 196616 | tf_op jit(solution)/shard_map/ppermute | solution.py:242
  38.8 3.9 %collective-permute-start.6 = (bf16[128,256]{1,0:T(8,128)(2,1)S(1)}, bf16[128,256]{1,0:T(8,128)(2,1)S(1)}, u32[]{:S(2)}, u32[]{:S(2)}) collective-permute-start(bf16[128,256]{1,0:T(8,128)(2,1)S(1)} %reduce_sum.25.own_ref), channel_id=1, source_target_pairs={{0,1},{1,0},{2,3},{3,2},{4,5},{5,4},{6,7},{7,6},{8,9},{9,8},{10,11... | collective-permute-start | bytes 196616 | tf_op jit(solution)/shard_map/ppermute | solution.py:172

commit v6 on v5

--- a/solution.py
+++ b/solution.py
@@ -38,7 +38,7 @@
     return jnp.where(zero, 0.0, jnp.float32(CELL) / jnp.where(zero, 1.0, sine))
 
 
-def picks_kernel(orders_ref, leg_ref, picks_ref, rows, sems):
+def picks_kernel(orders_ref, leg_ref, picks_ref, panel_orders, tables, sems):
     panels, sharers, degrees, cycles = picks_ref.shape
     orders = leg_ref.shape[0]
     half = cycles // 2
@@ -46,19 +46,22 @@
     core = lax.axis_index("core")
     own = pl.ds(pl.multiple_of(core * half, half), half)
     other = pl.ds(pl.multiple_of((1 - core) * half, half), half)
-    copies = []
-    for p in range(panels):
-        place = jnp.clip(orders_ref[p] - first_order, 0, orders - 1)
-        copies.append(pltpu.make_async_copy(leg_ref.at[place], rows.at[p], sems.at[p]))
-        copies[p].start()
+    copies = [
+        pltpu.make_async_copy(orders_ref, panel_orders, sems.at[0]),
+        pltpu.make_async_copy(leg_ref, tables, sems.at[1]),
+    ]
+    for copy in copies:
+        copy.start()
     degree = lax.broadcasted_iota(jnp.int32, (degrees, half), 0) + lax.axis_index(COL) * degrees
-    for p in range(panels):
-        panel = orders_ref[p]
+    for copy in copies:
+        copy.wait()
+    for p in range(panels):
+        panel = panel_orders[p]
         held = (panel >= first_order) & (panel < first_order + orders)
+        place = jnp.clip(panel - first_order, 0, orders - 1)
         kept = degree >= jnp.where(held, panel, orders * lax.axis_size(ROW))
-        copies[p].wait()
         for lanes, part in ((own, slice(0, half)), (other, slice(half, cycles))):
-            pick = jnp.where(kept, rows[p, :, lanes].astype(jnp.float32), 0.0).astype(jnp.bfloat16)
+            pick = jnp.where(kept, tables[place, :, lanes].astype(jnp.float32), 0.0).astype(jnp.bfloat16)
             for sharer in range(sharers):
                 picks_ref[p, sharer, :, part] = pick
 
@@ -187,12 +190,13 @@
     other_vectors = swapped(vectors)
     picks = pl.pallas_call(
         picks_kernel,
-        in_specs=[smem, pl.BlockSpec(memory_space=pltpu.HBM)],
+        in_specs=[pl.BlockSpec(memory_space=pltpu.HBM)] * 2,
         out_specs=vmem,
         out_shape=jax.ShapeDtypeStruct((panels, lax.axis_size("yl"), degrees, cycles), bf16),
         scratch_shapes=[
-            pltpu.VMEM((panels, degrees, cycles), bf16),
-            pltpu.SemaphoreType.DMA((panels,)),
+            pltpu.SMEM((panels,), jnp.int32),
+            pltpu.VMEM((orders, degrees, cycles), bf16),
+            pltpu.SemaphoreType.DMA((2,)),
         ],
         cost_estimate=pl.CostEstimate(flops=1_000_000, bytes_accessed=400_000, transcendentals=0),
         compiler_params=pltpu.CompilerParams(vmem_limit_bytes=60 * 1024 * 1024),

time: 60 us -> 59.3 us (0.988)
  transfers between devices with their start and end apart: 9 -> 9, of which waited for: 4 -> 4; matrix products, arithmetic and copies ran while one was open for 0% -> 0% of each run, Pallas kernels for 12% -> 11%
where the time goes in v6:
time: 59.3 us; the launch traced here: 59 us
  starting transfers between devices  26.7 us (45%)
  blocking collectives  16 us (27%)
  waiting for transfers between devices  8.13 us (14%)
  Pallas kernels  7.26 us (12%)
  local copies, waits for them, and re-layouts  0.63 us (1%)
    all_to_all x1, blocking collectives, stages(): shares = lax.all_to_all(applied, PLANE, 0, 0, tiled=True)  16 us
    ppermute x3, starting transfers between devices, stages(): lax.ppermute(joined, 'z', [(i, (i + distance) % count) for i in range(cou...  9.17 us
    ppermute x3, starting transfers between devices, swapped(): return lax.ppermute(array, 'core', [(0, 1), (1, 0)])  6.17 us
    all_to_all x1, starting transfers between devices, stages(): lax.all_to_all(picks.reshape(-1, degrees, cycles), ROW_PAIR, 0, 0, tiled=...  5.27 us
    pallas_call x1, Pallas kernels, stages(): pl.pallas_call(panel_kernel, in_specs=[smem] + [vmem] * 6, out_specs=pl.B...  4.38 us
    all_to_all x1, starting transfers between devices, stages(): pieces = lax.all_to_all(halves, ROW_PAIR, 0, 0, tiled=True)  4.34 us
    all_to_all x1, waiting for transfers between devices, stages(): pieces = lax.all_to_all(halves, ROW_PAIR, 0, 0, tiled=True)  3.62 us
    all_to_all x1, waiting for transfers between devices, stages(): lax.all_to_all(picks.reshape(-1, degrees, cycles), ROW_PAIR, 0, 0, tiled=...  2.35 us
  transfers between devices with their start and end apart: 9, of which 4 were waited for; matrix products, arithmetic and copies ran while one was open for 0% of the time, Pallas kernels for 11%

profile of v6, /device:TPU:1, one launch (start us, length us, event | category | flops | bytes accessed | tf_op | source)
XLA Modules:
  0.0 59.0 jit_solution(6958876010894936273)
XLA Ops:
  0.0 3.2 %collective-permute-start.4 = (bf16[64,16,512]{2,1,0:T(8,128)(2,1)}, bf16[64,16,512]{2,1,0:T(8,128)(2,1)S(1)}, u32[]{:S(2)}, u32[]{:S(2)}) collective-permute-start(bf16[64,16,512]{2,1,0:T(8,128)(2,1)} %own_t_ref.1), channel_id=1, source_target_pairs={{0,1},{1,0},{2,3},{3,2},{4,5},{5,4},{6,7},{7,6},{8,9},{9,8},{10,11... | collective-permute-start | bytes 3145736 | tf_op jit(solution)/shard_map/ppermute | solution.py:175
  3.2 0.0 collective-permute-start.5
  3.2 2.0 %shard_map.55 = bf16[8,2,16,512]{3,2,1,0:T(8,128)(2,1)} custom-call(s32[8]{0:T(128)} %orders_ref.3, bf16[64,16,512]{2,1,0:T(8,128)(2,1)} %own_t_ref.1), custom_call_target="tpu_custom_call" | custom-call | flops 1000000 | bytes 400000 | tf_op jit(solution)/shard_map/pallas_call | solution.py:191
  5.2 0.0 copy-start.2
  5.2 0.0 copy-start.3
  5.2 5.3 %all-to-all-start = ((bf16[16,16,512]{2,1,0:T(8,128)(2,1)}), bf16[16,16,512]{2,1,0:T(8,128)(2,1)S(1)}, u32[]{:S(2)}, u32[]{:S(2)}) async-start(bf16[16,16,512]{2,1,0:T(8,128)(2,1)} %bitcast.10), calls=%async_computation | async-start | bytes 524288 | tf_op jit(solution)/shard_map/all_to_all | solution.py:204
  10.5 0.0 collective-permute-done.5.other_v_ref
  10.5 0.0 collective-permute-done.4.other_t_ref
  10.5 0.0 copy-start.1
  10.6 0.0 copy-done
  10.6 0.0 copy-done.4
  10.6 0.0 copy-done.2
  10.6 0.0 copy-done.3
  10.6 0.6 %copy-done.1 = s32[8]{0:T(128)S(1)} copy-done((s32[8]{0:T(128)S(1)}, s32[8]{0:T(128)}, u32[]{:S(2)}) %copy-start.1) | copy-done | bytes 56
  11.2 4.4 %shard_map.58 = bf16[8,256,256]{2,1,0:T(8,128)(2,1)} custom-call(s32[8]{0:T(128)S(1)} %copy-done.1, s32[2,512]{1,0:T(2,128)S(1)} %bitcast.8, f32[1,512]{1,0:T(1,128)S(1)} %bitcast.9, bf16[64,16,512]{2,1,0:T(8,128)(2,1)S(1)} %copy-done, bf16[64,16,512]{2,1,0:T(8,128)(2,1)S(1)} %collective-permute-done.4.other_t_ref, bf16[64,16,256]{2,1,0:T(8,128)(2,1)S(1)} %copy-done.2, ...), custom_call_target="tpu_custom_call" | custom-call | flops 2147483648 | bytes 3500000 | tf_op jit(solution)/shard_map/pallas_call | solution.py:206
  15.6 2.4 %all-to-all-done = bf16[16,16,512]{2,1,0:T(8,128)(2,1)S(1)} async-done(((bf16[16,16,512]{2,1,0:T(8,128)(2,1)}), bf16[16,16,512]{2,1,0:T(8,128)(2,1)S(1)}, u32[]{:S(2)}, u32[]{:S(2)}) %all-to-all-start) | async-done | bytes 262176 | tf_op jit(solution)/shard_map/all_to_all | solution.py:204
  17.9 4.3 %all-to-all-start.1 = ((bf16[16,128,256]{2,1,0:T(8,128)(2,1)}), bf16[16,128,256]{2,1,0:T(8,128)(2,1)S(1)}, u32[]{:S(2)}, u32[]{:S(2)}) async-start(bf16[16,128,256]{2,1,0:T(8,128)(2,1)} %bitcast.5), calls=%async_computation.1 | async-start | bytes 2097152 | tf_op jit(solution)/shard_map/all_to_all | solution.py:257
  22.3 1.7 %collective-permute-start = (bf16[2,16,512]{2,1,0:T(8,128)(2,1)S(1)}, bf16[2,16,512]{2,1,0:T(8,128)(2,1)S(1)}, u32[]{:S(2)}, u32[]{:S(2)}) collective-permute-start(bf16[2,16,512]{2,1,0:T(8,128)(2,1)S(1)} %reduce_sum.24.own_ref), channel_id=1, source_target_pairs={{0,4},{4,0},{8,12},{12,8},{16,20},{20,16},{24,28},{28,24},{1,5},{5... | collective-permute-start | bytes 98312 | tf_op jit(solution)/shard_map/ppermute | solution.py:235
  24.1 1.3 %collective-permute-done.other_ref = bf16[2,16,512]{2,1,0:T(8,128)(2,1)S(1)} collective-permute-done((bf16[2,16,512]{2,1,0:T(8,128)(2,1)S(1)}, bf16[2,16,512]{2,1,0:T(8,128)(2,1)S(1)}, u32[]{:S(2)}, u32[]{:S(2)}) %collective-permute-start) | collective-permute-done | bytes 32800 | tf_op jit(solution)/shard_map/ppermute | solution.py:235
  25.4 6.8 %collective-permute-start.3 = (bf16[2,2,16,512]{3,2,1,0:T(8,128)(2,1)S(1)}, bf16[2,2,16,512]{3,2,1,0:T(8,128)(2,1)S(1)}, u32[]{:S(2)}, u32[]{:S(2)}) collective-permute-start(bf16[2,2,16,512]{3,2,1,0:T(8,128)(2,1)S(1)} %shard_map.56.refs_0_), channel_id=1, source_target_pairs={{0,16},{4,20},{8,24},{12,28},{16,0},{20,4},{24,8},{28,12},{1,17},{... | collective-permute-start | bytes 196616 | tf_op jit(solution)/shard_map/ppermute | solution.py:246
  32.2 0.0 collective-permute-start.2
  32.2 2.4 %collective-permute-start.1 = (bf16[2,2,16,512]{3,2,1,0:T(8,128)(2,1)S(1)}, bf16[2,2,16,512]{3,2,1,0:T(8,128)(2,1)S(1)}, u32[]{:S(2)}, u32[]{:S(2)}) collective-permute-start(bf16[2,2,16,512]{3,2,1,0:T(8,128)(2,1)S(1)} %shard_map.56.refs_0_), channel_id=1, source_target_pairs={{0,8},{4,12},{8,16},{12,20},{16,24},{20,28},{24,0},{28,4},{1,9},{5... | collective-permute-start | bytes 196616 | tf_op jit(solution)/shard_map/ppermute | solution.py:246
  34.6 3.6 %all-to-all-done.1 = bf16[16,128,256]{2,1,0:T(8,128)(2,1)S(1)} async-done(((bf16[16,128,256]{2,1,0:T(8,128)(2,1)}), bf16[16,128,256]{2,1,0:T(8,128)(2,1)S(1)}, u32[]{:S(2)}, u32[]{:S(2)}) %all-to-all-start.1) | async-done | bytes 1048608 | tf_op jit(solution)/shard_map/all_to_all | solution.py:257
  38.2 0.1 reduce_sum.25.own_ref
  38.3 3.0 %collective-permute-start.6 = (bf16[128,256]{1,0:T(8,128)(2,1)S(1)}, bf16[128,256]{1,0:T(8,128)(2,1)S(1)}, u32[]{:S(2)}, u32[]{:S(2)}) collective-permute-start(bf16[128,256]{1,0:T(8,128)(2,1)S(1)} %reduce_sum.25.own_ref), channel_id=1, source_target_pairs={{0,1},{1,0},{2,3},{3,2},{4,5},{5,4},{6,7},{7,6},{8,9},{9,8},{10,11... | collective-permute-start | bytes 196616 | tf_op jit(solution)/shard_map/ppermute | solution.py:175
  41.3 0.0 collective-permute-done.3.refs_3_
  41.3 0.0 collective-permute-done.2.refs_2_
  41.3 0.0 collective-permute-done.1.refs_1_
  41.3 0.8 %collective-permute-done.6.other_ref = bf16[128,256]{1,0:T(8,128)(2,1)S(1)} collective-permute-done((bf16[128,256]{1,0:T(8,128)(2,1)S(1)}, bf16[128,256]{1,0:T(8,128)(2,1)S(1)}, u32[]{:S(2)}, u32[]{:S(2)}) %collective-permute-start.6) | collective-permute-done | bytes 65568 | tf_op jit(solution)/shard_map/ppermute | solution.py:175
  42.2 0.2 shard_map.59
  42.4 16.0 %all_to_all.15.shares_ref = bf16[16,16,128]{2,1,0:T(8,128)(2,1)S(1)} all-to-all(bf16[16,16,128]{2,1,0:T(8,128)(2,1)S(1)} %shard_map.59), channel_id=1, replica_groups=mesh['yh'=2,'x'=4,'z'=8,'yl'=2,'core'=2] {'z','yl'}, dimensions={0} | all-to-all | bytes 131072 | tf_op jit(solution)/shard_map/all_to_all | solution.py:268
  58.4 0.6 %shard_map.60 = bf16[16,256]{1,0:T(8,128)(2,1)} custom-call(bf16[16,16,128]{2,1,0:T(8,128)(2,1)S(1)} %all_to_all.15.shares_ref), custom_call_target="tpu_custom_call" | custom-call | flops 32768 | bytes 200000 | tf_op jit(solution)/shard_map/pallas_call | solution.py:269
  (5 shorter events, 0.1 us)
Async XLA Ops:
  0.0 10.6 %copy-start = (bf16[64,16,512]{2,1,0:T(8,128)(2,1)S(1)}, bf16[64,16,512]{2,1,0:T(8,128)(2,1)}, u32[]{:S(2)}) copy-start(bf16[64,16,512]{2,1,0:T(8,128)(2,1)} %own_t_ref.1) | copy-start | bytes 3145732
  0.0 10.5 %collective-permute-start.4 = (bf16[64,16,512]{2,1,0:T(8,128)(2,1)}, bf16[64,16,512]{2,1,0:T(8,128)(2,1)S(1)}, u32[]{:S(2)}, u32[]{:S(2)}) collective-permute-start(bf16[64,16,512]{2,1,0:T(8,128)(2,1)} %own_t_ref.1), channel_id=1, source_target_pairs={{0,1},{1,0},{2,3},{3,2},{4,5},{5,4},{6,7},{7,6},{8,9},{9,8},{10,11... | collective-permute-start | bytes 3145736 | tf_op jit(solution)/shard_map/ppermute | solution.py:175
  3.2 7.3 %collective-permute-start.5 = (bf16[64,16,256]{2,1,0:T(8,128)(2,1)}, bf16[64,16,256]{2,1,0:T(8,128)(2,1)S(1)}, u32[]{:S(2)}, u32[]{:S(2)}) collective-permute-start(bf16[64,16,256]{2,1,0:T(8,128)(2,1)} %own_v_ref.1), channel_id=1, source_target_pairs={{0,1},{1,0},{2,3},{3,2},{4,5},{5,4},{6,7},{7,6},{8,9},{9,8},{10,11... | collective-permute-start | bytes 1572872 | tf_op jit(solution)/shard_map/ppermute | solution.py:175
  3.2 7.4 %copy-start.4 = (f32[512]{0:T(512)S(1)}, f32[512]{0:T(512)}, u32[]{:S(2)}) copy-start(f32[512]{0:T(512)} %param.9) | copy-start | bytes 6148
  5.2 5.4 %copy-start.2 = (bf16[64,16,256]{2,1,0:T(8,128)(2,1)S(1)}, bf16[64,16,256]{2,1,0:T(8,128)(2,1)}, u32[]{:S(2)}) copy-start(bf16[64,16,256]{2,1,0:T(8,128)(2,1)} %own_v_ref.1) | copy-start | bytes 1572868
  5.2 5.4 %copy-start.3 = (s32[512,2]{0,1:T(2,128)S(1)}, s32[512,2]{0,1:T(2,128)}, u32[]{:S(2)}) copy-start(s32[512,2]{0,1:T(2,128)} %param.8) | copy-start | bytes 12292
  5.2 12.7 %all-to-all-start = ((bf16[16,16,512]{2,1,0:T(8,128)(2,1)}), bf16[16,16,512]{2,1,0:T(8,128)(2,1)S(1)}, u32[]{:S(2)}, u32[]{:S(2)}) async-start(bf16[16,16,512]{2,1,0:T(8,128)(2,1)} %bitcast.10), calls=%async_computation | async-start | bytes 524288 | tf_op jit(solution)/shard_map/all_to_all | solution.py:204
  10.5 0.7 %copy-start.1 = (s32[8]{0:T(128)S(1)}, s32[8]{0:T(128)}, u32[]{:S(2)}) copy-start(s32[8]{0:T(128)} %orders_ref.3) | copy-start | bytes 100
  17.9 20.2 %all-to-all-start.1 = ((bf16[16,128,256]{2,1,0:T(8,128)(2,1)}), bf16[16,128,256]{2,1,0:T(8,128)(2,1)S(1)}, u32[]{:S(2)}, u32[]{:S(2)}) async-start(bf16[16,128,256]{2,1,0:T(8,128)(2,1)} %bitcast.5), calls=%async_computation.1 | async-start | bytes 2097152 | tf_op jit(solution)/shard_map/all_to_all | solution.py:257
  22.3 3.0 %collective-permute-start = (bf16[2,16,512]{2,1,0:T(8,128)(2,1)S(1)}, bf16[2,16,512]{2,1,0:T(8,128)(2,1)S(1)}, u32[]{:S(2)}, u32[]{:S(2)}) collective-permute-start(bf16[2,16,512]{2,1,0:T(8,128)(2,1)S(1)} %reduce_sum.24.own_ref), channel_id=1, source_target_pairs={{0,4},{4,0},{8,12},{12,8},{16,20},{20,16},{24,28},{28,24},{1,5},{5... | collective-permute-start | bytes 98312 | tf_op jit(solution)/shard_map/ppermute | solution.py:235
  25.4 15.9 %collective-permute-start.3 = (bf16[2,2,16,512]{3,2,1,0:T(8,128)(2,1)S(1)}, bf16[2,2,16,512]{3,2,1,0:T(8,128)(2,1)S(1)}, u32[]{:S(2)}, u32[]{:S(2)}) collective-permute-start(bf16[2,2,16,512]{3,2,1,0:T(8,128)(2,1)S(1)} %shard_map.56.refs_0_), channel_id=1, source_target_pairs={{0,16},{4,20},{8,24},{12,28},{16,0},{20,4},{24,8},{28,12},{1,17},{... | collective-permute-start | bytes 196616 | tf_op jit(solution)/shard_map/ppermute | solution.py:246
  32.2 9.1 %collective-permute-start.2 = (bf16[2,2,16,512]{3,2,1,0:T(8,128)(2,1)S(1)}, bf16[2,2,16,512]{3,2,1,0:T(8,128)(2,1)S(1)}, u32[]{:S(2)}, u32[]{:S(2)}) collective-permute-start(bf16[2,2,16,512]{3,2,1,0:T(8,128)(2,1)S(1)} %shard_map.56.refs_0_), channel_id=1, source_target_pairs={{0,24},{4,28},{8,0},{12,4},{16,8},{20,12},{24,16},{28,20},{1,25},{... | collective-permute-start | bytes 196616 | tf_op jit(solution)/shard_map/ppermute | solution.py:246
  32.2 9.1 %collective-permute-start.1 = (bf16[2,2,16,512]{3,2,1,0:T(8,128)(2,1)S(1)}, bf16[2,2,16,512]{3,2,1,0:T(8,128)(2,1)S(1)}, u32[]{:S(2)}, u32[]{:S(2)}) collective-permute-start(bf16[2,2,16,512]{3,2,1,0:T(8,128)(2,1)S(1)} %shard_map.56.refs_0_), channel_id=1, source_target_pairs={{0,8},{4,12},{8,16},{12,20},{16,24},{20,28},{24,0},{28,4},{1,9},{5... | collective-permute-start | bytes 196616 | tf_op jit(solution)/shard_map/ppermute | solution.py:246
  38.3 3.9 %collective-permute-start.6 = (bf16[128,256]{1,0:T(8,128)(2,1)S(1)}, bf16[128,256]{1,0:T(8,128)(2,1)S(1)}, u32[]{:S(2)}, u32[]{:S(2)}) collective-permute-start(bf16[128,256]{1,0:T(8,128)(2,1)S(1)} %reduce_sum.25.own_ref), channel_id=1, source_target_pairs={{0,1},{1,0},{2,3},{3,2},{4,5},{5,4},{6,7},{7,6},{8,9},{9,8},{10,11... | collective-permute-start | bytes 196616 | tf_op jit(solution)/shard_map/ppermute | solution.py:175

commit v7 on v6

--- a/solution.py
+++ b/solution.py
@@ -46,10 +46,10 @@
     core = lax.axis_index("core")
     own = pl.ds(pl.multiple_of(core * half, half), half)
     other = pl.ds(pl.multiple_of((1 - core) * half, half), half)
-    copies = [
-        pltpu.make_async_copy(orders_ref, panel_orders, sems.at[0]),
-        pltpu.make_async_copy(leg_ref, tables, sems.at[1]),
-    ]
+    copies = [pltpu.make_async_copy(orders_ref, panel_orders, sems.at[0])]
+    share = orders // (sems.shape[0] - 1)
+    for i in range(1, sems.shape[0]):
+        copies.append(pltpu.make_async_copy(leg_ref.at[pl.ds((i - 1) * share, share)], tables.at[pl.ds((i - 1) * share, share)], sems.at[i]))
     for copy in copies:
         copy.start()
     degree = lax.broadcasted_iota(jnp.int32, (degrees, half), 0) + lax.axis_index(COL) * degrees
@@ -196,7 +196,7 @@
         scratch_shapes=[
             pltpu.SMEM((panels,), jnp.int32),
             pltpu.VMEM((orders, degrees, cycles), bf16),
-            pltpu.SemaphoreType.DMA((2,)),
+            pltpu.SemaphoreType.DMA((5,)),
         ],
         cost_estimate=pl.CostEstimate(flops=1_000_000, bytes_accessed=400_000, transcendentals=0),
         compiler_params=pltpu.CompilerParams(vmem_limit_bytes=60 * 1024 * 1024),

time: 59.3 us -> 59.3 us (level)
  no operation moved by 1% of the time
where the time goes in v7:
time: 59.3 us; the launch traced here: 59 us
  starting transfers between devices  26.7 us (45%)
  blocking collectives  16 us (27%)
  waiting for transfers between devices  8.1 us (14%)
  Pallas kernels  7.26 us (12%)
  local copies, waits for them, and re-layouts  0.63 us (1%)
    all_to_all x1, blocking collectives, stages(): shares = lax.all_to_all(applied, PLANE, 0, 0, tiled=True)  16 us
    ppermute x3, starting transfers between devices, stages(): lax.ppermute(joined, 'z', [(i, (i + distance) % count) for i in range(cou...  9.19 us
    ppermute x3, starting transfers between devices, swapped(): return lax.ppermute(array, 'core', [(0, 1), (1, 0)])  6.17 us
    all_to_all x1, starting transfers between devices, stages(): lax.all_to_all(picks.reshape(-1, degrees, cycles), ROW_PAIR, 0, 0, tiled=...  5.27 us
    pallas_call x1, Pallas kernels, stages(): pl.pallas_call(panel_kernel, in_specs=[smem] + [vmem] * 6, out_specs=pl.B...  4.4 us
    all_to_all x1, starting transfers between devices, stages(): pieces = lax.all_to_all(halves, ROW_PAIR, 0, 0, tiled=True)  4.33 us
    all_to_all x1, waiting for transfers between devices, stages(): pieces = lax.all_to_all(halves, ROW_PAIR, 0, 0, tiled=True)  3.6 us
    all_to_all x1, waiting for transfers between devices, stages(): lax.all_to_all(picks.reshape(-1, degrees, cycles), ROW_PAIR, 0, 0, tiled=...  2.34 us
  transfers between devices with their start and end apart: 9, of which 4 were waited for; matrix products, arithmetic and copies ran while one was open for 0% of the time, Pallas kernels for 11%

profile of v7, /device:TPU:1, one launch (start us, length us, event | category | flops | bytes accessed | tf_op | source)
XLA Modules:
  0.0 59.0 jit_solution(5576229524905738470)
XLA Ops:
  0.0 3.2 %collective-permute-start.4 = (bf16[64,16,512]{2,1,0:T(8,128)(2,1)}, bf16[64,16,512]{2,1,0:T(8,128)(2,1)S(1)}, u32[]{:S(2)}, u32[]{:S(2)}) collective-permute-start(bf16[64,16,512]{2,1,0:T(8,128)(2,1)} %own_t_ref.1), channel_id=1, source_target_pairs={{0,1},{1,0},{2,3},{3,2},{4,5},{5,4},{6,7},{7,6},{8,9},{9,8},{10,11... | collective-permute-start | bytes 3145736 | tf_op jit(solution)/shard_map/ppermute | solution.py:175
  3.2 0.0 collective-permute-start.5
  3.2 2.0 %shard_map.55 = bf16[8,2,16,512]{3,2,1,0:T(8,128)(2,1)} custom-call(s32[8]{0:T(128)} %orders_ref.3, bf16[64,16,512]{2,1,0:T(8,128)(2,1)} %own_t_ref.1), custom_call_target="tpu_custom_call" | custom-call | flops 1000000 | bytes 400000 | tf_op jit(solution)/shard_map/pallas_call | solution.py:191
  5.2 0.0 copy-start.2
  5.2 0.0 copy-start.3
  5.2 5.3 %all-to-all-start = ((bf16[16,16,512]{2,1,0:T(8,128)(2,1)}), bf16[16,16,512]{2,1,0:T(8,128)(2,1)S(1)}, u32[]{:S(2)}, u32[]{:S(2)}) async-start(bf16[16,16,512]{2,1,0:T(8,128)(2,1)} %bitcast.10), calls=%async_computation | async-start | bytes 524288 | tf_op jit(solution)/shard_map/all_to_all | solution.py:204
  10.5 0.0 collective-permute-done.5.other_v_ref
  10.5 0.0 collective-permute-done.4.other_t_ref
  10.5 0.0 copy-start.1
  10.5 0.0 copy-done
  10.6 0.0 copy-done.4
  10.6 0.0 copy-done.2
  10.6 0.0 copy-done.3
  10.6 0.6 %copy-done.1 = s32[8]{0:T(128)S(1)} copy-done((s32[8]{0:T(128)S(1)}, s32[8]{0:T(128)}, u32[]{:S(2)}) %copy-start.1) | copy-done | bytes 56
  11.2 4.4 %shard_map.58 = bf16[8,256,256]{2,1,0:T(8,128)(2,1)} custom-call(s32[8]{0:T(128)S(1)} %copy-done.1, s32[2,512]{1,0:T(2,128)S(1)} %bitcast.8, f32[1,512]{1,0:T(1,128)S(1)} %bitcast.9, bf16[64,16,512]{2,1,0:T(8,128)(2,1)S(1)} %copy-done, bf16[64,16,512]{2,1,0:T(8,128)(2,1)S(1)} %collective-permute-done.4.other_t_ref, bf16[64,16,256]{2,1,0:T(8,128)(2,1)S(1)} %copy-done.2, ...), custom_call_target="tpu_custom_call" | custom-call | flops 2147483648 | bytes 3500000 | tf_op jit(solution)/shard_map/pallas_call | solution.py:206
  15.6 2.3 %all-to-all-done = bf16[16,16,512]{2,1,0:T(8,128)(2,1)S(1)} async-done(((bf16[16,16,512]{2,1,0:T(8,128)(2,1)}), bf16[16,16,512]{2,1,0:T(8,128)(2,1)S(1)}, u32[]{:S(2)}, u32[]{:S(2)}) %all-to-all-start) | async-done | bytes 262176 | tf_op jit(solution)/shard_map/all_to_all | solution.py:204
  17.9 4.3 %all-to-all-start.1 = ((bf16[16,128,256]{2,1,0:T(8,128)(2,1)}), bf16[16,128,256]{2,1,0:T(8,128)(2,1)S(1)}, u32[]{:S(2)}, u32[]{:S(2)}) async-start(bf16[16,128,256]{2,1,0:T(8,128)(2,1)} %bitcast.5), calls=%async_computation.1 | async-start | bytes 2097152 | tf_op jit(solution)/shard_map/all_to_all | solution.py:257
  22.3 1.7 %collective-permute-start = (bf16[2,16,512]{2,1,0:T(8,128)(2,1)S(1)}, bf16[2,16,512]{2,1,0:T(8,128)(2,1)S(1)}, u32[]{:S(2)}, u32[]{:S(2)}) collective-permute-start(bf16[2,16,512]{2,1,0:T(8,128)(2,1)S(1)} %reduce_sum.24.own_ref), channel_id=1, source_target_pairs={{0,4},{4,0},{8,12},{12,8},{16,20},{20,16},{24,28},{28,24},{1,5},{5... | collective-permute-start | bytes 98312 | tf_op jit(solution)/shard_map/ppermute | solution.py:235
  24.0 1.3 %collective-permute-done.other_ref = bf16[2,16,512]{2,1,0:T(8,128)(2,1)S(1)} collective-permute-done((bf16[2,16,512]{2,1,0:T(8,128)(2,1)S(1)}, bf16[2,16,512]{2,1,0:T(8,128)(2,1)S(1)}, u32[]{:S(2)}, u32[]{:S(2)}) %collective-permute-start) | collective-permute-done | bytes 32800 | tf_op jit(solution)/shard_map/ppermute | solution.py:235
  25.4 6.8 %collective-permute-start.3 = (bf16[2,2,16,512]{3,2,1,0:T(8,128)(2,1)S(1)}, bf16[2,2,16,512]{3,2,1,0:T(8,128)(2,1)S(1)}, u32[]{:S(2)}, u32[]{:S(2)}) collective-permute-start(bf16[2,2,16,512]{3,2,1,0:T(8,128)(2,1)S(1)} %shard_map.56.refs_0_), channel_id=1, source_target_pairs={{0,16},{4,20},{8,24},{12,28},{16,0},{20,4},{24,8},{28,12},{1,17},{... | collective-permute-start | bytes 196616 | tf_op jit(solution)/shard_map/ppermute | solution.py:246
  32.2 0.0 collective-permute-start.2
  32.2 2.4 %collective-permute-start.1 = (bf16[2,2,16,512]{3,2,1,0:T(8,128)(2,1)S(1)}, bf16[2,2,16,512]{3,2,1,0:T(8,128)(2,1)S(1)}, u32[]{:S(2)}, u32[]{:S(2)}) collective-permute-start(bf16[2,2,16,512]{3,2,1,0:T(8,128)(2,1)S(1)} %shard_map.56.refs_0_), channel_id=1, source_target_pairs={{0,8},{4,12},{8,16},{12,20},{16,24},{20,28},{24,0},{28,4},{1,9},{5... | collective-permute-start | bytes 196616 | tf_op jit(solution)/shard_map/ppermute | solution.py:246
  34.6 3.6 %all-to-all-done.1 = bf16[16,128,256]{2,1,0:T(8,128)(2,1)S(1)} async-done(((bf16[16,128,256]{2,1,0:T(8,128)(2,1)}), bf16[16,128,256]{2,1,0:T(8,128)(2,1)S(1)}, u32[]{:S(2)}, u32[]{:S(2)}) %all-to-all-start.1) | async-done | bytes 1048608 | tf_op jit(solution)/shard_map/all_to_all | solution.py:257
  38.2 0.1 reduce_sum.25.own_ref
  38.3 3.0 %collective-permute-start.6 = (bf16[128,256]{1,0:T(8,128)(2,1)S(1)}, bf16[128,256]{1,0:T(8,128)(2,1)S(1)}, u32[]{:S(2)}, u32[]{:S(2)}) collective-permute-start(bf16[128,256]{1,0:T(8,128)(2,1)S(1)} %reduce_sum.25.own_ref), channel_id=1, source_target_pairs={{0,1},{1,0},{2,3},{3,2},{4,5},{5,4},{6,7},{7,6},{8,9},{9,8},{10,11... | collective-permute-start | bytes 196616 | tf_op jit(solution)/shard_map/ppermute | solution.py:175
  41.3 0.0 collective-permute-done.3.refs_3_
  41.3 0.0 collective-permute-done.2.refs_2_
  41.3 0.0 collective-permute-done.1.refs_1_
  41.3 0.8 %collective-permute-done.6.other_ref = bf16[128,256]{1,0:T(8,128)(2,1)S(1)} collective-permute-done((bf16[128,256]{1,0:T(8,128)(2,1)S(1)}, bf16[128,256]{1,0:T(8,128)(2,1)S(1)}, u32[]{:S(2)}, u32[]{:S(2)}) %collective-permute-start.6) | collective-permute-done | bytes 65568 | tf_op jit(solution)/shard_map/ppermute | solution.py:175
  42.2 0.2 shard_map.59
  42.4 16.0 %all_to_all.15.shares_ref = bf16[16,16,128]{2,1,0:T(8,128)(2,1)S(1)} all-to-all(bf16[16,16,128]{2,1,0:T(8,128)(2,1)S(1)} %shard_map.59), channel_id=1, replica_groups=mesh['yh'=2,'x'=4,'z'=8,'yl'=2,'core'=2] {'z','yl'}, dimensions={0} | all-to-all | bytes 131072 | tf_op jit(solution)/shard_map/all_to_all | solution.py:268
  58.4 0.6 %shard_map.60 = bf16[16,256]{1,0:T(8,128)(2,1)} custom-call(bf16[16,16,128]{2,1,0:T(8,128)(2,1)S(1)} %all_to_all.15.shares_ref), custom_call_target="tpu_custom_call" | custom-call | flops 32768 | bytes 200000 | tf_op jit(solution)/shard_map/pallas_call | solution.py:269
  (5 shorter events, 0.1 us)
Async XLA Ops:
  0.0 10.5 %copy-start = (bf16[64,16,512]{2,1,0:T(8,128)(2,1)S(1)}, bf16[64,16,512]{2,1,0:T(8,128)(2,1)}, u32[]{:S(2)}) copy-start(bf16[64,16,512]{2,1,0:T(8,128)(2,1)} %own_t_ref.1) | copy-start | bytes 3145732
  0.0 10.5 %collective-permute-start.4 = (bf16[64,16,512]{2,1,0:T(8,128)(2,1)}, bf16[64,16,512]{2,1,0:T(8,128)(2,1)S(1)}, u32[]{:S(2)}, u32[]{:S(2)}) collective-permute-start(bf16[64,16,512]{2,1,0:T(8,128)(2,1)} %own_t_ref.1), channel_id=1, source_target_pairs={{0,1},{1,0},{2,3},{3,2},{4,5},{5,4},{6,7},{7,6},{8,9},{9,8},{10,11... | collective-permute-start | bytes 3145736 | tf_op jit(solution)/shard_map/ppermute | solution.py:175
  3.2 7.3 %collective-permute-start.5 = (bf16[64,16,256]{2,1,0:T(8,128)(2,1)}, bf16[64,16,256]{2,1,0:T(8,128)(2,1)S(1)}, u32[]{:S(2)}, u32[]{:S(2)}) collective-permute-start(bf16[64,16,256]{2,1,0:T(8,128)(2,1)} %own_v_ref.1), channel_id=1, source_target_pairs={{0,1},{1,0},{2,3},{3,2},{4,5},{5,4},{6,7},{7,6},{8,9},{9,8},{10,11... | collective-permute-start | bytes 1572872 | tf_op jit(solution)/shard_map/ppermute | solution.py:175
  3.2 7.3 %copy-start.4 = (f32[512]{0:T(512)S(1)}, f32[512]{0:T(512)}, u32[]{:S(2)}) copy-start(f32[512]{0:T(512)} %param.9) | copy-start | bytes 6148
  5.2 5.4 %copy-start.2 = (bf16[64,16,256]{2,1,0:T(8,128)(2,1)S(1)}, bf16[64,16,256]{2,1,0:T(8,128)(2,1)}, u32[]{:S(2)}) copy-start(bf16[64,16,256]{2,1,0:T(8,128)(2,1)} %own_v_ref.1) | copy-start | bytes 1572868
  5.2 5.4 %copy-start.3 = (s32[512,2]{0,1:T(2,128)S(1)}, s32[512,2]{0,1:T(2,128)}, u32[]{:S(2)}) copy-start(s32[512,2]{0,1:T(2,128)} %param.8) | copy-start | bytes 12292
  5.2 12.7 %all-to-all-start = ((bf16[16,16,512]{2,1,0:T(8,128)(2,1)}), bf16[16,16,512]{2,1,0:T(8,128)(2,1)S(1)}, u32[]{:S(2)}, u32[]{:S(2)}) async-start(bf16[16,16,512]{2,1,0:T(8,128)(2,1)} %bitcast.10), calls=%async_computation | async-start | bytes 524288 | tf_op jit(solution)/shard_map/all_to_all | solution.py:204
  10.5 0.7 %copy-start.1 = (s32[8]{0:T(128)S(1)}, s32[8]{0:T(128)}, u32[]{:S(2)}) copy-start(s32[8]{0:T(128)} %orders_ref.3) | copy-start | bytes 100
  17.9 20.2 %all-to-all-start.1 = ((bf16[16,128,256]{2,1,0:T(8,128)(2,1)}), bf16[16,128,256]{2,1,0:T(8,128)(2,1)S(1)}, u32[]{:S(2)}, u32[]{:S(2)}) async-start(bf16[16,128,256]{2,1,0:T(8,128)(2,1)} %bitcast.5), calls=%async_computation.1 | async-start | bytes 2097152 | tf_op jit(solution)/shard_map/all_to_all | solution.py:257
  22.3 3.0 %collective-permute-start = (bf16[2,16,512]{2,1,0:T(8,128)(2,1)S(1)}, bf16[2,16,512]{2,1,0:T(8,128)(2,1)S(1)}, u32[]{:S(2)}, u32[]{:S(2)}) collective-permute-start(bf16[2,16,512]{2,1,0:T(8,128)(2,1)S(1)} %reduce_sum.24.own_ref), channel_id=1, source_target_pairs={{0,4},{4,0},{8,12},{12,8},{16,20},{20,16},{24,28},{28,24},{1,5},{5... | collective-permute-start | bytes 98312 | tf_op jit(solution)/shard_map/ppermute | solution.py:235
  25.4 15.9 %collective-permute-start.3 = (bf16[2,2,16,512]{3,2,1,0:T(8,128)(2,1)S(1)}, bf16[2,2,16,512]{3,2,1,0:T(8,128)(2,1)S(1)}, u32[]{:S(2)}, u32[]{:S(2)}) collective-permute-start(bf16[2,2,16,512]{3,2,1,0:T(8,128)(2,1)S(1)} %shard_map.56.refs_0_), channel_id=1, source_target_pairs={{0,16},{4,20},{8,24},{12,28},{16,0},{20,4},{24,8},{28,12},{1,17},{... | collective-permute-start | bytes 196616 | tf_op jit(solution)/shard_map/ppermute | solution.py:246
  32.2 9.1 %collective-permute-start.2 = (bf16[2,2,16,512]{3,2,1,0:T(8,128)(2,1)S(1)}, bf16[2,2,16,512]{3,2,1,0:T(8,128)(2,1)S(1)}, u32[]{:S(2)}, u32[]{:S(2)}) collective-permute-start(bf16[2,2,16,512]{3,2,1,0:T(8,128)(2,1)S(1)} %shard_map.56.refs_0_), channel_id=1, source_target_pairs={{0,24},{4,28},{8,0},{12,4},{16,8},{20,12},{24,16},{28,20},{1,25},{... | collective-permute-start | bytes 196616 | tf_op jit(solution)/shard_map/ppermute | solution.py:246
  32.2 9.1 %collective-permute-start.1 = (bf16[2,2,16,512]{3,2,1,0:T(8,128)(2,1)S(1)}, bf16[2,2,16,512]{3,2,1,0:T(8,128)(2,1)S(1)}, u32[]{:S(2)}, u32[]{:S(2)}) collective-permute-start(bf16[2,2,16,512]{3,2,1,0:T(8,128)(2,1)S(1)} %shard_map.56.refs_0_), channel_id=1, source_target_pairs={{0,8},{4,12},{8,16},{12,20},{16,24},{20,28},{24,0},{28,4},{1,9},{5... | collective-permute-start | bytes 196616 | tf_op jit(solution)/shard_map/ppermute | solution.py:246
  38.3 3.9 %collective-permute-start.6 = (bf16[128,256]{1,0:T(8,128)(2,1)S(1)}, bf16[128,256]{1,0:T(8,128)(2,1)S(1)}, u32[]{:S(2)}, u32[]{:S(2)}) collective-permute-start(bf16[128,256]{1,0:T(8,128)(2,1)S(1)} %reduce_sum.25.own_ref), channel_id=1, source_target_pairs={{0,1},{1,0},{2,3},{3,2},{4,5},{5,4},{6,7},{7,6},{8,9},{9,8},{10,11... | collective-permute-start | bytes 196616 | tf_op jit(solution)/shard_map/ppermute | solution.py:175
